TPU v7x, 128 devices: a whole 4x4x4 slice. The times are simulated.
128 devices in a mesh: gx: 4 (over z), gy: 8 (over x_lo, y), gz: 4 (over x_hi, core).
Axes of the slice: x: 4 (x_hi: 2, x_lo: 2; x = x_hi * 2 + x_lo), y: 4, z: 4, core: 2. Of those that a mesh axis runs over, the one named last changes fastest.
Arguments:
- cell_counts: int32 [16, 16, 16], P('gx', 'gy', 'gz'), may hold values from 64 to 128
- grid_offset: int32 [16, 16, 16, 3, 128], P('gx', 'gy', 'gz'), may hold values from 0 to 14
- fraction: float32 [16, 16, 16, 3, 128], P('gx', 'gy', 'gz'), may hold values from 0 to 1
- species: int32 [16, 16, 16, 128], P('gx', 'gy', 'gz'), may hold values from 0 to 1
- species_density: float32 [2], replicated, may hold values from 0.01 to 0.03
- species_pair: float32 [2], replicated, may hold values from 0.05 to 0.2
- species_embed: float32 [2], replicated, may hold values from 0.5 to 2
- species_charge: float32 [2], replicated, may hold values from -3 to 3
Outputs:
- forces: float32 [16, 16, 16, 3, 128], P('gx', 'gy', 'gz')
- density: float32 [16, 16, 16, 128], P('gx', 'gy', 'gz')
Inputs may be any that keep to these rules, and one draw needn't show every extreme that they name: `cell_counts`: slots below the count hold atoms; the others are padding. `grid_offset`: an atom's stencil points lie in its own cell.
All inputs are finite; a program needn't handle non-finite values.
Results may differ from a plain program's by a relative error of at most 0.0003.
Values sent between devices are 32-bit elements; how exact they have to be, the bound alone decides.
A program may use at most 128 MiB of HBM per device.

v0:
```python
import math

import jax
import jax.numpy as jnp
from jax import lax
from jax.sharding import PartitionSpec as P

NSPEC = 2
PPC = 16


EWALD_SPLIT = 0.7
COUPLING = 8.0
HIGHEST_PRECISION = lax.Precision.HIGHEST
neighbour_shifts = [
    (shift_x, shift_y, shift_z)
    for shift_x in (-1, 0, 1)
    for shift_y in (-1, 0, 1)
    for shift_z in (-1, 0, 1)
]


def padded(block, sides, width):
    for axis, dim in sides:
        count = lax.axis_size(axis)
        forward = [(i, i + 1) for i in range(count - 1)]
        forward.append((count - 1, 0))
        backward = [(target, source) for source, target in forward]
        low = lax.ppermute(
            lax.slice_in_dim(block, block.shape[dim] - width, None, axis=dim), axis, forward
        )
        high = lax.ppermute(lax.slice_in_dim(block, 0, width, axis=dim), axis, backward)
        block = jnp.concatenate([low, block, high], axis=dim)
    return block


def species_value(species, lookup_table):
    result = jnp.zeros(species.shape, jnp.float32)
    for kind_index in range(NSPEC):
        result = result + jnp.where(species == kind_index, lookup_table[kind_index], 0.0)
    return result


def stencil(offsets, fractions):
    points = lax.broadcasted_iota(jnp.int32, offsets.shape + (PPC,), offsets.ndim)
    lower_point = (points == offsets[..., None]).astype(jnp.float32)
    upper_point = (points == offsets[..., None] + 1).astype(jnp.float32)
    weights = lower_point * (1.0 - fractions[..., None]) + upper_point * fractions[..., None]
    return (weights, upper_point - lower_point)


def spread_cells(charges, weights_x, weights_y, weights_z):
    batch_size, slot_count = charges.shape
    pair_plane = (weights_y[:, :, :, None] * weights_z[:, :, None, :]).reshape(
        batch_size, slot_count, PPC * PPC
    )
    return jnp.einsum(
        "bax,bay->bxy", weights_x * charges[:, :, None], pair_plane, precision=HIGHEST_PRECISION
    )


def outer_plane(first_weights, second_weights):
    batch_size, slot_count, width_count = first_weights.shape
    return (first_weights[:, :, :, None] * second_weights[:, :, None, :]).reshape(
        batch_size, slot_count, width_count * width_count
    )


def sample_cells(blocks, charges, weights_x, weights_y, weights_z, slope_x, slope_y, slope_z):
    plain_x = jnp.einsum("bax,bxy->bay", weights_x, blocks, precision=HIGHEST_PRECISION)
    tilted_x = jnp.einsum("bax,bxy->bay", slope_x, blocks, precision=HIGHEST_PRECISION)
    force_x = -charges * jnp.sum(tilted_x * outer_plane(weights_y, weights_z), axis=2)
    force_y = -charges * jnp.sum(plain_x * outer_plane(slope_y, weights_z), axis=2)
    force_z = -charges * jnp.sum(plain_x * outer_plane(weights_y, slope_z), axis=2)
    return jnp.stack([force_x, force_y, force_z], axis=1)


def signed_modes(indices, total):
    return jnp.where(2 * indices >= total, indices - total, indices)


def green_factor(modes_x, modes_y, modes_z, length_x, length_y, length_z):
    wave_x = modes_x.astype(jnp.float32) * (2.0 * math.pi / length_x)
    wave_y = modes_y.astype(jnp.float32) * (2.0 * math.pi / length_y)
    wave_z = modes_z.astype(jnp.float32) * (2.0 * math.pi / length_z)
    squared = wave_x * wave_x + wave_y * wave_y + wave_z * wave_z
    anchor = (modes_x == 0) & (modes_y == 0) & (modes_z == 0)
    safe_square = jnp.where(anchor, 1.0, squared)
    return jnp.where(
        anchor,
        0.0,
        4.0 * math.pi * jnp.exp(-squared / (4.0 * EWALD_SPLIT * EWALD_SPLIT)) / safe_square,
    )


def dft_tables(length):
    product = lax.broadcasted_iota(jnp.int32, (length, length), 0) * lax.broadcasted_iota(
        jnp.int32, (length, length), 1
    )
    phases = (product % length).astype(jnp.float32) * (2.0 * math.pi / length)
    return (jnp.cos(phases), jnp.sin(phases))


def line_transform(real_part, imag_part, along_axis, sign_value):
    cosine_table, sine_table = dft_tables(real_part.shape[along_axis])
    real_last = jnp.moveaxis(real_part, along_axis, -1)
    imag_last = jnp.moveaxis(imag_part, along_axis, -1)
    real_cos = jnp.matmul(real_last, cosine_table, precision=HIGHEST_PRECISION)
    real_sin = jnp.matmul(real_last, sine_table, precision=HIGHEST_PRECISION)
    imag_cos = jnp.matmul(imag_last, cosine_table, precision=HIGHEST_PRECISION)
    imag_sin = jnp.matmul(imag_last, sine_table, precision=HIGHEST_PRECISION)
    new_real = real_cos - sign_value * imag_sin
    new_imag = imag_cos + sign_value * real_sin
    return (jnp.moveaxis(new_real, -1, along_axis), jnp.moveaxis(new_imag, -1, along_axis))


def pair_terms(positions, other_positions, shift_triple, not_self):
    shift_vector = jnp.asarray(shift_triple, jnp.float32)
    separation = (
        shift_vector[:, None, None] + other_positions[..., :, None, :] - positions[..., :, :, None]
    )
    squared = jnp.sum(separation * separation, axis=-3)
    weight = jnp.maximum(1.0 - squared, 0.0)
    if shift_triple == (0, 0, 0):
        weight = weight * not_self
    return (separation, weight)


def window(rows, shift_triple, cells_y, cells_z):
    return rows[
        1 + shift_triple[0],
        1 + shift_triple[1] : 1 + shift_triple[1] + cells_y,
        1 + shift_triple[2] : 1 + shift_triple[2] + cells_z,
    ]


def on_device(
    cell_counts,
    grid_offset,
    fraction,
    species,
    species_density,
    species_pair,
    species_embed,
    species_charge,
):
    cells_x, cells_y, cells_z, components, slot_count = fraction.shape
    slot_index = lax.broadcasted_iota(jnp.int32, species.shape, 3)
    alive_mask = (slot_index < cell_counts[..., None]).astype(jnp.float32)
    positions = (grid_offset.astype(jnp.float32) + 0.5 + fraction) / PPC
    density_coef = species_value(species, species_density) * alive_mask
    repulsion = species_value(species, species_pair) * alive_mask
    embedding = species_value(species, species_embed)
    charge = species_value(species, species_charge) * alive_mask
    not_self = (
        lax.broadcasted_iota(jnp.int32, (slot_count, slot_count), 0)
        != lax.broadcasted_iota(jnp.int32, (slot_count, slot_count), 1)
    ).astype(jnp.float32)
    packed_atoms = jnp.concatenate(
        [positions, density_coef[:, :, :, None, :], repulsion[:, :, :, None, :]], axis=3
    )
    extended = padded(packed_atoms, (("gx", 0), ("gy", 1), ("gz", 2)), 1)
    row_ids = jnp.arange(cells_x, dtype=jnp.int32)

    def density_row(row):
        near_rows = lax.dynamic_slice_in_dim(extended, row, 3, 0)
        own = lax.dynamic_index_in_dim(positions, row, 0, keepdims=False)
        total = jnp.zeros((cells_y, cells_z, slot_count), jnp.float32)
        for shift_triple in neighbour_shifts:
            near = window(near_rows, shift_triple, cells_y, cells_z)
            separation, weight = pair_terms(own, near[:, :, 0:3, :], shift_triple, not_self)
            total = total + jnp.sum(
                weight * weight * weight * near[:, :, 3, :][..., None, :], axis=-1
            )
        return total

    density = lax.map(density_row, row_ids) * alive_mask
    slope_embed = -embedding * alive_mask / (2.0 * jnp.sqrt(1.0 + density))
    extended_slope = padded(slope_embed, (("gx", 0), ("gy", 1), ("gz", 2)), 1)

    def force_row(row):
        near_rows = lax.dynamic_slice_in_dim(extended, row, 3, 0)
        near_slopes = lax.dynamic_slice_in_dim(extended_slope, row, 3, 0)
        own = lax.dynamic_index_in_dim(positions, row, 0, keepdims=False)
        own_rep = lax.dynamic_index_in_dim(repulsion, row, 0, keepdims=False)
        own_coef = lax.dynamic_index_in_dim(density_coef, row, 0, keepdims=False)
        own_slope = lax.dynamic_index_in_dim(slope_embed, row, 0, keepdims=False)
        total = jnp.zeros((cells_y, cells_z, 3, slot_count), jnp.float32)
        for shift_triple in neighbour_shifts:
            near = window(near_rows, shift_triple, cells_y, cells_z)
            separation, weight = pair_terms(own, near[:, :, 0:3, :], shift_triple, not_self)
            other_coef = near[:, :, 3, :][..., None, :]
            other_rep = near[:, :, 4, :][..., None, :]
            other_slope = window(near_slopes, shift_triple, cells_y, cells_z)[..., None, :]
            coefficient = -2.0 * own_rep[
                ..., :, None
            ] * other_rep * weight - 3.0 * weight * weight * (
                own_slope[..., :, None] * other_coef + other_slope * own_coef[..., :, None]
            )
            total = total + 2.0 * jnp.sum(coefficient[..., None, :, :] * separation, axis=-1)
        return total

    eam_force = lax.map(force_row, row_ids)
    flat_cells = cells_x * cells_y * cells_z

    def flatten(values):
        return values.reshape((flat_cells,) + values.shape[3:])

    stencils = [
        stencil(
            flatten(grid_offset[:, :, :, axis_index, :]), flatten(fraction[:, :, :, axis_index, :])
        )
        for axis_index in range(3)
    ]
    flat_charge = flatten(charge)
    blocks = spread_cells(flat_charge, stencils[0][0], stencils[1][0], stencils[2][0])
    charge_brick = (
        blocks.reshape(cells_x, cells_y, cells_z, PPC, PPC, PPC)
        .transpose(0, 3, 1, 4, 2, 5)
        .reshape(cells_x * PPC, cells_y * PPC, cells_z * PPC)
    )
    brick_x, brick_y, brick_z = charge_brick.shape
    length_x = brick_x * lax.axis_size("gx")
    length_y = brick_y * lax.axis_size("gy")
    depth_lines = lax.all_to_all(charge_brick, "gz", split_axis=1, concat_axis=2, tiled=True)
    quarter_y = depth_lines.shape[1]
    depth_length = depth_lines.shape[2]
    cosine_table, sine_table = dft_tables(depth_length)
    line_real = jnp.matmul(depth_lines, cosine_table, precision=HIGHEST_PRECISION)
    line_imag = -jnp.matmul(depth_lines, sine_table, precision=HIGHEST_PRECISION)
    stacked = jnp.stack([line_real, line_imag])[:, None]
    planes = lax.all_to_all(stacked, ("gx", "gy", "gz"), split_axis=4, concat_axis=1, tiled=True)
    group_size = planes.shape[1]
    rows_gx = lax.axis_size("gx")
    rest_count = group_size // rows_gx
    plane_depth = planes.shape[4]
    planes = (
        planes.reshape(2, rows_gx, rest_count, brick_x, quarter_y, plane_depth)
        .transpose(0, 5, 1, 3, 2, 4)
        .reshape(2, plane_depth, length_x, length_y)
    )
    real_part, imag_part = line_transform(planes[0], planes[1], 2, -1.0)
    real_part, imag_part = line_transform(real_part, imag_part, 1, -1.0)
    first_mode = lax.axis_index(("gx", "gy", "gz")) * plane_depth
    modes_z = signed_modes(
        first_mode + lax.broadcasted_iota(jnp.int32, (plane_depth, 1, 1), 0), depth_length
    )
    modes_x = signed_modes(lax.broadcasted_iota(jnp.int32, (1, length_x, 1), 1), length_x)
    modes_y = signed_modes(lax.broadcasted_iota(jnp.int32, (1, 1, length_y), 2), length_y)
    factor = green_factor(modes_x, modes_y, modes_z, length_x, length_y, depth_length)
    real_part, imag_part = line_transform(real_part * factor, imag_part * factor, 1, 1.0)
    real_part, imag_part = line_transform(real_part, imag_part, 2, 1.0)
    planes_return = (
        jnp.stack([real_part, imag_part])
        .reshape(2, plane_depth, rows_gx, brick_x, rest_count, quarter_y)
        .transpose(0, 2, 4, 3, 5, 1)
        .reshape(2, group_size, brick_x, quarter_y, plane_depth)
    )
    returned = lax.all_to_all(
        planes_return, ("gx", "gy", "gz"), split_axis=1, concat_axis=4, tiled=True
    )
    real_part, imag_part = (returned[0, 0], returned[1, 0])
    potential_lines = (
        jnp.matmul(real_part, cosine_table, precision=HIGHEST_PRECISION)
        - jnp.matmul(imag_part, sine_table, precision=HIGHEST_PRECISION)
    ) / (length_x * length_y * depth_length)
    potential = lax.all_to_all(potential_lines, "gz", split_axis=2, concat_axis=1, tiled=True)
    blocks_back = (
        potential.reshape(cells_x, PPC, cells_y, PPC, cells_z, PPC)
        .transpose(0, 2, 4, 1, 3, 5)
        .reshape(flat_cells, PPC, PPC * PPC)
    )
    electric = sample_cells(
        blocks_back,
        flat_charge,
        stencils[0][0],
        stencils[1][0],
        stencils[2][0],
        stencils[0][1],
        stencils[1][1],
        stencils[2][1],
    ).reshape(cells_x, cells_y, cells_z, 3, slot_count)
    forces = (eam_force + COUPLING * electric) * alive_mask[:, :, :, None, :]
    return (forces, density)


def solution(mesh):
    return jax.shard_map(
        on_device,
        mesh=mesh,
        in_specs=(
            P("gx", "gy", "gz"),
            P("gx", "gy", "gz", None, None),
            P("gx", "gy", "gz", None, None),
            P("gx", "gy", "gz", None),
            P(),
            P(),
            P(),
            P(),
        ),
        out_specs=(P("gx", "gy", "gz", None, None), P("gx", "gy", "gz", None)),
        check_vma=False,
    )
```

profile of v0, /device:TPU:25, one launch (start us, length us, event | category | flops | bytes accessed | tf_op | source)
XLA Modules:
  0.0 467.9 jit_solution(1647297114058793032)
XLA Ops:
  3.7 4.5 broadcast_multiply_fusion
  10.1 3.6 fusion.250
  13.8 2.6 reshape.1344
  16.4 6.8 %copy.319 = f32[4,2,4,16,16,16]{5,2,4,1,3,0:T(4,128)} copy(f32[4,2,4,16,16,16]{5,4,3,2,1,0:T(8,128)} %reshape.1344) | data formatting | bytes 1048576 | tf_op jit(solution)/shard_map/reshape | solution.py:218
  23.2 3.7 reshape.1345
  29.1 5.2 %all-to-all-start = ((f32[4,1,32768]{2,1,0:T(1,128)}), f32[4,1,32768]{2,1,0:T(1,128)S(1)}, u32[]{:S(2)}, u32[]{:S(2)}) async-start(f32[4,1,32768]{2,1,0:T(1,128)} %reshape.1378), calls=%async_computation | async-start | bytes 1048576 | tf_op jit(solution)/shard_map/all_to_all | solution.py:225
  34.8 8.8 %all-to-all-done = f32[4,1,32768]{2,1,0:T(1,128)S(1)} async-done(((f32[4,1,32768]{2,1,0:T(1,128)}), f32[4,1,32768]{2,1,0:T(1,128)S(1)}, u32[]{:S(2)}, u32[]{:S(2)}) %all-to-all-start) | async-done | bytes 524320 | tf_op jit(solution)/shard_map/all_to_all | solution.py:225
  52.7 2.4 reshape.1380
  55.0 8.9 %all-to-all-start.1 = ((f32[128,1,2048]{2,1,0:T(1,128)}), f32[128,1,2048]{2,1,0:T(1,128)S(1)}, u32[]{:S(2)}, u32[]{:S(2)}) async-start(f32[128,1,2048]{2,1,0:T(1,128)} %reshape.1380), calls=%async_computation.1 | async-start | bytes 2097152 | tf_op jit(solution)/shard_map/all_to_all | solution.py:232
  66.0 14.8 %all-to-all-done.1 = f32[128,1,2048]{2,1,0:T(1,128)S(1)} async-done(((f32[128,1,2048]{2,1,0:T(1,128)}), f32[128,1,2048]{2,1,0:T(1,128)S(1)}, u32[]{:S(2)}, u32[]{:S(2)}) %all-to-all-start.1) | async-done | bytes 1048608 | tf_op jit(solution)/shard_map/all_to_all | solution.py:232
  80.8 3.0 reduce.1
  121.4 6.3 %all-to-all-start.2 = ((f32[128,1,2048]{2,1,0:T(1,128)}), f32[128,1,2048]{2,1,0:T(1,128)S(1)}, u32[]{:S(2)}, u32[]{:S(2)}) async-start(f32[128,1,2048]{2,1,0:T(1,128)} %reshape.1382), calls=%async_computation.2 | async-start | bytes 2097152 | tf_op jit(solution)/shard_map/all_to_all | solution.py:259
  127.7 2.6 add_select_fusion.3
  133.7 5.6 %collective-permute-done = f32[1,2,4,5,128]{4,3,2,1,0:T(8,128)S(1)} collective-permute-done((f32[1,2,4,5,128]{4,3,2,1,0:T(8,128)S(1)}, f32[1,2,4,5,128]{4,3,2,1,0:T(8,128)S(1)}, u32[]{:S(2)}, u32[]{:S(2)}) %collective-permute-start) | collective-permute-done | bytes 20512 | tf_op jit(solution)/shard_map/ppermute | solution.py:29
  139.3 5.6 %collective-permute-start.2 = (f32[6,1,4,5,128]{4,3,2,1,0:T(8,128)S(1)}, f32[6,1,4,5,128]{4,3,2,1,0:T(8,128)S(1)}, u32[]{:S(2)}, u32[]{:S(2)}) collective-permute-start(f32[6,1,4,5,128]{4,3,2,1,0:T(8,128)S(1)} %get-tuple-element.964), channel_id=1, source_target_pairs={{0,4},{4,8},{8,12},{12,16},{16,20},{20,24},{24,28},{28,0},{1,5},{5... | collective-permute-start | bytes 184328 | tf_op jit(solution)/shard_map/ppermute | solution.py:29
  144.9 5.6 %copy.281 = f32[32,128,256]{2,1,0:T(8,128)} copy(f32[32,128,256]{1,2,0:T(8,128)} %bitcast.756) | data formatting | bytes 8388608 | tf_op jit(solution)/shard_map/mul | solution.py:54
  150.5 5.6 %copy.282 = f32[32,128,256]{2,1,0:T(8,128)} copy(f32[32,128,256]{1,2,0:T(8,128)} %bitcast.760) | data formatting | bytes 8388608 | tf_op jit(solution)/shard_map/mul | solution.py:64
  156.1 5.6 %copy.283 = f32[32,128,256]{2,1,0:T(8,128)} copy(f32[32,128,256]{1,2,0:T(8,128)} %bitcast.759) | data formatting | bytes 8388608 | tf_op jit(solution)/shard_map/mul | solution.py:64
  161.8 3.6 collective-permute-start.4
  167.4 3.5 collective-permute-done.5
  171.1 4.3 reduce.2
  179.0 2.6 fusion.229
  185.7 3.7 all-to-all-start.3
  189.5 87.6 %while.26 = (s32[]{:T(128)}, f32[4,2,4,128]{3,2,1,0:T(4,128)S(1)}, s32[4]{0:T(128)S(1)}, f32[6,4,6,5,128]{4,2,1,3,0:T(8,128)S(1)}, f32[4,2,4,3,128]{4,3,2,1,0:T(...) while((s32[]{:T(128)}, f32[4,2,4,128]{3,2,1,0:T(4,128)S(1)}, ...), condition=%wide.region_55.56_spmd.clone.clone.clone, body=%wide.region_0.55_spmd.sunk.clone.clone.sunk.clone | while | flops 49787912 | bytes 31814928 | solution.py:177
  196.9 5.2 %multiply_reduce_fusion.35 = (f32[2,4,128,128]{3,2,1,0:T(8,128)S(1)}, f32[2,4,128,128]{3,2,1,0:T(8,128)S(1)}, f32[2,4,128,128]{3,2,1,0:T(8,128)S(1)}, f32[2,4,12...) fusion(f32[2,4,3,128]{3,2,1,0:T(4,128)S(1)} %copy.441, ...), kind=kLoop, calls=%fused_computation.27.clone.1.clone | loop fusion | flops 18874368 | bytes 9670656 | tf_op jit(solution)/shard_map/while/body/eval_jaxpr/reduce_sum | solution.py:122
  206.6 2.5 multiply_reduce_fusion.34
  218.6 5.2 %multiply_reduce_fusion.35 = (f32[2,4,128,128]{3,2,1,0:T(8,128)S(1)}, f32[2,4,128,128]{3,2,1,0:T(8,128)S(1)}, f32[2,4,128,128]{3,2,1,0:T(8,128)S(1)}, f32[2,4,12...) fusion(f32[2,4,3,128]{3,2,1,0:T(4,128)S(1)} %copy.441, ...), kind=kLoop, calls=%fused_computation.27.clone.1.clone | loop fusion | flops 18874368 | bytes 9670656 | tf_op jit(solution)/shard_map/while/body/eval_jaxpr/reduce_sum | solution.py:122
  228.4 2.5 multiply_reduce_fusion.34
  240.4 5.2 %multiply_reduce_fusion.35 = (f32[2,4,128,128]{3,2,1,0:T(8,128)S(1)}, f32[2,4,128,128]{3,2,1,0:T(8,128)S(1)}, f32[2,4,128,128]{3,2,1,0:T(8,128)S(1)}, f32[2,4,12...) fusion(f32[2,4,3,128]{3,2,1,0:T(4,128)S(1)} %copy.441, ...), kind=kLoop, calls=%fused_computation.27.clone.1.clone | loop fusion | flops 18874368 | bytes 9670656 | tf_op jit(solution)/shard_map/while/body/eval_jaxpr/reduce_sum | solution.py:122
  250.1 2.5 multiply_reduce_fusion.34
  262.2 5.2 %multiply_reduce_fusion.35 = (f32[2,4,128,128]{3,2,1,0:T(8,128)S(1)}, f32[2,4,128,128]{3,2,1,0:T(8,128)S(1)}, f32[2,4,128,128]{3,2,1,0:T(8,128)S(1)}, f32[2,4,12...) fusion(f32[2,4,3,128]{3,2,1,0:T(4,128)S(1)} %copy.441, ...), kind=kLoop, calls=%fused_computation.27.clone.1.clone | loop fusion | flops 18874368 | bytes 9670656 | tf_op jit(solution)/shard_map/while/body/eval_jaxpr/reduce_sum | solution.py:122
  271.9 2.5 multiply_reduce_fusion.34
  280.6 3.2 reshape.1348
  283.8 4.7 copy.280
  288.5 3.5 reshape.1349
  292.0 5.8 %multiply_reduce_fusion.29 = f32[32,128]{1,0:T(8,128)S(1)} fusion(f32[32,128,256]{2,1,0:T(8,128)} %copy.281, f32[32,16,256]{2,1,0:T(8,128)S(1)} %reshape.1349, s32[32,128]{1,0:T(8,128)S(1)} %bitcast.782, s32[32,128]{1,0:T(8,128)S(1)} %broadcast_add_fusion.3), kind=kOutput, calls=%fused_computation.579 | convolution fusion | flops 203747328 | bytes 4767744 | tf_op jit(solution)/shard_map/bax,bxy->bay/dot_general | solution.py:71
  298.0 6.6 %multiply_reduce_fusion.28 = (f32[32,128]{1,0:T(8,128)S(1)}, f32[32,128]{1,0:T(8,128)S(1)}) fusion(f32[32,128,256]{2,1,0:T(8,128)S(1)} %copy-done.1, f32[32,128,256]{2,1,0:T(8,128)} %copy.283, f32[32,16,256]{2,1,0:T(8,128)S(1)} %reshape.1349, f32[32,128]{1,0:T(8,128)S(1)} %bitcast.786, f32[32,128]{1,0:T(8,128)S(1)} %broadcast_subtract_fusion.2, ...), kind=kOutput, calls=%fused_computation.578 | convolution fusion | flops 205840384 | bytes 9011200 | tf_op jit(solution)/shard_map/bax,bxy->bay/dot_general | solution.py:70
  304.6 3.1 multiply_bitcast_fusion.2
  307.9 2.6 collective-permute-start.7
  311.5 3.0 collective-permute-start.8
  315.3 3.8 collective-permute-done.9
  319.1 5.5 %collective-permute-start.10 = (f32[6,4,1,128]{3,2,1,0:T(1,128)S(1)}, f32[6,4,1,128]{3,2,1,0:T(1,128)S(1)}, u32[]{:S(2)}, u32[]{:S(2)}) collective-permute-start(f32[6,4,1,128]{3,2,1,0:T(1,128)S(1)} %get-tuple-element.974), channel_id=1, source_target_pairs={{0,1},{1,2},{2,3},{3,0},{4,5},{5,6},{6,7},{7,4},{8,9},{9,10},{10,1... | collective-permute-start | bytes 36872 | tf_op jit(solution)/shard_map/ppermute | solution.py:29
  325.5 3.8 collective-permute-done.11
  329.5 137.5 %while.27 = (s32[]{:T(128)}, f32[4,2,4,3,128]{4,2,1,0,3:T(4,128)S(1)}, s32[4]{0:T(128)S(1)}, f32[4,2,4,128]{3,2,1,0:T(4,128)S(1)}, f32[6,4,6,5,128]{4,2,1,3,0:T(...) while((s32[]{:T(128)}, ...), condition=%wide.region_111.112_spmd.clone.clone.clone, body=%wide.region_56.111_spmd.sunk.clone.clone.sunk.clone | while | flops 99335176 | bytes 61772524 | solution.py:203
  335.7 3.0 fusion.540
  340.4 4.6 fusion.542
  348.1 3.8 fusion.552
  353.8 4.7 %fusion.550 = (f32[2,4,3,128]{3,2,1,0:T(4,128)S(1)}, f32[2,4,3,128]{3,2,1,0:T(4,128)S(1)}, f32[2,4,3,128]{3,2,1,0:T(4,128)S(1)}, f32[2,4,3,128]{3,2,1,0:T(4,128)...) fusion(f32[2,4,128,128]{3,2,1,0:T(8,128)S(1)} %get-tuple-elemen, ...), kind=kLoop, calls=%fused_computation.265.clone.1.clone | loop fusion | flops 10589184 | bytes 4952064 | tf_op jit(solution)/shard_map/while/body/eval_jaxpr/reduce_sum | solution.py:200
  359.2 4.7 %fusion.546 = (f32[2,4,3,128]{3,2,1,0:T(4,128)S(1)}, f32[2,4,3,128]{3,2,1,0:T(4,128)S(1)}, f32[2,4,3,128]{3,2,1,0:T(4,128)S(1)}, f32[2,4,3,128]{3,2,1,0:T(4,128)...) fusion(f32[2,4,128,128]{3,2,1,0:T(8,128)S(1)} %get-tuple-elemen, ...), kind=kLoop, calls=%fused_computation.263.clone.1.clone | loop fusion | flops 10589184 | bytes 4952064 | tf_op jit(solution)/shard_map/while/body/eval_jaxpr/reduce_sum | solution.py:200
  370.0 3.0 fusion.540
  374.8 4.6 fusion.542
  382.4 3.8 fusion.552
  388.1 4.7 %fusion.550 = (f32[2,4,3,128]{3,2,1,0:T(4,128)S(1)}, f32[2,4,3,128]{3,2,1,0:T(4,128)S(1)}, f32[2,4,3,128]{3,2,1,0:T(4,128)S(1)}, f32[2,4,3,128]{3,2,1,0:T(4,128)...) fusion(f32[2,4,128,128]{3,2,1,0:T(8,128)S(1)} %get-tuple-elemen, ...), kind=kLoop, calls=%fused_computation.265.clone.1.clone | loop fusion | flops 10589184 | bytes 4952064 | tf_op jit(solution)/shard_map/while/body/eval_jaxpr/reduce_sum | solution.py:200
  393.6 4.7 %fusion.546 = (f32[2,4,3,128]{3,2,1,0:T(4,128)S(1)}, f32[2,4,3,128]{3,2,1,0:T(4,128)S(1)}, f32[2,4,3,128]{3,2,1,0:T(4,128)S(1)}, f32[2,4,3,128]{3,2,1,0:T(4,128)...) fusion(f32[2,4,128,128]{3,2,1,0:T(8,128)S(1)} %get-tuple-elemen, ...), kind=kLoop, calls=%fused_computation.263.clone.1.clone | loop fusion | flops 10589184 | bytes 4952064 | tf_op jit(solution)/shard_map/while/body/eval_jaxpr/reduce_sum | solution.py:200
  404.4 3.0 fusion.540
  409.1 4.6 fusion.542
  416.8 3.8 fusion.552
  422.4 4.7 %fusion.550 = (f32[2,4,3,128]{3,2,1,0:T(4,128)S(1)}, f32[2,4,3,128]{3,2,1,0:T(4,128)S(1)}, f32[2,4,3,128]{3,2,1,0:T(4,128)S(1)}, f32[2,4,3,128]{3,2,1,0:T(4,128)...) fusion(f32[2,4,128,128]{3,2,1,0:T(8,128)S(1)} %get-tuple-elemen, ...), kind=kLoop, calls=%fused_computation.265.clone.1.clone | loop fusion | flops 10589184 | bytes 4952064 | tf_op jit(solution)/shard_map/while/body/eval_jaxpr/reduce_sum | solution.py:200
  427.9 4.7 %fusion.546 = (f32[2,4,3,128]{3,2,1,0:T(4,128)S(1)}, f32[2,4,3,128]{3,2,1,0:T(4,128)S(1)}, f32[2,4,3,128]{3,2,1,0:T(4,128)S(1)}, f32[2,4,3,128]{3,2,1,0:T(4,128)...) fusion(f32[2,4,128,128]{3,2,1,0:T(8,128)S(1)} %get-tuple-elemen, ...), kind=kLoop, calls=%fused_computation.263.clone.1.clone | loop fusion | flops 10589184 | bytes 4952064 | tf_op jit(solution)/shard_map/while/body/eval_jaxpr/reduce_sum | solution.py:200
  438.7 3.0 fusion.540
  443.4 4.6 fusion.542
  451.1 3.8 fusion.552
  456.8 4.7 %fusion.550 = (f32[2,4,3,128]{3,2,1,0:T(4,128)S(1)}, f32[2,4,3,128]{3,2,1,0:T(4,128)S(1)}, f32[2,4,3,128]{3,2,1,0:T(4,128)S(1)}, f32[2,4,3,128]{3,2,1,0:T(4,128)...) fusion(f32[2,4,128,128]{3,2,1,0:T(8,128)S(1)} %get-tuple-elemen, ...), kind=kLoop, calls=%fused_computation.265.clone.1.clone | loop fusion | flops 10589184 | bytes 4952064 | tf_op jit(solution)/shard_map/while/body/eval_jaxpr/reduce_sum | solution.py:200
  462.2 4.7 %fusion.546 = (f32[2,4,3,128]{3,2,1,0:T(4,128)S(1)}, f32[2,4,3,128]{3,2,1,0:T(4,128)S(1)}, f32[2,4,3,128]{3,2,1,0:T(4,128)S(1)}, f32[2,4,3,128]{3,2,1,0:T(4,128)...) fusion(f32[2,4,128,128]{3,2,1,0:T(8,128)S(1)} %get-tuple-elemen, ...), kind=kLoop, calls=%fused_computation.263.clone.1.clone | loop fusion | flops 10589184 | bytes 4952064 | tf_op jit(solution)/shard_map/while/body/eval_jaxpr/reduce_sum | solution.py:200
  (876 shorter events, 158.3 us)
Async XLA Ops:
  29.1 14.5 %all-to-all-start = ((f32[4,1,32768]{2,1,0:T(1,128)}), f32[4,1,32768]{2,1,0:T(1,128)S(1)}, u32[]{:S(2)}, u32[]{:S(2)}) async-start(f32[4,1,32768]{2,1,0:T(1,128)} %reshape.1378), calls=%async_computation | async-start | bytes 1048576 | tf_op jit(solution)/shard_map/all_to_all | solution.py:225
  55.0 8.9 %copy-start.39 = (f32[2]{0:T(128)S(1)}, f32[2]{0:T(128)}, u32[]{:S(2)}) copy-start(f32[2]{0:T(128)} %param.71) | copy-start | bytes 28
  55.0 9.5 %copy-start.40 = (f32[2]{0:T(128)S(1)}, f32[2]{0:T(128)}, u32[]{:S(2)}) copy-start(f32[2]{0:T(128)} %param.70) | copy-start | bytes 28
  55.0 10.8 %copy-start.2 = (f32[4,2,4,3,128]{4,2,3,1,0:T(4,128)S(1)}, f32[4,2,4,3,128]{4,2,3,1,0:T(4,128)}, u32[]{:S(2)}) copy-start(f32[4,2,4,3,128]{4,2,3,1,0:T(4,128)} %param.68) | copy-start | bytes 147460
  55.0 10.8 %copy-start.3 = (s32[4,2,4,3,128]{4,2,3,1,0:T(4,128)S(1)}, s32[4,2,4,3,128]{4,2,3,1,0:T(4,128)}, u32[]{:S(2)}) copy-start(s32[4,2,4,3,128]{4,2,3,1,0:T(4,128)} %param.67) | copy-start | bytes 147460
  55.0 25.8 %all-to-all-start.1 = ((f32[128,1,2048]{2,1,0:T(1,128)}), f32[128,1,2048]{2,1,0:T(1,128)S(1)}, u32[]{:S(2)}, u32[]{:S(2)}) async-start(f32[128,1,2048]{2,1,0:T(1,128)} %reshape.1380), calls=%async_computation.1 | async-start | bytes 2097152 | tf_op jit(solution)/shard_map/all_to_all | solution.py:232
  121.4 49.7 %all-to-all-start.2 = ((f32[128,1,2048]{2,1,0:T(1,128)}), f32[128,1,2048]{2,1,0:T(1,128)S(1)}, u32[]{:S(2)}, u32[]{:S(2)}) async-start(f32[128,1,2048]{2,1,0:T(1,128)} %reshape.1382), calls=%async_computation.2 | async-start | bytes 2097152 | tf_op jit(solution)/shard_map/all_to_all | solution.py:259
  130.3 8.9 %collective-permute-start = (f32[1,2,4,5,128]{4,3,2,1,0:T(8,128)S(1)}, f32[1,2,4,5,128]{4,3,2,1,0:T(8,128)S(1)}, u32[]{:S(2)}, u32[]{:S(2)}) collective-permute-start(f32[1,2,4,5,128]{4,3,2,1,0:T(8,128)S(1)} %get-tuple-element.966), channel_id=1, source_target_pairs={{0,32},{32,64},{64,96},{96,0},{1,33},{33,65},{65,97},{97,1},{2,34}... | collective-permute-start | bytes 61448 | tf_op jit(solution)/shard_map/ppermute | solution.py:29
  131.8 7.4 %collective-permute-start.1 = (f32[1,2,4,5,128]{4,3,2,1,0:T(8,128)S(1)}, f32[1,2,4,5,128]{4,3,2,1,0:T(8,128)S(1)}, u32[]{:S(2)}, u32[]{:S(2)}) collective-permute-start(f32[1,2,4,5,128]{4,3,2,1,0:T(8,128)S(1)} %get-tuple-element.967), channel_id=1, source_target_pairs={{32,0},{64,32},{96,64},{0,96},{33,1},{65,33},{97,65},{1,97},{34,2}... | collective-permute-start | bytes 61448 | tf_op jit(solution)/shard_map/ppermute | solution.py:32
  139.3 22.4 %collective-permute-start.2 = (f32[6,1,4,5,128]{4,3,2,1,0:T(8,128)S(1)}, f32[6,1,4,5,128]{4,3,2,1,0:T(8,128)S(1)}, u32[]{:S(2)}, u32[]{:S(2)}) collective-permute-start(f32[6,1,4,5,128]{4,3,2,1,0:T(8,128)S(1)} %get-tuple-element.964), channel_id=1, source_target_pairs={{0,4},{4,8},{8,12},{12,16},{16,20},{20,24},{24,28},{28,0},{1,5},{5... | collective-permute-start | bytes 184328 | tf_op jit(solution)/shard_map/ppermute | solution.py:29
  144.9 16.9 %collective-permute-start.3 = (f32[6,1,4,5,128]{4,3,2,1,0:T(8,128)S(1)}, f32[6,1,4,5,128]{4,3,2,1,0:T(8,128)S(1)}, u32[]{:S(2)}, u32[]{:S(2)}) collective-permute-start(f32[6,1,4,5,128]{4,3,2,1,0:T(8,128)S(1)} %get-tuple-element.965), channel_id=1, source_target_pairs={{4,0},{8,4},{12,8},{16,12},{20,16},{24,20},{28,24},{0,28},{5,1},{9... | collective-permute-start | bytes 184328 | tf_op jit(solution)/shard_map/ppermute | solution.py:32
  156.1 9.3 %copy-start.41 = (f32[2]{0:T(128)S(1)}, f32[2]{0:T(128)}, u32[]{:S(2)}) copy-start(f32[2]{0:T(128)} %param.72) | copy-start | bytes 28
  161.8 5.6 %collective-permute-start.4 = (f32[6,4,1,5,128]{4,3,2,1,0:T(8,128)S(1)}, f32[6,4,1,5,128]{4,3,2,1,0:T(8,128)S(1)}, u32[]{:S(2)}, u32[]{:S(2)}) collective-permute-start(f32[6,4,1,5,128]{4,3,2,1,0:T(8,128)S(1)} %get-tuple-element.959), channel_id=1, source_target_pairs={{0,1},{1,2},{2,3},{3,0},{4,5},{5,6},{6,7},{7,4},{8,9},{9,10},{10,1... | collective-permute-start | bytes 184328 | tf_op jit(solution)/shard_map/ppermute | solution.py:29
  165.4 5.5 %collective-permute-start.5 = (f32[6,4,1,5,128]{4,3,2,1,0:T(8,128)S(1)}, f32[6,4,1,5,128]{4,3,2,1,0:T(8,128)S(1)}, u32[]{:S(2)}, u32[]{:S(2)}) collective-permute-start(f32[6,4,1,5,128]{4,3,2,1,0:T(8,128)S(1)} %get-tuple-element.960), channel_id=1, source_target_pairs={{1,0},{2,1},{3,2},{0,3},{5,4},{6,5},{7,6},{4,7},{9,8},{10,9},{11,1... | collective-permute-start | bytes 184328 | tf_op jit(solution)/shard_map/ppermute | solution.py:32
  185.7 91.3 %all-to-all-start.3 = ((f32[4,1,32768]{2,1,0:T(1,128)}), f32[4,1,32768]{2,1,0:T(1,128)S(1)}, u32[]{:S(2)}, u32[]{:S(2)}) async-start(f32[4,1,32768]{2,1,0:T(1,128)} %reshape.1384), calls=%async_computation.3 | async-start | bytes 1048576 | tf_op jit(solution)/shard_map/all_to_all | solution.py:267
  189.5 5.7 %copy-start.15 = (f32[3]{0:T(128)S(1)}, f32[3]{0:T(128)}, u32[]{:S(2)}) copy-start(f32[3]{0:T(128)} %get-tuple-element.2319) | copy-start | bytes 40 | tf_op jit(solution)/shard_map/while
  189.5 5.8 %copy-start.19 = (f32[3]{0:T(128)S(1)}, f32[3]{0:T(128)}, u32[]{:S(2)}) copy-start(f32[3]{0:T(128)} %get-tuple-element.2321) | copy-start | bytes 40 | tf_op jit(solution)/shard_map/while
  189.5 5.8 %copy-start.21 = (f32[3]{0:T(128)S(1)}, f32[3]{0:T(128)}, u32[]{:S(2)}) copy-start(f32[3]{0:T(128)} %get-tuple-element.2320) | copy-start | bytes 40 | tf_op jit(solution)/shard_map/while
  189.5 5.9 %copy-start.23 = (f32[3]{0:T(128)S(1)}, f32[3]{0:T(128)}, u32[]{:S(2)}) copy-start(f32[3]{0:T(128)} %get-tuple-element.2323) | copy-start | bytes 40 | tf_op jit(solution)/shard_map/while
  189.5 5.9 %copy-start.25 = (f32[3]{0:T(128)S(1)}, f32[3]{0:T(128)}, u32[]{:S(2)}) copy-start(f32[3]{0:T(128)} %get-tuple-element.2322) | copy-start | bytes 40 | tf_op jit(solution)/shard_map/while
  189.5 5.9 %copy-start.27 = (f32[3]{0:T(128)S(1)}, f32[3]{0:T(128)}, u32[]{:S(2)}) copy-start(f32[3]{0:T(128)} %get-tuple-element.2325) | copy-start | bytes 40 | tf_op jit(solution)/shard_map/while
  189.6 5.9 %copy-start.29 = (f32[3]{0:T(128)S(1)}, f32[3]{0:T(128)}, u32[]{:S(2)}) copy-start(f32[3]{0:T(128)} %get-tuple-element.2324) | copy-start | bytes 40 | tf_op jit(solution)/shard_map/while
  211.2 5.7 %copy-start.15 = (f32[3]{0:T(128)S(1)}, f32[3]{0:T(128)}, u32[]{:S(2)}) copy-start(f32[3]{0:T(128)} %get-tuple-element.2319) | copy-start | bytes 40 | tf_op jit(solution)/shard_map/while
  211.3 5.8 %copy-start.19 = (f32[3]{0:T(128)S(1)}, f32[3]{0:T(128)}, u32[]{:S(2)}) copy-start(f32[3]{0:T(128)} %get-tuple-element.2321) | copy-start | bytes 40 | tf_op jit(solution)/shard_map/while
  211.3 5.8 %copy-start.21 = (f32[3]{0:T(128)S(1)}, f32[3]{0:T(128)}, u32[]{:S(2)}) copy-start(f32[3]{0:T(128)} %get-tuple-element.2320) | copy-start | bytes 40 | tf_op jit(solution)/shard_map/while
  211.3 5.9 %copy-start.23 = (f32[3]{0:T(128)S(1)}, f32[3]{0:T(128)}, u32[]{:S(2)}) copy-start(f32[3]{0:T(128)} %get-tuple-element.2323) | copy-start | bytes 40 | tf_op jit(solution)/shard_map/while
  211.3 5.9 %copy-start.25 = (f32[3]{0:T(128)S(1)}, f32[3]{0:T(128)}, u32[]{:S(2)}) copy-start(f32[3]{0:T(128)} %get-tuple-element.2322) | copy-start | bytes 40 | tf_op jit(solution)/shard_map/while
  211.3 5.9 %copy-start.27 = (f32[3]{0:T(128)S(1)}, f32[3]{0:T(128)}, u32[]{:S(2)}) copy-start(f32[3]{0:T(128)} %get-tuple-element.2325) | copy-start | bytes 40 | tf_op jit(solution)/shard_map/while
  211.3 5.9 %copy-start.29 = (f32[3]{0:T(128)S(1)}, f32[3]{0:T(128)}, u32[]{:S(2)}) copy-start(f32[3]{0:T(128)} %get-tuple-element.2324) | copy-start | bytes 40 | tf_op jit(solution)/shard_map/while
  233.0 5.8 %copy-start.19 = (f32[3]{0:T(128)S(1)}, f32[3]{0:T(128)}, u32[]{:S(2)}) copy-start(f32[3]{0:T(128)} %get-tuple-element.2321) | copy-start | bytes 40 | tf_op jit(solution)/shard_map/while
  233.1 5.8 %copy-start.21 = (f32[3]{0:T(128)S(1)}, f32[3]{0:T(128)}, u32[]{:S(2)}) copy-start(f32[3]{0:T(128)} %get-tuple-element.2320) | copy-start | bytes 40 | tf_op jit(solution)/shard_map/while
  233.1 5.9 %copy-start.23 = (f32[3]{0:T(128)S(1)}, f32[3]{0:T(128)}, u32[]{:S(2)}) copy-start(f32[3]{0:T(128)} %get-tuple-element.2323) | copy-start | bytes 40 | tf_op jit(solution)/shard_map/while
  233.1 5.9 %copy-start.25 = (f32[3]{0:T(128)S(1)}, f32[3]{0:T(128)}, u32[]{:S(2)}) copy-start(f32[3]{0:T(128)} %get-tuple-element.2322) | copy-start | bytes 40 | tf_op jit(solution)/shard_map/while
  233.1 5.9 %copy-start.27 = (f32[3]{0:T(128)S(1)}, f32[3]{0:T(128)}, u32[]{:S(2)}) copy-start(f32[3]{0:T(128)} %get-tuple-element.2325) | copy-start | bytes 40 | tf_op jit(solution)/shard_map/while
  233.1 5.9 %copy-start.29 = (f32[3]{0:T(128)S(1)}, f32[3]{0:T(128)}, u32[]{:S(2)}) copy-start(f32[3]{0:T(128)} %get-tuple-element.2324) | copy-start | bytes 40 | tf_op jit(solution)/shard_map/while
  254.8 5.8 %copy-start.19 = (f32[3]{0:T(128)S(1)}, f32[3]{0:T(128)}, u32[]{:S(2)}) copy-start(f32[3]{0:T(128)} %get-tuple-element.2321) | copy-start | bytes 40 | tf_op jit(solution)/shard_map/while
  254.8 5.8 %copy-start.21 = (f32[3]{0:T(128)S(1)}, f32[3]{0:T(128)}, u32[]{:S(2)}) copy-start(f32[3]{0:T(128)} %get-tuple-element.2320) | copy-start | bytes 40 | tf_op jit(solution)/shard_map/while
  254.8 5.9 %copy-start.23 = (f32[3]{0:T(128)S(1)}, f32[3]{0:T(128)}, u32[]{:S(2)}) copy-start(f32[3]{0:T(128)} %get-tuple-element.2323) | copy-start | bytes 40 | tf_op jit(solution)/shard_map/while
  254.9 5.9 %copy-start.25 = (f32[3]{0:T(128)S(1)}, f32[3]{0:T(128)}, u32[]{:S(2)}) copy-start(f32[3]{0:T(128)} %get-tuple-element.2322) | copy-start | bytes 40 | tf_op jit(solution)/shard_map/while
  254.9 5.9 %copy-start.27 = (f32[3]{0:T(128)S(1)}, f32[3]{0:T(128)}, u32[]{:S(2)}) copy-start(f32[3]{0:T(128)} %get-tuple-element.2325) | copy-start | bytes 40 | tf_op jit(solution)/shard_map/while
  254.9 5.9 %copy-start.29 = (f32[3]{0:T(128)S(1)}, f32[3]{0:T(128)}, u32[]{:S(2)}) copy-start(f32[3]{0:T(128)} %get-tuple-element.2324) | copy-start | bytes 40 | tf_op jit(solution)/shard_map/while
  291.9 5.9 %copy-start.1 = (f32[32,128,256]{2,1,0:T(8,128)S(1)}, f32[32,128,256]{2,1,0:T(8,128)}, u32[]{:S(2)}) copy-start(f32[32,128,256]{2,1,0:T(8,128)} %copy.282) | copy-start | bytes 12582916
  297.8 31.5 %copy-start.7 = (f32[3]{0:T(128)S(1)}, f32[3]{0:T(128)}, u32[]{:S(2)}) copy-start(f32[3]{0:T(128)} %get-tuple-element.2442) | copy-start | bytes 40
  297.8 31.5 %copy-start.8 = (f32[3]{0:T(128)S(1)}, f32[3]{0:T(128)}, u32[]{:S(2)}) copy-start(f32[3]{0:T(128)} %get-tuple-element.2443) | copy-start | bytes 40
  297.8 31.5 %copy-start.9 = (f32[3]{0:T(128)S(1)}, f32[3]{0:T(128)}, u32[]{:S(2)}) copy-start(f32[3]{0:T(128)} %get-tuple-element.2444) | copy-start | bytes 40
  297.8 31.5 %copy-start.10 = (f32[3]{0:T(128)S(1)}, f32[3]{0:T(128)}, u32[]{:S(2)}) copy-start(f32[3]{0:T(128)} %get-tuple-element.2445) | copy-start | bytes 40
  297.9 31.5 %copy-start.11 = (f32[3]{0:T(128)S(1)}, f32[3]{0:T(128)}, u32[]{:S(2)}) copy-start(f32[3]{0:T(128)} %get-tuple-element.2446) | copy-start | bytes 40
  297.9 31.5 %copy-start.12 = (f32[3]{0:T(128)S(1)}, f32[3]{0:T(128)}, u32[]{:S(2)}) copy-start(f32[3]{0:T(128)} %get-tuple-element.2447) | copy-start | bytes 40
  297.9 31.5 %copy-start.13 = (f32[3]{0:T(128)S(1)}, f32[3]{0:T(128)}, u32[]{:S(2)}) copy-start(f32[3]{0:T(128)} %get-tuple-element.2448) | copy-start | bytes 40
  297.9 31.5 %copy-start.14 = (f32[3]{0:T(128)S(1)}, f32[3]{0:T(128)}, u32[]{:S(2)}) copy-start(f32[3]{0:T(128)} %get-tuple-element.2449) | copy-start | bytes 40
  297.9 31.5 %copy-start.16 = (f32[3]{0:T(128)S(1)}, f32[3]{0:T(128)}, u32[]{:S(2)}) copy-start(f32[3]{0:T(128)} %get-tuple-element.2450) | copy-start | bytes 40
  297.9 31.5 %copy-start.18 = (f32[3]{0:T(128)S(1)}, f32[3]{0:T(128)}, u32[]{:S(2)}) copy-start(f32[3]{0:T(128)} %get-tuple-element.2451) | copy-start | bytes 40
  297.9 31.5 %copy-start.20 = (f32[3]{0:T(128)S(1)}, f32[3]{0:T(128)}, u32[]{:S(2)}) copy-start(f32[3]{0:T(128)} %get-tuple-element.2452) | copy-start | bytes 40
  297.9 31.5 %copy-start.22 = (f32[3]{0:T(128)S(1)}, f32[3]{0:T(128)}, u32[]{:S(2)}) copy-start(f32[3]{0:T(128)} %get-tuple-element.2453) | copy-start | bytes 40
  298.0 31.5 %copy-start.24 = (f32[3]{0:T(128)S(1)}, f32[3]{0:T(128)}, u32[]{:S(2)}) copy-start(f32[3]{0:T(128)} %get-tuple-element.2454) | copy-start | bytes 40
  298.0 31.5 %copy-start.26 = (f32[3]{0:T(128)S(1)}, f32[3]{0:T(128)}, u32[]{:S(2)}) copy-start(f32[3]{0:T(128)} %get-tuple-element.2455) | copy-start | bytes 40
  298.0 31.5 %copy-start.28 = (f32[3]{0:T(128)S(1)}, f32[3]{0:T(128)}, u32[]{:S(2)}) copy-start(f32[3]{0:T(128)} %get-tuple-element.2456) | copy-start | bytes 40
  298.0 31.5 %copy-start.30 = (f32[3]{0:T(128)S(1)}, f32[3]{0:T(128)}, u32[]{:S(2)}) copy-start(f32[3]{0:T(128)} %get-tuple-element.2457) | copy-start | bytes 40
  307.8 3.7 collective-permute-start.6
  307.9 3.6 collective-permute-start.7
  311.5 3.8 collective-permute-start.8
  314.5 4.7 collective-permute-start.9
  319.1 6.4 %collective-permute-start.10 = (f32[6,4,1,128]{3,2,1,0:T(1,128)S(1)}, f32[6,4,1,128]{3,2,1,0:T(1,128)S(1)}, u32[]{:S(2)}, u32[]{:S(2)}) collective-permute-start(f32[6,4,1,128]{3,2,1,0:T(1,128)S(1)} %get-tuple-element.974), channel_id=1, source_target_pairs={{0,1},{1,2},{2,3},{3,0},{4,5},{5,6},{6,7},{7,4},{8,9},{9,10},{10,1... | collective-permute-start | bytes 36872 | tf_op jit(solution)/shard_map/ppermute | solution.py:29
  324.7 4.6 collective-permute-start.11
  (19 other events, 94.2 us)
where the time goes:
time: 477 us; the launch traced here: 468 us
  other arithmetic  212 us (44%)
  local copies, waits for them, and re-layouts  80 us (17%)
  matrix products  52.6 us (11%)
  starting transfers between devices  47.7 us (10%)
  waiting for transfers between devices  44.2 us (9%)
  loops' own time  29.3 us (6%)
    reduce_sum x16, other arithmetic, force_row(): jnp.sum(coefficient[..., None, :, :] * separation, axis=-1)  71.3 us
    reduce_sum x16, other arithmetic, pair_terms(): squared = jnp.sum(separation * separation, axis=-3)  44.5 us
    sub x32, other arithmetic, force_row(): -2.0 * own_rep[..., :, None] * other_rep * weight  27.6 us
    reduce_sum x108, other arithmetic, density_row(): jnp.sum(weight * weight * weight * near[:, :, 3, :][..., None, :], axis=-1)  23.8 us
    ppermute x6, starting transfers between devices, padded(): lax.ppermute(lax.slice_in_dim(block, block.shape[dim] - width, None, axis...  19.3 us
    add x104, other arithmetic, pair_terms(): shift_vector[:, None, None] + other_positions[..., :, None, :]  18.6 us
    another operation x1, loops' own time, on_device(): eam_force = lax.map(force_row, row_ids)  15.6 us
    all_to_all x1, waiting for transfers between devices, on_device(): lax.all_to_all(stacked, ('gx', 'gy', 'gz'), split_axis=4, concat_axis=1,...  14.8 us
  transfers between devices with their start and end apart: 16, of which 10 were waited for; matrix products, arithmetic and copies ran while one was open for 21% of the time, Pallas kernels for 0%

commit v1 on v0

v1 whole, which is shorter than its diff:
```python
import itertools
import math

import jax
import jax.numpy as jnp
import numpy as np
from jax import lax
from jax.experimental import pallas as pl
from jax.experimental.pallas import tpu as pltpu
from jax.sharding import PartitionSpec as P

NSPEC = 2
PPC = 16
COUPLING = 8.0
F32, BF16 = jnp.float32, jnp.bfloat16
VMEM_SPEC = pl.BlockSpec(memory_space=pltpu.VMEM)
SMEM_SPEC = pl.BlockSpec(memory_space=pltpu.SMEM)


MESH = pl.DeviceIdType.MESH
AXES = ("gx", "gy", "gz")
SIZES = (4, 8, 4)
SIDES = [side for side in itertools.product((-1, 0, 1), repeat=3) if side != (0, 0, 0)]


def here():
    return [lax.axis_index(axis) for axis in AXES]


def toward(place, side):
    return tuple(lax.rem(p + s + n, n) for p, s, n in zip(place, side, SIZES))


def greet(devices):
    barrier = pltpu.get_barrier_semaphore()
    for device in devices:
        pl.semaphore_signal(barrier, inc=1, device_id=device, device_id_type=MESH)
    pl.semaphore_wait(barrier, len(devices))


def send(src, dst, send_sem, recv_sem, device):
    copy = pltpu.make_async_remote_copy(
        src_ref=src, dst_ref=dst, send_sem=send_sem, recv_sem=recv_sem, device_id=device, device_id_type=MESH)
    copy.start()
    return copy


def halo_copies(own_ref, ext_ref, place, send_sem, recv_sem):
    copies = []
    for n, side in enumerate(SIDES):
        src, dst = [], []
        for s, cells in zip(side, (4, 2, 4)):
            src.append(pl.ds(0, cells) if s == 0 else pl.ds(cells - 1 if s == 1 else 0, 1))
            dst.append(pl.ds(1, cells) if s == 0 else pl.ds(0 if s == 1 else cells + 1, 1))
        copies.append(send(own_ref.at[tuple(src)], ext_ref.at[tuple(dst)], send_sem.at[n], recv_sem.at[n],
                           toward(place, side)))
    return copies


def column_copies(src_ref, dst_ref, place, send_sem, recv_sem):
    gx, gy, gz = place
    copies = []
    for n in range(3):
        other = lax.rem(gz + n + 1, 4)
        copies.append(send(src_ref.at[other], dst_ref.at[gz], send_sem.at[n], recv_sem.at[n], (gx, gy, other)))
    return copies


def column_devices(place):
    gx, gy, gz = place
    return [(gx, gy, lax.rem(gz + n + 1, 4)) for n in range(3)]


def halo_kernel(own_ref, atoms_ref, ext_ref, got_ref, send_sem, recv_sem, column_send, column_recv, local_sem):
    place = here()
    greet([toward(place, side) for side in SIDES] + [column_devices(place)[1]])
    copies = column_copies(atoms_ref, got_ref, place, column_send, column_recv)
    copies += halo_copies(own_ref, ext_ref, place, send_sem, recv_sem)
    inner = pltpu.make_async_copy(own_ref, ext_ref.at[pl.ds(1, 4), pl.ds(1, 2), pl.ds(1, 4)], local_sem.at[0])
    inner.start()
    mine = pltpu.make_async_copy(atoms_ref.at[place[2]], got_ref.at[place[2]], local_sem.at[1])
    mine.start()
    inner.wait()
    mine.wait()
    for copy in copies:
        copy.wait()


def slope_kernel(own_ref, ext_ref, send_sem, recv_sem, local_sem):
    place = here()
    greet([toward(place, side) for side in SIDES])
    copies = halo_copies(own_ref, ext_ref, place, send_sem, recv_sem)
    inner = pltpu.make_async_copy(own_ref, ext_ref.at[pl.ds(1, 4), pl.ds(1, 2), pl.ds(1, 4)], local_sem.at[0])
    inner.start()
    inner.wait()
    for copy in copies:
        copy.wait()


def return_kernel(src_ref, dst_ref, send_sem, recv_sem, local_sem):
    place = here()
    greet(column_devices(place))
    copies = column_copies(src_ref, dst_ref, place, send_sem, recv_sem)
    mine = pltpu.make_async_copy(src_ref.at[place[2]], dst_ref.at[place[2]], local_sem.at[0])
    mine.start()
    mine.wait()
    for copy in copies:
        copy.wait()


COMM_SPEC = pl.BlockSpec(memory_space=pltpu.VMEM)
DMA = pltpu.SemaphoreType.DMA


def comm_params(number):
    return pltpu.CompilerParams(collective_id=number, has_side_effects=True, vmem_limit_bytes=16 << 20)


def halo_exchange(own, atoms):
    return pl.pallas_call(
        halo_kernel,
        out_shape=[jax.ShapeDtypeStruct((6, 4, 6, 8, 128), F32), jax.ShapeDtypeStruct((4, 8, 8, 128), F32)],
        in_specs=[COMM_SPEC] * 2,
        out_specs=[COMM_SPEC] * 2,
        scratch_shapes=[DMA((26,)), DMA((26,)), DMA((3,)), DMA((3,)), DMA((2,))],
        compiler_params=comm_params(0),
        name="halo_exchange",
    )(own, atoms)


def slope_exchange(own):
    return pl.pallas_call(
        slope_kernel,
        out_shape=jax.ShapeDtypeStruct((6, 4, 6, 1, 128), F32),
        in_specs=[COMM_SPEC],
        out_specs=COMM_SPEC,
        scratch_shapes=[DMA((26,)), DMA((26,)), DMA((1,))],
        compiler_params=comm_params(1),
        name="slope_exchange",
    )(own)


def return_exchange(electric):
    return pl.pallas_call(
        return_kernel,
        out_shape=jax.ShapeDtypeStruct((4, 8, 8, 128), F32),
        in_specs=[COMM_SPEC],
        out_specs=COMM_SPEC,
        scratch_shapes=[DMA((3,)), DMA((3,)), DMA((1,))],
        compiler_params=comm_params(2),
        name="return_exchange",
    )(electric)


ROWS = 32
KF = 32


def pieces(value):
    first = value.astype(BF16).astype(F32)
    rest = value - first
    second = rest.astype(BF16).astype(F32)
    third = (rest - second).astype(BF16).astype(F32)
    return first, second, third


def cell_rows(ref, f, cells):
    return ref[pl.ds(f, cells, stride=8), :]


def source_features(ext_ref, coord, feat_f, feat_b, scale_row):
    cell = lax.broadcasted_iota(jnp.int32, (144, 128), 0)
    x = cell_rows(ext_ref, 0, 144) + (lax.div(cell, 24) - 3).astype(F32)
    y = cell_rows(ext_ref, 1, 144) + (lax.rem(lax.div(cell, 6), 4) - 2).astype(F32)
    z = cell_rows(ext_ref, 2, 144) + (lax.rem(cell, 6) - 3).astype(F32)
    if coord is not None:
        coord[0], coord[1], coord[2] = x, y, z
    scale = cell_rows(ext_ref, scale_row, 144)
    square = x * x + y * y + z * z
    k = 0
    for value in (scale, 2.0 * scale * x, 2.0 * scale * y, 2.0 * scale * z):
        first, second, third = pieces(value)
        for piece in (first, second, first, second, third, first):
            feat_f[pl.ds(k, 144, stride=KF), :] = piece
            k += 1
    for piece in pieces(-scale * square):
        feat_f[pl.ds(k, 144, stride=KF), :] = piece
        k += 1
    for k in range(k, KF):
        feat_f[pl.ds(k, 144, stride=KF), :] = jnp.zeros((144, 128), F32)
    feat_b[...] = feat_f[...].astype(BF16)


def target_features(own_ref, own_f, own_t, extra):
    cell = lax.broadcasted_iota(jnp.int32, (32, 128), 0)
    x = cell_rows(own_ref, 0, 32) + (lax.div(cell, 8) - 2).astype(F32)
    y = cell_rows(own_ref, 1, 32) + (lax.rem(lax.div(cell, 4), 2) - 1).astype(F32)
    z = cell_rows(own_ref, 2, 32) + (lax.rem(cell, 4) - 2).astype(F32)
    k = 0
    for value in (1.0 - (x * x + y * y + z * z), x, y, z):
        first, second, third = pieces(value)
        for piece in (first, first, second, second, first, third):
            own_f[pl.ds(k, 32, stride=KF), :] = piece
            k += 1
    for k in range(k, k + 3):
        own_f[pl.ds(k, 32, stride=KF), :] = jnp.ones((32, 128), F32)
    k = 27
    for value in extra:
        first, second, third = pieces(value)
        for piece in (first, second):
            own_f[pl.ds(k, 32, stride=KF), :] = piece
            k += 1
    for k in range(k, KF):
        own_f[pl.ds(k, 32, stride=KF), :] = jnp.zeros((32, 128), F32)

    def turn(t, _):
        own_t[t] = own_f[pl.ds(pl.multiple_of(t * KF, KF), KF), :].T.astype(BF16)
        return 0

    lax.fori_loop(0, 32, turn, 0)
    return x, y, z


def right_side(feat_b, cell):
    r = pl.multiple_of(cell * KF, KF)
    return jnp.concatenate([feat_b[pl.ds(r + KF * dz, KF), :] for dz in range(3)], axis=1)


def density_kernel(own_ref, ext_ref, density_ref, slope_ref, feat_f, feat_b, own_f, own_t, mat):
    source_features(ext_ref, None, feat_f, feat_b, 3)
    target_features(own_ref, own_f, own_t, ())
    mat[...] = jnp.zeros((128, 128), F32)
    lanes = lax.broadcasted_iota(jnp.int32, (128, 128), 1)
    other = lanes != lax.broadcasted_iota(jnp.int32, (128, 128), 0)

    def target(t, _):
        cx, cy, cz = lax.div(t, 8), lax.rem(lax.div(t, 4), 2), lax.rem(t, 4)
        left = own_t[t]
        total = jnp.zeros((128, 128), F32)
        for dx in range(3):
            for dy in range(3):
                right = right_side(feat_b, ((cx + dx) * 4 + cy + dy) * 6 + cz)
                weight = jnp.dot(left, right, preferred_element_type=F32)
                weight = jnp.maximum(weight, 0.0)
                for dz in range(3):
                    part = weight[:, dz * 128:(dz + 1) * 128]
                    if dx == 1 and dy == 1 and dz == 1:
                        part = jnp.where(other, part, 0.0)
                    total = total + part * part * part
        sums = jnp.sum(total, axis=1, keepdims=True)
        mat[...] = jnp.where(lanes == t, sums, mat[...])
        return 0

    lax.fori_loop(0, 32, target, 0)
    density = mat[...].T[0:32] * cell_rows(own_ref, 7, 32)
    density_ref[...] = density
    slope_ref[...] = (cell_rows(own_ref, 6, 32) / jnp.sqrt(1.0 + density)).reshape(32, 1, 128)


def force_kernel(count_ref, own_ref, ext_ref, gain_ref, slope_ref, out_ref, feat_f, feat_b, own_f, own_t, coord, wide,
                 near, prod, mat, items):
    source_features(ext_ref, coord, feat_f, feat_b, 4)
    x, y, z = target_features(own_ref, own_f, own_t, (gain_ref[0], gain_ref[2]))
    select = sel_matrix()

    def spread(r, _):
        for q in range(3):
            wide[r, q] = jnp.broadcast_to(coord[q, pl.ds(r, 1), :], (8, 128))
        wide[r, 3] = jnp.broadcast_to(ext_ref[pl.ds(r * 8 + 5, 1), :], (8, 128))
        wide[r, 4] = jnp.broadcast_to(slope_ref[r], (8, 128))
        return 0

    lax.fori_loop(0, 144, spread, 0)
    mat[...] = jnp.zeros((128, 128), F32)

    def list_target(t, n):
        def list_rows(c, n):
            items[n] = t * 4 + c
            return n + 1

        return lax.fori_loop(0, lax.div(count_ref[t] + ROWS - 1, ROWS), list_rows, n)

    count = lax.fori_loop(0, 32, list_target, 0)
    items[count] = 0
    lane = lax.broadcasted_iota(jnp.int32, (ROWS, 128), 1)
    lane3 = lax.broadcasted_iota(jnp.int32, (ROWS // 8, 8, 128), 2)
    row3 = lax.broadcasted_iota(jnp.int32, (ROWS // 8, 8, 128), 0) * 8 + lax.broadcasted_iota(
        jnp.int32, (ROWS // 8, 8, 128), 1)

    def place(n):
        item = items[n]
        t, c = lax.div(item, 4), lax.rem(item, 4)
        return t, c, lax.div(t, 8), lax.rem(lax.div(t, 4), 2), lax.rem(t, 4)

    def multiply(n, slot):
        t, c, cx, cy, cz = place(n)
        left = own_t[t, pl.ds(pl.multiple_of(c * ROWS, ROWS), ROWS), :]
        near[slot, :, 3456:3712] = jnp.dot(left, select, preferred_element_type=F32)
        for q in range(9):
            right = right_side(feat_b, ((cx + q // 3) * 4 + cy + q % 3) * 6 + cz)
            near[slot, :, q * 384:(q + 1) * 384] = jnp.dot(left, right, preferred_element_type=F32)

    def reduce(n, slot):
        t, c, cx, cy, cz = place(n)
        rows = pl.ds(pl.multiple_of(c * ROWS, ROWS), ROWS)
        value = mat[rows, :]
        for m in range(4):
            value = jnp.where(lane == t * 4 + m, jnp.sum(prod[slot, m], axis=1, keepdims=True), value)
        mat[rows, :] = value

    multiply(0, 0)

    def step(n, _):
        slot = lax.rem(n, 2)
        multiply(n + 1, 1 - slot)
        t, c, cx, cy, cz = place(n)

        def block(offset):
            return near[slot, :, offset:offset + 128].reshape(ROWS // 8, 8, 128)

        gain, tilt = block(3456), block(3584)
        zero = jnp.zeros((ROWS // 8, 8, 128), F32)
        m0, mx, my, mz = zero, zero, zero, zero
        for q in range(9):
            for dz in range(3):
                r = ((cx + q // 3) * 4 + cy + q % 3) * 6 + cz + dz
                w = jnp.maximum(block(q * 384 + dz * 128), 0.0)
                if q == 4 and dz == 1:
                    w = jnp.where(lane3 != row3 + c * ROWS, w, 0.0)
                value = ((tilt * wide[r, 3] + wide[r, 4]) * w + gain) * w
                m0 = m0 + value
                mx = mx + value * wide[r, 0]
                my = my + value * wide[r, 1]
                mz = mz + value * wide[r, 2]
        for m, value in enumerate((m0, mx, my, mz)):
            prod[slot, m] = value.reshape(ROWS, 128)

        @pl.when(n > 0)
        def _():
            reduce(n - 1, 1 - slot)

        return 0

    lax.fori_loop(0, count, step, 0)
    reduce(count - 1, lax.rem(count - 1, 2))
    mat[...] = mat[...].T

    whole = mat[pl.ds(0, 32, stride=4), :]
    for m, place_own in enumerate((x, y, z)):
        out_ref[m] = gain_ref[1] * (mat[pl.ds(m + 1, 32, stride=4), :] - place_own * whole)


def sel_matrix():
    row = lax.broadcasted_iota(jnp.int32, (KF, 256), 0)
    lane = lax.broadcasted_iota(jnp.int32, (KF, 256), 1)
    first = (row >= 27) & (row < 29) & (lane < 128)
    second = (row >= 29) & (row < 31) & (lane >= 128)
    return jnp.where(first | second, 1.0, 0.0).astype(BF16)


def features_scratch():
    return [
        pltpu.VMEM((144 * KF, 128), F32),
        pltpu.VMEM((144 * KF, 128), BF16),
        pltpu.VMEM((32 * KF, 128), F32),
        pltpu.VMEM((32, 128, KF), BF16),
    ]


def density_pass(own, ext):
    return pl.pallas_call(
        density_kernel,
        out_shape=[jax.ShapeDtypeStruct((32, 128), F32), jax.ShapeDtypeStruct((32, 1, 128), F32)],
        in_specs=[VMEM_SPEC] * 2,
        out_specs=[VMEM_SPEC] * 2,
        scratch_shapes=features_scratch() + [pltpu.VMEM((128, 128), F32)],
        compiler_params=pltpu.CompilerParams(vmem_limit_bytes=32 << 20),
        cost_estimate=pl.CostEstimate(flops=10_000_000_000, bytes_accessed=1_000_000, transcendentals=0),
        name="density_pass",
    )(own, ext)


def force_pass(counts, own, ext, gain, slope):
    return pl.pallas_call(
        force_kernel,
        out_shape=jax.ShapeDtypeStruct((3, 32, 128), F32),
        in_specs=[SMEM_SPEC] + [VMEM_SPEC] * 4,
        out_specs=VMEM_SPEC,
        scratch_shapes=features_scratch() + [
            pltpu.VMEM((3, 144, 128), F32),
            pltpu.VMEM((144, 5, 8, 128), F32),
            pltpu.VMEM((2, ROWS, 3712), F32),
            pltpu.VMEM((2, 4, ROWS, 128), F32),
            pltpu.VMEM((128, 128), F32),
            pltpu.SMEM((136,), jnp.int32),
        ],
        compiler_params=pltpu.CompilerParams(vmem_limit_bytes=48 << 20),
        cost_estimate=pl.CostEstimate(flops=20_000_000_000, bytes_accessed=1_000_000, transcendentals=0),
        name="force_pass",
    )(counts, own, ext, gain, slope)


EWALD_SPLIT = 0.7


def tables():
    mode = np.arange(256)[:, None]
    point = np.arange(256)[None, :]
    cosine = np.cos(2 * np.pi * (mode * point % 256) / 256) * np.sqrt(2 / 256)
    cosine[0] /= np.sqrt(2)
    cosine[128] /= np.sqrt(2)
    sine = np.sin(2 * np.pi * ((mode - 128) * point % 256) / 256) * np.sqrt(2 / 256)
    table = np.where(mode <= 128, cosine, sine)
    row = np.arange(512)
    xr, cell, s = row // 128, row // 8 % 16, row % 8
    mixed = table[:, cell * 16 + s % 4 * 4 + xr]
    return table, mixed


def halves(array):
    high = array.astype(np.float32).astype(jnp.bfloat16)
    low = (array - high.astype(np.float64)).astype(np.float32).astype(jnp.bfloat16)
    return np.stack([high, low])


def split(value):
    high = value.astype(BF16)
    return high, (value - high.astype(F32)).astype(BF16)


def dot(a, b):
    return jnp.dot(a, b, preferred_element_type=F32)


def dot3(a, b):
    return dot(a[0], b[0]) + (dot(a[1], b[0]) + dot(a[0], b[1]))


def hat(count, lower, weight):
    point = lax.broadcasted_iota(jnp.int32, (count, lower.shape[1]), 0).astype(F32)
    return jnp.where(point == lower, 1.0 - weight, 0.0) + jnp.where(point == lower + 1.0, weight, 0.0)


def spread_kernel(atoms_ref, table_ref, out_ref, rho):
    def layer(cz, _):
        base = lax.div(cz, 4) * 8 + lax.rem(cz, 4)

        def row(f, shift=0.0):
            first = atoms_ref[pl.ds(base * 8 + f, 1), :]
            second = atoms_ref[pl.ds((base + 4) * 8 + f, 1), :] + shift
            return jnp.concatenate([first, second], axis=1)

        ox, oy, oz, fx, fy, fz, charge = row(0), row(1, 16.0), row(2), row(3), row(4), row(5), row(6)
        wy = hat(32, oy, fy)
        wz = split(hat(16, oz, fz) * charge)
        parts = []
        for x in range(16):
            wx = jnp.where(ox == x, 1.0 - fx, 0.0) + jnp.where(ox == x - 1, fx, 0.0)
            parts.append(wx * wy)
        plane = split(jnp.concatenate(parts, axis=0))
        dims = (((1,), (1,)), ((), ()))

        def against(a, b):
            return lax.dot_general(a, b, dims, preferred_element_type=F32)

        value = against(wz[0], plane[0]) + (against(wz[1], plane[0]) + against(wz[0], plane[1]))
        rho[pl.ds(pl.multiple_of(cz * 16, 16), 16), :] = value
        return 0

    lax.fori_loop(0, 16, layer, 0)
    lines = dot3((table_ref[0], table_ref[1]), split(rho[...]))
    for plane in range(2):
        for xq in range(4):
            out_ref[pl.ds(plane * 4 + xq, 128, stride=8), :] = lines[
                plane * 128:(plane + 1) * 128, xq * 128:(xq + 1) * 128]


def plane_kernel(device_ref, in_ref, table_ref, turned_ref, mixed_ref, mixed_turned_ref, out_ref):
    lane = lax.broadcasted_iota(jnp.int32, (16, 8, 128), 2)

    def pick(ref, half, g):
        return jnp.concatenate([ref[gx, half * 4 + g] for gx in range(4)], axis=0)

    rows = []
    for xr in range(4):
        pair = []
        for half in range(2):
            value = jnp.zeros((16, 8, 128), F32)
            for g in range(4):
                block = pick(in_ref, half, g)
                if g != xr:
                    block = pltpu.roll(block.reshape(128, 128), (g - xr) * 32 % 128, 1).reshape(16, 8, 128)
                value = jnp.where(lax.div(lane, 32) == g, block, value)
            pair.append(value.reshape(128, 128))
        rows.append(jnp.concatenate(pair, axis=1))
    plane = jnp.concatenate(rows, axis=0)
    turned = (turned_ref[0], turned_ref[1])
    along_y = split(dot3(split(plane), turned))

    me = device_ref[0]
    row = lax.broadcasted_iota(jnp.int32, (256, 256), 0)
    col = lax.broadcasted_iota(jnp.int32, (256, 256), 1)
    scale = 2.0 * math.pi / 256
    wave_x = jnp.where(row <= 128, row, row - 128).astype(F32) * scale
    wave_y = jnp.where(col <= 128, col, col - 128).astype(F32) * scale
    flat = wave_x * wave_x + wave_y * wave_y
    side = lax.div(lax.rem(lax.broadcasted_iota(jnp.int32, (256, 512), 1), 8), 4)
    side_turned = lax.div(lax.rem(lax.broadcasted_iota(jnp.int32, (512, 256), 0), 8), 4)
    total = None
    for p in range(2):
        mode = me if p == 0 else jnp.where(me == 0, 128, me)
        wave_z = jnp.full((256, 256), mode, jnp.int32).astype(F32) * scale
        squared = flat + wave_z * wave_z
        anchor = squared == 0.0
        green = jnp.where(anchor, 0.0, 4.0 * math.pi * jnp.exp(-squared / (4.0 * EWALD_SPLIT * EWALD_SPLIT))
                          / jnp.where(anchor, 1.0, squared))
        left = [jnp.where(side == p, mixed_ref[i].astype(F32), 0.0).astype(BF16) for i in range(2)]
        modes = split(dot3(left, along_y) * green)
        back = [jnp.where(side_turned == p, mixed_turned_ref[i].astype(F32), 0.0).astype(BF16) for i in range(2)]
        part = dot3(back, modes)
        total = part if total is None else total + part
    field = dot3(split(total), (table_ref[0], table_ref[1]))
    for half in range(2):
        block = [field[xr * 128:(xr + 1) * 128, half * 128:(half + 1) * 128] for xr in range(4)]
        for g in range(4):
            value = jnp.zeros((16, 8, 128), F32)
            for xr in range(4):
                moved = block[xr]
                if g != xr:
                    moved = pltpu.roll(moved, (xr - g) * 32 % 128, 1)
                value = jnp.where(lax.div(lane, 32) == xr, moved.reshape(16, 8, 128), value)
            for gx in range(4):
                out_ref[gx, half * 4 + g] = value[gx * 4:(gx + 1) * 4]


def sample_kernel(in_ref, atoms_ref, turned_ref, out_ref, field):
    columns = [
        jnp.concatenate([in_ref[pl.ds(plane * 4 + xq, 128, stride=8), :] for xq in range(4)], axis=1)
        for plane in range(2)
    ]
    modes = jnp.concatenate(columns, axis=0)
    lines = jnp.concatenate([modes[:, i * 128:(i + 1) * 128].T for i in range(4)], axis=0)
    high, low = split(dot3(split(lines), (turned_ref[0], turned_ref[1])))
    for group in range(2):
        field[group, :, 0:128] = high[:, group * 128:(group + 1) * 128]
        field[group, :, 128:256] = low[:, group * 128:(group + 1) * 128]
    point = lax.broadcasted_iota(jnp.int32, (128, 128), 0).astype(F32)

    def cell(n, _):
        cyl, cz = lax.rem(n, 2), lax.div(n, 2)
        source = lax.div(cz, 4) * 8 + cyl * 4 + lax.rem(cz, 4)

        def row(f):
            return atoms_ref[pl.ds(source * 8 + f, 1), :]

        ox, oy, oz, fx, fy, fz, charge = [row(f) for f in range(7)]
        lower_z = oz + (lax.rem(cz, 8) * 16).astype(F32)
        lower = jnp.where(point == lower_z, 1.0, 0.0)
        slope = jnp.where(point == lower_z + 1.0, 1.0, 0.0) - lower
        right = jnp.concatenate([lower, slope], axis=1).astype(BF16)
        right = jnp.concatenate([right, right], axis=0)
        left = field_rows(field, lax.div(cz, 8), cyl)
        both = dot(left, right)
        tilt = both[:, 128:256].reshape(16, 16, 128)
        plain = both[:, 0:128].reshape(16, 16, 128) + fz * tilt
        spot = lax.broadcasted_iota(jnp.int32, (16, 128), 0).astype(F32)
        low_y, high_y = spot == oy, spot == oy + 1.0
        wy = jnp.where(low_y, 1.0 - fy, 0.0) + jnp.where(high_y, fy, 0.0)
        sy = jnp.where(high_y, 1.0, 0.0) - jnp.where(low_y, 1.0, 0.0)

        def fold(value):
            return value[:, 0:8] + value[:, 8:16]

        plain_w, plain_s, tilt_w = fold(plain * wy), fold(plain * sy), fold(tilt * wy)
        x_sum = jnp.zeros((8, 128), F32)
        y_sum, z_sum = x_sum, x_sum
        for x in range(16):
            low_x, high_x = ox == x, ox == x - 1
            wx = jnp.where(low_x, 1.0 - fx, 0.0) + jnp.where(high_x, fx, 0.0)
            sx = jnp.where(high_x, 1.0, 0.0) - jnp.where(low_x, 1.0, 0.0)
            x_sum = x_sum + sx * plain_w[x]
            y_sum = y_sum + wx * plain_s[x]
            z_sum = z_sum + wx * tilt_w[x]
        for f, value in enumerate((x_sum, y_sum, z_sum)):
            out_ref[pl.ds(source * 8 + f, 1), :] = -charge * jnp.sum(value, axis=0, keepdims=True)
        return 0

    lax.fori_loop(0, 32, cell, 0)


def field_rows(field, group, cyl):
    start = pl.multiple_of(cyl * 16, 16)
    return jnp.concatenate([field[group, pl.ds(start + 32 * x, 16), :] for x in range(16)], axis=0)


TABLE, MIXED = tables()


def constants():
    return (halves(TABLE), halves(TABLE.T), halves(MIXED), halves(MIXED.T))


def params(mib=32):
    return pltpu.CompilerParams(vmem_limit_bytes=mib << 20)


def spread_pass(atoms, table):
    return pl.pallas_call(
        spread_kernel,
        out_shape=jax.ShapeDtypeStruct((1024, 128), F32),
        in_specs=[VMEM_SPEC] * 2,
        out_specs=VMEM_SPEC,
        scratch_shapes=[pltpu.VMEM((256, 512), F32)],
        compiler_params=params(),
        name="spread_pass",
    )(atoms, table)


def plane_pass(device, planes, table, turned, mixed, mixed_turned):
    return pl.pallas_call(
        plane_kernel,
        out_shape=jax.ShapeDtypeStruct((4, 8, 4, 8, 128), F32),
        in_specs=[SMEM_SPEC] + [VMEM_SPEC] * 5,
        out_specs=VMEM_SPEC,
        compiler_params=params(),
        name="plane_pass",
    )(device, planes, table, turned, mixed, mixed_turned)


def sample_pass(lines, atoms, turned):
    return pl.pallas_call(
        sample_kernel,
        out_shape=jax.ShapeDtypeStruct((256, 128), F32),
        in_specs=[VMEM_SPEC] * 3,
        out_specs=VMEM_SPEC,
        scratch_shapes=[pltpu.VMEM((2, 512, 256), BF16)],
        compiler_params=params(),
        name="sample_pass",
    )(lines, atoms, turned)


def species_value(species, lookup_table):
    result = jnp.zeros(species.shape, F32)
    for kind_index in range(NSPEC):
        result = result + jnp.where(species == kind_index, lookup_table[kind_index], 0.0)
    return result


def on_device(cell_counts, grid_offset, fraction, species, species_density, species_pair, species_embed, species_charge):
    slots = lax.broadcasted_iota(jnp.int32, species.shape, 3)
    alive = (slots < cell_counts[..., None]).astype(F32)
    offset = grid_offset.astype(F32)
    positions = (offset + 0.5 + fraction) / PPC
    pair = species_pair
    root = species_value(species, jnp.cbrt(species_density)) * alive
    repulsion = species_value(species, pair) * alive
    ratio = species_value(species, species_density / (pair * pair))
    tilt = species_value(species, 3.0 * species_embed / (pair * pair)) * alive
    charge = species_value(species, species_charge) * alive
    zero = jnp.zeros_like(alive)
    rows = [positions[:, :, :, d] for d in range(3)] + [root, repulsion, ratio, tilt, alive]
    own = jnp.stack(rows, axis=3)
    rows = [offset[:, :, :, d] for d in range(3)] + [fraction[:, :, :, d] for d in range(3)] + [charge, zero]
    atoms = jnp.stack(rows, axis=3).reshape(4, 8, 8, 128)
    extended, columns = halo_exchange(own, atoms)
    own = own.reshape(256, 128)
    extended = extended.reshape(1152, 128)
    columns = columns.reshape(256, 128)
    table, turned, mixed, mixed_turned = constants()

    lines = spread_pass(columns, table).reshape(128, 8, 128)
    planes = lax.all_to_all(lines, AXES, split_axis=0, concat_axis=0, tiled=True)
    density, slope = density_pass(own, extended)
    device = (lax.axis_index("gx") * 32 + lax.axis_index("gy") * 4 + lax.axis_index("gz")).reshape(1)
    planes = plane_pass(device, planes.reshape(4, 8, 4, 8, 128), table, turned, mixed, mixed_turned)
    lines = lax.all_to_all(planes.reshape(128, 8, 128), AXES, split_axis=0, concat_axis=0, tiled=True)

    wide_slope = slope_exchange(slope.reshape(4, 2, 4, 1, 128)).reshape(144, 1, 128)
    gain = jnp.stack([
        species_value(species, -4.0 * pair / species_density).reshape(32, 128),
        species_value(species, species_density).reshape(32, 128),
        slope.reshape(32, 128) / ratio.reshape(32, 128),
    ])
    eam = force_pass(cell_counts.reshape(32), own, extended, gain, wide_slope)
    electric = sample_pass(lines.reshape(1024, 128), columns, table)
    electric = return_exchange(electric.reshape(4, 8, 8, 128)).reshape(4, 2, 4, 8, 128)[:, :, :, 0:3]
    eam = eam.reshape(3, 4, 2, 4, 128).transpose(1, 2, 3, 0, 4)
    forces = (eam + COUPLING * electric) * alive[:, :, :, None, :]
    return forces, density.reshape(4, 2, 4, 128)


def solution(mesh):
    return jax.shard_map(
        on_device,
        mesh=mesh,
        in_specs=(
            P("gx", "gy", "gz"),
            P("gx", "gy", "gz", None, None),
            P("gx", "gy", "gz", None, None),
            P("gx", "gy", "gz", None),
            P(),
            P(),
            P(),
            P(),
        ),
        out_specs=(P("gx", "gy", "gz", None, None), P("gx", "gy", "gz", None)),
        check_vma=False,
    )
```

time: 477 us -> 171 us (0.36)
  the two profiles are of different devices: /device:TPU:25 before, /device:TPU:1 now
where the time goes in v1:
time: 171 us; the launch traced here: 170 us
  Pallas kernels  141 us (82%)
  starting transfers between devices  12.2 us (7%)
  other arithmetic  10.8 us (6%)
  local copies, waits for them, and re-layouts  5.65 us (3%)
    pallas_call x1, Pallas kernels, force_pass(): pl.pallas_call(force_kernel, out_shape=jax.ShapeDtypeStruct((3, 32, 128),...  63.4 us
    pallas_call x1, Pallas kernels, density_pass(): pl.pallas_call(density_kernel, out_shape=[jax.ShapeDtypeStruct((32, 128),...  21.3 us
    pallas_call x1, Pallas kernels, halo_exchange(): pl.pallas_call(halo_kernel, out_shape=[jax.ShapeDtypeStruct((6, 4, 6, 8,...  18.3 us
    pallas_call x1, Pallas kernels, slope_exchange(): pl.pallas_call(slope_kernel, out_shape=jax.ShapeDtypeStruct((6, 4, 6, 1,...  11.7 us
    pallas_call x1, Pallas kernels, sample_pass(): pl.pallas_call(sample_kernel, out_shape=jax.ShapeDtypeStruct((256, 128),...  7.7 us
    mul x1, other arithmetic, on_device(): charge = species_value(species, species_charge) * alive  7.59 us
    pallas_call x1, Pallas kernels, return_exchange(): pl.pallas_call(return_kernel, out_shape=jax.ShapeDtypeStruct((4, 8, 8, 12...  7.35 us
    pallas_call x1, Pallas kernels, spread_pass(): pl.pallas_call(spread_kernel, out_shape=jax.ShapeDtypeStruct((1024, 128),...  6.95 us
  transfers between devices with their start and end apart: 2, of which 0 were waited for; matrix products, arithmetic and copies ran while one was open for 0% of the time, Pallas kernels for 57%

profile of v1, /device:TPU:1, one launch (start us, length us, event | category | flops | bytes accessed | tf_op | source)
XLA Modules:
  0.0 170.1 jit_solution(14200161717928117493)
XLA Ops:
  0.6 0.0 copy-start.9
  0.6 1.4 fusion.4
  2.0 0.0 copy-done.9
  2.0 0.0 copy-start.8
  2.0 0.0 copy-start.11
  2.0 0.6 fusion.8
  2.6 0.0 copy-done.8
  2.7 0.0 copy-done.11
  2.7 0.0 copy-start.10
  2.7 0.6 copy-done.10
  3.4 0.6 fusion.5
  4.0 0.0 copy-start.4
  4.0 0.0 copy-start.6
  4.0 0.9 copy_convert_fusion
  4.9 0.0 copy-done.4
  4.9 0.0 copy-done.6
  4.9 0.0 copy-start.5
  5.0 0.6 copy-done.5
  5.6 0.1 compare_convert_fusion
  5.7 0.0 copy-start.7
  5.7 0.7 fusion.9
  6.4 0.7 fusion.6
  7.0 0.1 pad.6.clone
  7.1 0.0 copy-done.7
  7.1 1.4 select_add_fusion.1
  8.5 7.6 %add_select_fusion = (f32[4,2,4,128]{3,2,1,0:T(4,128)S(1)}, f32[4,2,4,128]{3,2,1,0:T(4,128)S(1)}, f32[4,2,4,128]{3,2,1,0:T(4,128)S(1)}, f32[4,2,4,128]{3,2,1,0:T...) fusion(pred[4,2,4,128]{3,2,1,0:T(4,128)(4,1)S(1)} %get-tuple-element.12, ...), kind=kLoop, calls=%fused_computation.11 | loop fusion | flops 94208 | bytes 106672 | tf_op jit(solution)/shard_map/mul | solution.py:659
  16.1 0.1 maximum_maximum_fusion.atoms_ref
  16.2 0.0 copy-start
  16.2 0.2 stack.35.own_ref
  16.3 18.3 %halo_exchange.1 = (f32[6,4,6,8,128]{4,3,2,1,0:T(8,128)S(1)}, f32[4,8,8,128]{3,2,1,0:T(8,128)S(1)}) custom-call(f32[4,2,4,8,128]{4,3,2,1,0:T(8,128)S(1)} %stack.35.own_ref, f32[4,8,8,128]{3,2,1,0:T(8,128)S(1)} %maximum_maximum_fusion.atoms_ref), custom_call_target="tpu_custom_call" | custom-call | tf_op jit(solution)/shard_map/halo_exchange/pallas_call | solution.py:120
  34.6 0.0 copy-done
  34.6 7.0 %spread_pass.1 = f32[1024,128]{1,0:T(8,128)} custom-call(f32[256,128]{1,0:T(8,128)S(1)} %bitcast.54, bf16[2,256,256]{2,1,0:T(8,128)(2,1)S(1)} %copy-done), custom_call_target="tpu_custom_call" | custom-call | tf_op jit(solution)/shard_map/spread_pass/pallas_call | solution.py:608
  41.6 5.5 %all-to-all-start = ((f32[128,8,128]{2,1,0:T(8,128)}), f32[128,8,128]{2,1,0:T(8,128)S(1)}, u32[]{:S(2)}, u32[]{:S(2)}) async-start(f32[128,8,128]{2,1,0:T(8,128)} %bitcast.36), calls=%async_computation | async-start | bytes 1048576 | tf_op jit(solution)/shard_map/all_to_all | solution.py:672
  47.0 0.0 copy-start.1
  47.1 0.0 copy-start.2
  47.1 21.3 %density_pass.1 = (f32[32,128]{1,0:T(8,128)}, f32[32,1,128]{2,1,0:T(1,128)S(1)}) custom-call(f32[256,128]{1,0:T(8,128)S(1)} %bitcast.52, f32[1152,128]{1,0:T(8,128)S(1)} %bitcast.62), custom_call_target="tpu_custom_call" | custom-call | flops 10000000000 | bytes 1000000 | tf_op jit(solution)/shard_map/density_pass/pallas_call | solution.py:371
  68.4 0.0 copy-start.3
  68.4 0.1 reshape.90.count_ref
  68.5 11.7 %slope_exchange.1 = f32[6,4,6,1,128]{4,3,2,1,0:T(1,128)S(1)} custom-call(f32[4,2,4,1,128]{4,3,2,1,0:T(1,128)S(1)} %bitcast.59), custom_call_target="tpu_custom_call" | custom-call | tf_op jit(solution)/shard_map/slope_exchange/pallas_call | solution.py:132
  80.2 0.0 all-to-all-done
  80.2 0.0 copy-done.1
  80.2 0.0 copy-done.2
  80.2 0.0 copy-done.3
  80.3 3.9 %plane_pass.1 = f32[4,8,4,8,128]{4,3,2,1,0:T(8,128)} custom-call(s32[1]{0:T(128)} %bitcast.34.device_ref, f32[4,8,4,8,128]{4,3,2,1,0:T(8,128)S(1)} %bitcast.51, bf16[2,256,256]{2,1,0:T(8,128)(2,1)S(1)} %copy-done, bf16[2,256,256]{2,1,0:T(8,128)(2,1)S(1)} %copy-done.3, bf16[2,256,512]{2,1,0:T(8,128)(2,1)S(1)} %copy-done.1, bf16[2,512,256]{2,1,0:T(8,128)(2,1)S(1)} %copy-done.2), custom_call_target="tpu_custom_call" | custom-call | tf_op jit(solution)/shard_map/plane_pass/pallas_call | solution.py:620
  84.1 6.7 %all-to-all-start.1 = ((f32[128,8,128]{2,1,0:T(8,128)}), f32[128,8,128]{2,1,0:T(8,128)S(1)}, u32[]{:S(2)}, u32[]{:S(2)}) async-start(f32[128,8,128]{2,1,0:T(8,128)} %bitcast.38), calls=%async_computation.1 | async-start | bytes 1048576 | tf_op jit(solution)/shard_map/all_to_all | solution.py:676
  90.9 63.4 %force_pass.1 = f32[3,32,128]{2,1,0:T(8,128)S(1)} custom-call(s32[32]{0:T(128)S(1)} %reshape.90.count_ref, f32[256,128]{1,0:T(8,128)S(1)} %bitcast.53, f32[1152,128]{1,0:T(8,128)S(1)} %bitcast.63, f32[3,32,128]{2,1,0:T(8,128)S(1)} %pad_maximum_fusion.gain_ref, f32[144,1,128]{2,1,0:T(1,128)S(1)} %bitcast.58), custom_call_target="tpu_custom_call" | custom-call | flops 20000000000 | bytes 1000000 | tf_op jit(solution)/shard_map/force_pass/pallas_call | solution.py:384
  154.3 0.1 fusion.2
  154.4 0.0 all-to-all-done.1
  154.4 7.7 %sample_pass.1 = f32[256,128]{1,0:T(8,128)S(1)} custom-call(f32[1024,128]{1,0:T(8,128)S(1)} %bitcast.50, f32[256,128]{1,0:T(8,128)S(1)} %bitcast.55, bf16[2,256,256]{2,1,0:T(8,128)(2,1)S(1)} %copy-done), custom_call_target="tpu_custom_call" | custom-call | tf_op jit(solution)/shard_map/sample_pass/pallas_call | solution.py:631
  162.1 7.3 %return_exchange.1 = f32[4,8,8,128]{3,2,1,0:T(8,128)S(1)} custom-call(f32[4,8,8,128]{3,2,1,0:T(8,128)S(1)} %bitcast.56), custom_call_target="tpu_custom_call" | custom-call | tf_op jit(solution)/shard_map/return_exchange/pallas_call | solution.py:144
  169.5 0.6 fusion.1
  (5 shorter events, 0.1 us)
Async XLA Ops:
  0.6 1.4 copy-start.9
  2.0 0.7 copy-start.8
  2.0 0.7 copy-start.11
  2.7 0.7 copy-start.10
  4.0 0.9 copy-start.4
  4.0 0.9 copy-start.6
  4.9 0.7 copy-start.5
  5.7 1.4 copy-start.7
  16.2 18.4 %copy-start = (bf16[2,256,256]{2,1,0:T(8,128)(2,1)S(1)}, bf16[2,256,256]{2,1,0:T(8,128)(2,1)}, u32[]{:S(2)}) copy-start(bf16[2,256,256]{2,1,0:T(8,128)(2,1)} %constant.47.clone.table_ref.turned_ref) | copy-start | bytes 786436
  41.6 38.6 %all-to-all-start = ((f32[128,8,128]{2,1,0:T(8,128)}), f32[128,8,128]{2,1,0:T(8,128)S(1)}, u32[]{:S(2)}, u32[]{:S(2)}) async-start(f32[128,8,128]{2,1,0:T(8,128)} %bitcast.36), calls=%async_computation | async-start | bytes 1048576 | tf_op jit(solution)/shard_map/all_to_all | solution.py:672
  47.0 33.2 %copy-start.1 = (bf16[2,256,512]{2,1,0:T(8,128)(2,1)S(1)}, bf16[2,256,512]{2,1,0:T(8,128)(2,1)}, u32[]{:S(2)}) copy-start(bf16[2,256,512]{2,1,0:T(8,128)(2,1)} %constant.49.clone.mixed_ref) | copy-start | bytes 1572868
  47.1 33.2 %copy-start.2 = (bf16[2,512,256]{2,1,0:T(8,128)(2,1)S(1)}, bf16[2,512,256]{2,1,0:T(8,128)(2,1)}, u32[]{:S(2)}) copy-start(bf16[2,512,256]{2,1,0:T(8,128)(2,1)} %constant.50.clone.mixed_turned_ref) | copy-start | bytes 1572868
  68.4 11.8 %copy-start.3 = (bf16[2,256,256]{2,1,0:T(8,128)(2,1)S(1)}, bf16[2,256,256]{2,1,0:T(8,128)(2,1)}, u32[]{:S(2)}) copy-start(bf16[2,256,256]{2,1,0:T(8,128)(2,1)} %constant.48.clone.turned_ref) | copy-start | bytes 786436
  84.1 70.3 %all-to-all-start.1 = ((f32[128,8,128]{2,1,0:T(8,128)}), f32[128,8,128]{2,1,0:T(8,128)S(1)}, u32[]{:S(2)}, u32[]{:S(2)}) async-start(f32[128,8,128]{2,1,0:T(8,128)} %bitcast.38), calls=%async_computation.1 | async-start | bytes 1048576 | tf_op jit(solution)/shard_map/all_to_all | solution.py:676

commit v2 on v1

v2 whole, which is shorter than its diff:
```python
import itertools
import math

import jax
import jax.numpy as jnp
import numpy as np
from jax import lax
from jax.experimental import pallas as pl
from jax.experimental.pallas import tpu as pltpu
from jax.sharding import PartitionSpec as P

PPC = 16
COUPLING = 8.0
F32, BF16 = jnp.float32, jnp.bfloat16
VMEM_SPEC = pl.BlockSpec(memory_space=pltpu.VMEM)
SMEM_SPEC = pl.BlockSpec(memory_space=pltpu.SMEM)


MESH = pl.DeviceIdType.MESH
AXES = ("gx", "gy", "gz")
SIZES = (4, 8, 4)
SIDES = [side for side in itertools.product((-1, 0, 1), repeat=3) if side != (0, 0, 0)]


def here():
    return [lax.axis_index(axis) for axis in AXES]


def toward(place, side):
    return tuple(lax.rem(p + s + n, n) for p, s, n in zip(place, side, SIZES))


def signal(devices):
    barrier = pltpu.get_barrier_semaphore()
    for device in devices:
        pl.semaphore_signal(barrier, inc=1, device_id=device, device_id_type=MESH)


def await_signals(count):
    pl.semaphore_wait(pltpu.get_barrier_semaphore(), count)


def send(src, dst, send_sem, recv_sem, device):
    copy = pltpu.make_async_remote_copy(
        src_ref=src, dst_ref=dst, send_sem=send_sem, recv_sem=recv_sem, device_id=device, device_id_type=MESH)
    copy.start()
    return copy


def halo_copies(own_ref, rim, ext_ref, place, send_sem, recv_sem):
    copies = []
    for n, side in enumerate(SIDES):
        src, dst = [], []
        for s, cells in zip(side, (4, 2, 4)):
            src.append(pl.ds(rim, cells) if s == 0 else pl.ds(rim + (cells - 1 if s == 1 else 0), 1))
            dst.append(pl.ds(1, cells) if s == 0 else pl.ds(0 if s == 1 else cells + 1, 1))
        copies.append(send(own_ref.at[tuple(src)], ext_ref.at[tuple(dst)], send_sem.at[n], recv_sem.at[n],
                           toward(place, side)))
    return copies


def column_copy(src_ref, dst_ref, place, send_sem, recv_sem, n):
    gx, gy, gz = place
    other = lax.rem(gz + n + 1, 4)
    return send(src_ref.at[other], dst_ref.at[gz], send_sem.at[n], recv_sem.at[n], (gx, gy, other))


def column_copies(src_ref, dst_ref, place, send_sem, recv_sem):
    return [column_copy(src_ref, dst_ref, place, send_sem, recv_sem, n) for n in range(3)]


def column_devices(place):
    gx, gy, gz = place
    return [(gx, gy, lax.rem(gz + n + 1, 4)) for n in range(3)]


DMA = pltpu.SemaphoreType.DMA


def comm_params(number):
    return pltpu.CompilerParams(collective_id=number, has_side_effects=True, vmem_limit_bytes=32 << 20)


ROWS = 16
KF = 32


def pieces(value):
    first = value.astype(BF16).astype(F32)
    rest = value - first
    second = rest.astype(BF16).astype(F32)
    third = (rest - second).astype(BF16).astype(F32)
    return first, second, third


def by_species(code, values):
    return jnp.where(code == 0.0, values[0], jnp.where(code == 1.0, values[1], 0.0))


def filled(ref, k):
    return jnp.full((8, 128), ref[k], F32)


def cube_root(value):
    guess = jnp.exp(jnp.log(value) * (1.0 / 3.0))
    return guess - (guess * guess * guess - value) / (3.0 * guess * guess)


def sublane():
    return lax.broadcasted_iota(jnp.int32, (8, 128), 0)


def assemble(blocks, ones, twos):
    rows = []
    for value, one, two in zip(blocks, ones, twos):
        first, second, third = pieces(value)
        rows.append(jnp.where(one, first, jnp.where(two, second, third)))
    return jnp.concatenate(rows, axis=0)


def patterns(first, second, last_first, last_second):
    ones, twos = [], []
    for block in range(4):
        one = two = None
        for k in range(block * 8, block * 8 + 8):
            here_one = (k % 6 in first) if k < 24 else k in last_first
            here_two = (k % 6 in second) if k < 24 else k in last_second
            if here_one:
                one = (sublane() == k % 8) if one is None else one | (sublane() == k % 8)
            if here_two:
                two = (sublane() == k % 8) if two is None else two | (sublane() == k % 8)
        ones.append(one)
        twos.append(two)
    return ones, twos


def source_features(ext_ref, slope_ref, wide, feat_b, scales, ratios):
    ones, twos = patterns((0, 2, 5), (1, 3), (24,), (25,))
    low_six, low_four, low_two, low_three = [sublane() < n for n in (6, 4, 2, 3)]

    def cell(r, _):
        def row(f):
            return jnp.broadcast_to(ext_ref[r, f:f + 1, :], (8, 128))

        x = row(0) + (lax.div(r, 24) - 3).astype(F32)
        y = row(1) + (lax.rem(lax.div(r, 6), 4) - 2).astype(F32)
        z = row(2) + (lax.rem(r, 6) - 3).astype(F32)
        code = row(3)
        scale = by_species(code, scales)
        if wide is not None:
            wide[r, 0], wide[r, 1], wide[r, 2] = x, y, z
            wide[r, 3] = jnp.where(code == 1.0, ratios[1], ratios[0])
            wide[r, 4] = jnp.broadcast_to(slope_ref[r], (8, 128))
        square = -scale * (x * x + y * y + z * z)
        double = scale + scale
        x, y, z = double * x, double * y, double * z
        blocks = [jnp.where(low_six, scale, x), jnp.where(low_four, x, y), jnp.where(low_two, y, z),
                  jnp.where(low_three, square, 0.0)]
        feat_b[pl.ds(pl.multiple_of(r * KF, KF), KF), :] = assemble(blocks, ones, twos).astype(BF16)
        return 0

    lax.fori_loop(0, 144, cell, 0, unroll=4)


def corner(t):
    return (lax.div(t, 8) * 4 + lax.rem(lax.div(t, 4), 2)) * 6 + lax.rem(t, 4)


def target_features(ext_ref, own_t, keep, slope_ref, gains, ratios):
    ones, twos = patterns((0, 1, 4), (2, 3), (24, 25, 26, 27, 29), (28, 30))
    low_six, low_four, low_two, low_three = [sublane() < n for n in (6, 4, 2, 3)]
    low_five, low_seven = sublane() < 5, sublane() < 7

    def cell(t, _):
        r = corner(t) + 31

        def row(f):
            return jnp.broadcast_to(ext_ref[r, f:f + 1, :], (8, 128))

        x = row(0) + (lax.div(t, 8) - 2).astype(F32)
        y = row(1) + (lax.rem(lax.div(t, 4), 2) - 1).astype(F32)
        z = row(2) + (lax.rem(t, 4) - 2).astype(F32)
        code = row(3)
        for n, value in enumerate((x, y, z, code)):
            keep[n, pl.ds(t, 1), :] = value[0:1]
        rest = 1.0 - (x * x + y * y + z * z)
        tail = jnp.zeros((8, 128), F32)
        if gains is not None:
            second = code == 1.0
            tilt = jnp.broadcast_to(slope_ref[r], (8, 128)) / jnp.where(second, ratios[1], ratios[0])
            tail = jnp.where(low_five, jnp.where(second, gains[1], gains[0]), jnp.where(low_seven, tilt, 0.0))
        blocks = [jnp.where(low_six, rest, x), jnp.where(low_four, x, y), jnp.where(low_two, y, z),
                  jnp.where(low_three, 1.0, tail)]
        own_t[t] = assemble(blocks, ones, twos).T.astype(BF16)
        return 0

    lax.fori_loop(0, 32, cell, 0, unroll=4)


def right_side(feat_b, cell):
    r = pl.multiple_of(cell * KF, KF)
    return jnp.concatenate([feat_b[pl.ds(r + KF * dz, KF), :] for dz in range(3)], axis=1)


def density_kernel(amplitude_ref, pair_ref, embed_ref, ext_ref, density_ref, slope_ref, feat_b, own_t, keep, mat):
    amplitudes, pairs, embeds = [[filled(ref, k) for k in range(2)] for ref in (amplitude_ref, pair_ref, embed_ref)]
    source_features(ext_ref, None, None, feat_b, [cube_root(value) for value in amplitudes], None)
    target_features(ext_ref, own_t, keep, None, None, None)
    mat[...] = jnp.zeros((128, 128), F32)
    lanes = lax.broadcasted_iota(jnp.int32, (128, 128), 1)
    other = lanes != lax.broadcasted_iota(jnp.int32, (128, 128), 0)

    def target(t):
        cx, cy, cz = lax.div(t, 8), lax.rem(lax.div(t, 4), 2), lax.rem(t, 4)
        left = own_t[t]
        total = jnp.zeros((128, 128), F32)
        for dx in range(3):
            for dy in range(3):
                right = right_side(feat_b, ((cx + dx) * 4 + cy + dy) * 6 + cz)
                weight = jnp.dot(left, right, preferred_element_type=F32)
                weight = jnp.maximum(weight, 0.0)
                for dz in range(3):
                    part = weight[:, dz * 128:(dz + 1) * 128]
                    if dx == 1 and dy == 1 and dz == 1:
                        part = jnp.where(other, part, 0.0)
                    total = total + part * part * part
        sums = jnp.sum(total, axis=1, keepdims=True)
        return sums

    def both(n, _):
        first, second = target(2 * n), target(2 * n + 1)
        mat[...] = jnp.where(lanes == 2 * n, first, jnp.where(lanes == 2 * n + 1, second, mat[...]))
        return 0

    lax.fori_loop(0, 16, both, 0)
    code = keep[3]
    alive = by_species(code, (1.0, 1.0))
    density = mat[...].T[0:32] * alive
    density_ref[...] = density.reshape(8, 4, 128)
    tilts = [jnp.concatenate([3.0 * embed / (pair * pair)] * 4, axis=0) for embed, pair in zip(embeds, pairs)]
    slope_ref[...] = (by_species(code, tilts) / jnp.sqrt(1.0 + density)).reshape(32, 1, 128)


def force_kernel(count_ref, amplitude_ref, pair_ref, ext_ref, slope_ref, out_ref, feat_b, own_t, keep, wide, near_a, near_b,
                 mat, table):
    amplitudes, pairs = [[filled(ref, k) for k in range(2)] for ref in (amplitude_ref, pair_ref)]
    ratios = [amplitude / (pair * pair) for amplitude, pair in zip(amplitudes, pairs)]
    gains = [-4.0 * pair / amplitude for amplitude, pair in zip(amplitudes, pairs)]
    source_features(ext_ref, slope_ref, wide, feat_b, pairs, ratios)
    target_features(ext_ref, own_t, keep, slope_ref, gains, ratios)
    feat_b[144 * KF:146 * KF, :] = jnp.concatenate([sel_matrix()[:, 0:128], sel_matrix()[:, 128:256]], axis=0)

    def fill(n, _):
        table[n] = jnp.where(n < 27, (lax.div(n, 9) * 4 + lax.rem(lax.div(n, 3), 3)) * 6 + lax.rem(n, 3),
                             jnp.where(n == 28, 145, 144))
        table[32 + n] = jnp.where(n < 27, 1, 0)
        return 0

    lax.fori_loop(0, 32, fill, 0)
    mat[...] = jnp.zeros((128, 128), F32)
    lane = lax.broadcasted_iota(jnp.int32, (ROWS, 128), 1)
    lane3 = lax.broadcasted_iota(jnp.int32, (ROWS // 8, 8, 128), 2)
    row3 = lax.broadcasted_iota(jnp.int32, (ROWS // 8, 8, 128), 0) * 8 + lax.broadcasted_iota(
        jnp.int32, (ROWS // 8, 8, 128), 1)

    def around(base, k):
        return base + (k // 9 * 4 + k // 3 % 3) * 6 + k % 3

    def multiply(t, near, part):
        left, base = own_t[t], corner(t)
        for k in range(0, 8, 2):
            right = []
            for n in (part * 8 + k, part * 8 + k + 1):
                start = pl.multiple_of((table[n] + table[32 + n] * base) * KF, KF)
                right.append(feat_b[pl.ds(start, KF), :])
            product = jnp.dot(left, jnp.concatenate(right, axis=1), preferred_element_type=F32)
            near[part * 8 + k] = product[:, 0:128]
            near[part * 8 + k + 1] = product[:, 128:256]

    def chunk(t, near, c):
        rows = pl.ds(pl.multiple_of(c * ROWS, ROWS), ROWS)
        base = corner(t)

        def block(k):
            return near[k, rows, :].reshape(ROWS // 8, 8, 128)

        gain, tilt = block(27), block(28)
        zero = jnp.zeros((ROWS // 8, 8, 128), F32)
        m0, mx, my, mz = zero, zero, zero, zero
        for k in range(27):
            r = around(base, k)
            w = jnp.maximum(block(k), 0.0)
            if k == 13:
                w = jnp.where(lane3 != row3 + c * ROWS, w, 0.0)
            value = ((tilt * wide[r, 3] + wide[r, 4]) * w + gain) * w
            m0 = m0 + value
            mx = mx + value * wide[r, 0]
            my = my + value * wide[r, 1]
            mz = mz + value * wide[r, 2]
        old = mat[rows, :]
        for m, value in enumerate((m0, mx, my, mz)):
            total = jnp.sum(value.reshape(ROWS, 128), axis=1, keepdims=True)
            old = jnp.where(lane == t * 4 + m, total, old)
        mat[rows, :] = old

    for part in range(4):
        multiply(0, near_a, part)

    def target(t, near, following):
        later = jnp.minimum(t + 1, 31)

        def rest(c, _):
            chunk(t, near, c)
            return 0

        for part in range(4):
            multiply(later, following, part)
            chunk(t, near, part)
        lax.fori_loop(4, lax.div(count_ref[t] + ROWS - 1, ROWS), rest, 0)

    def pair(n, _):
        target(2 * n, near_a, near_b)
        target(2 * n + 1, near_b, near_a)
        return 0

    lax.fori_loop(0, 16, pair, 0)
    mat[...] = mat[...].T

    whole = mat[pl.ds(0, 32, stride=4), :]
    amplitude = by_species(keep[3], [jnp.concatenate([value] * 4, axis=0) for value in amplitudes])
    for m in range(3):
        out_ref[m] = amplitude * (mat[pl.ds(m + 1, 32, stride=4), :] - keep[m] * whole)


def sel_matrix():
    row = lax.broadcasted_iota(jnp.int32, (KF, 256), 0)
    lane = lax.broadcasted_iota(jnp.int32, (KF, 256), 1)
    first = (row >= 27) & (row < 29) & (lane < 128)
    second = (row >= 29) & (row < 31) & (lane >= 128)
    return jnp.where(first | second, 1.0, 0.0).astype(BF16)


def features_scratch():
    return [pltpu.VMEM((146 * KF, 128), BF16), pltpu.VMEM((32, 128, KF), BF16), pltpu.VMEM((4, 32, 128), F32)]


def density_pass(amplitude, pair, embed, ext):
    return pl.pallas_call(
        density_kernel,
        out_shape=[jax.ShapeDtypeStruct((8, 4, 128), F32), jax.ShapeDtypeStruct((32, 1, 128), F32)],
        in_specs=[SMEM_SPEC] * 3 + [VMEM_SPEC],
        out_specs=[VMEM_SPEC] * 2,
        scratch_shapes=features_scratch() + [pltpu.VMEM((128, 128), F32)],
        compiler_params=pltpu.CompilerParams(vmem_limit_bytes=16 << 20),
        cost_estimate=pl.CostEstimate(flops=10_000_000_000, bytes_accessed=1_000_000, transcendentals=0),
        name="density_pass",
    )(amplitude, pair, embed, ext)


def force_pass(counts, amplitude, pair, ext, slope):
    return pl.pallas_call(
        force_kernel,
        out_shape=jax.ShapeDtypeStruct((3, 32, 128), F32),
        in_specs=[SMEM_SPEC] * 3 + [VMEM_SPEC] * 2,
        out_specs=VMEM_SPEC,
        scratch_shapes=features_scratch() + [
            pltpu.VMEM((144, 5, 8, 128), F32),
            pltpu.VMEM((32, 128, 128), F32),
            pltpu.VMEM((32, 128, 128), F32),
            pltpu.VMEM((128, 128), F32),
            pltpu.SMEM((64,), jnp.int32),
        ],
        compiler_params=pltpu.CompilerParams(vmem_limit_bytes=24 << 20),
        cost_estimate=pl.CostEstimate(flops=20_000_000_000, bytes_accessed=1_000_000, transcendentals=0),
        name="force_pass",
    )(counts, amplitude, pair, ext, slope)


EWALD_SPLIT = 0.7


def tables():
    mode = np.arange(256)[:, None]
    point = np.arange(256)[None, :]
    cosine = np.cos(2 * np.pi * (mode * point % 256) / 256) * np.sqrt(2 / 256)
    cosine[0] /= np.sqrt(2)
    cosine[128] /= np.sqrt(2)
    sine = np.sin(2 * np.pi * ((mode - 128) * point % 256) / 256) * np.sqrt(2 / 256)
    table = np.where(mode <= 128, cosine, sine)
    row = np.arange(512)
    xr, cell, s = row // 128, row // 8 % 16, row % 8
    mixed = table[:, cell * 16 + s % 4 * 4 + xr]
    return table, mixed


def parts_of(array):
    parts = []
    for _ in range(3):
        parts.append(array.astype(np.float32).astype(jnp.bfloat16))
        array = array - parts[-1].astype(np.float64)
    return np.stack(parts)


def split(value):
    high = value.astype(BF16)
    return high, (value - high.astype(F32)).astype(BF16)


def dot(a, b):
    return jnp.dot(a, b, preferred_element_type=F32)


def dot3(a, b):
    return dot(a[0], b[0]) + (dot(a[1], b[0]) + dot(a[0], b[1]))


def split3(value):
    first = value.astype(BF16)
    rest = value - first.astype(F32)
    second = rest.astype(BF16)
    return first, second, (rest - second.astype(F32)).astype(BF16)


def dot6(a, b):
    small = dot(a[1], b[1]) + (dot(a[2], b[0]) + dot(a[0], b[2]))
    return dot(a[0], b[0]) + (dot(a[1], b[0]) + dot(a[0], b[1]) + small)


def hat(count, lower, weight):
    point = lax.broadcasted_iota(jnp.int32, (count, lower.shape[1]), 0).astype(F32)
    return jnp.where(point == lower, 1.0 - weight, 0.0) + jnp.where(point == lower + 1.0, weight, 0.0)


def spread_and_transform(atoms_ref, charges, table_ref, out_ref, rho):
    def layer(cz, _):
        source, cell = lax.div(cz, 4), lax.rem(cz, 4)

        def row(f, shift=0.0):
            first = atoms_ref[source, cell, f:f + 1, :]
            second = atoms_ref[source, cell + 4, f:f + 1, :] + shift
            return jnp.concatenate([first, second], axis=1)

        ox, oy, oz, fx, fy, fz = row(0), row(1, 16.0), row(2), row(3), row(4), row(5)
        charge = by_species(row(6), charges)
        wy = hat(32, oy, fy)
        wz = split(hat(16, oz, fz) * charge)
        parts = []
        for x in range(16):
            wx = jnp.where(ox == x, 1.0 - fx, 0.0) + jnp.where(ox == x - 1, fx, 0.0)
            parts.append(wx * wy)
        plane = split(jnp.concatenate(parts, axis=0))
        dims = (((1,), (1,)), ((), ()))

        def against(a, b):
            return lax.dot_general(a, b, dims, preferred_element_type=F32)

        value = against(wz[0], plane[0]) + (against(wz[1], plane[0]) + against(wz[0], plane[1]))
        rho[pl.ds(pl.multiple_of(cz * 16, 16), 16), :] = value
        return 0

    lax.fori_loop(0, 16, layer, 0)
    lines = dot3((table_ref[0], table_ref[1]), split(rho[...]))
    for plane in range(2):
        for xq in range(4):
            out_ref[pl.ds(plane * 4 + xq, 128, stride=8), :] = lines[
                plane * 128:(plane + 1) * 128, xq * 128:(xq + 1) * 128]


def gather_kernel(charge_ref, count_ref, offset_ref, fraction_ref, species_ref, table_ref, ext_ref, got_ref, out_ref,
                  atoms, rho, send_sem, recv_sem, column_send, column_recv):
    place = here()
    signal([toward(place, side) for side in SIDES] + [column_devices(place)[1]])
    slot = lax.broadcasted_iota(jnp.int32, (1, 128), 1)

    def pack(t, _):
        x, y, z = lax.div(t, 8), lax.rem(lax.div(t, 4), 2), lax.rem(t, 4)
        offset, fraction = offset_ref[t].astype(F32), fraction_ref[t]
        kind = species_ref[lax.div(t, 4), pl.ds(z, 1), :].astype(F32)
        code = jnp.where(slot < count_ref[t], kind, -1.0)
        ext_ref[x + 1, y + 1, z + 1, 0:3, :] = (offset + 0.5 + fraction) * (1.0 / PPC)
        ext_ref[x + 1, y + 1, z + 1, 3:4, :] = code
        atoms[x, y * 4 + z, 0:3, :] = offset
        atoms[x, y * 4 + z, 3:6, :] = fraction
        atoms[x, y * 4 + z, 6:7, :] = code
        atoms[x, y * 4 + z, 7:8, :] = code
        return 0

    lax.fori_loop(0, 32, pack, 0)

    def keep(n, _):
        got_ref[place[2], n] = atoms[place[2], n]
        return 0

    lax.fori_loop(0, 8, keep, 0)
    await_signals(27)
    columns = column_copies(atoms, got_ref, place, column_send, column_recv)
    halo = halo_copies(ext_ref, 1, ext_ref, place, send_sem, recv_sem)
    for copy in columns:
        copy.wait()
    spread_and_transform(got_ref, [charge_ref[k] for k in range(2)], table_ref, out_ref, rho)
    for copy in halo:
        copy.wait()


def plane_kernel(in_ref, slope_ref, table_ref, turned_ref, mixed_ref, mixed_turned_ref, out_ref, wide_ref, send_sem,
                 recv_sem):
    place = here()
    devices = [toward(place, side) for side in SIDES]
    signal(devices)

    def keep(t, _):
        x, y, z = lax.div(t, 8), lax.rem(lax.div(t, 4), 2), lax.rem(t, 4)
        wide_ref[x + 1, y + 1, z + 1] = slope_ref[x, y, z]
        return 0

    lax.fori_loop(0, 32, keep, 0)
    await_signals(26)
    halo = halo_copies(slope_ref, 0, wide_ref, place, send_sem, recv_sem)
    transform_planes(place[0] * 32 + place[1] * 4 + place[2], in_ref, table_ref, turned_ref, mixed_ref, mixed_turned_ref,
                     out_ref)
    for copy in halo:
        copy.wait()


def transform_planes(me, in_ref, table_ref, turned_ref, mixed_ref, mixed_turned_ref, out_ref):
    lane = lax.broadcasted_iota(jnp.int32, (16, 8, 128), 2)

    def pick(ref, half, g):
        return jnp.concatenate([ref[gx, half * 4 + g] for gx in range(4)], axis=0)

    rows = []
    for xr in range(4):
        pair = []
        for half in range(2):
            value = jnp.zeros((16, 8, 128), F32)
            for g in range(4):
                block = pick(in_ref, half, g)
                if g != xr:
                    block = pltpu.roll(block.reshape(128, 128), (g - xr) * 32 % 128, 1).reshape(16, 8, 128)
                value = jnp.where(lax.div(lane, 32) == g, block, value)
            pair.append(value.reshape(128, 128))
        rows.append(jnp.concatenate(pair, axis=1))
    plane = jnp.concatenate(rows, axis=0)
    turned = (turned_ref[0], turned_ref[1])
    along_y = split(dot3(split(plane), turned))

    row = lax.broadcasted_iota(jnp.int32, (256, 256), 0)
    col = lax.broadcasted_iota(jnp.int32, (256, 256), 1)
    scale = 2.0 * math.pi / 256
    wave_x = jnp.where(row <= 128, row, row - 128).astype(F32) * scale
    wave_y = jnp.where(col <= 128, col, col - 128).astype(F32) * scale
    flat = wave_x * wave_x + wave_y * wave_y
    side = lax.div(lax.rem(lax.broadcasted_iota(jnp.int32, (256, 512), 1), 8), 4)
    side_turned = lax.div(lax.rem(lax.broadcasted_iota(jnp.int32, (512, 256), 0), 8), 4)
    total = None
    for p in range(2):
        mode = me if p == 0 else jnp.where(me == 0, 128, me)
        wave_z = jnp.full((256, 256), mode, jnp.int32).astype(F32) * scale
        squared = flat + wave_z * wave_z
        anchor = squared == 0.0
        green = jnp.where(anchor, 0.0, 4.0 * math.pi * jnp.exp(-squared / (4.0 * EWALD_SPLIT * EWALD_SPLIT))
                          / jnp.where(anchor, 1.0, squared))
        left = [jnp.where(side == p, mixed_ref[i].astype(F32), 0.0).astype(BF16) for i in range(2)]
        modes = split3(dot3(left, along_y) * green)
        back = [jnp.where(side_turned == p, mixed_turned_ref[i].astype(F32), 0.0).astype(BF16) for i in range(3)]
        part = dot6(back, modes)
        total = part if total is None else total + part
    field = dot6(split3(total), [table_ref[i] for i in range(3)])
    for half in range(2):
        block = [field[xr * 128:(xr + 1) * 128, half * 128:(half + 1) * 128] for xr in range(4)]
        for g in range(4):
            value = jnp.zeros((16, 8, 128), F32)
            for xr in range(4):
                moved = block[xr]
                if g != xr:
                    moved = pltpu.roll(moved, (xr - g) * 32 % 128, 1)
                value = jnp.where(lax.div(lane, 32) == xr, moved.reshape(16, 8, 128), value)
            for gx in range(4):
                out_ref[gx, half * 4 + g] = value[gx * 4:(gx + 1) * 4]


def sample_kernel(charge_ref, in_ref, atoms_ref, table_ref, back_ref, field, out, send_sem, recv_sem):
    place = here()
    signal(column_devices(place))
    charges = [charge_ref[k] for k in range(2)]
    columns = [
        jnp.concatenate([in_ref[pl.ds(plane * 4 + xq, 128, stride=8), :] for xq in range(4)], axis=1)
        for plane in range(2)
    ]
    modes = jnp.concatenate(columns, axis=0)
    lines = jnp.concatenate([modes[:, i * 128:(i + 1) * 128].T for i in range(4)], axis=0)
    pieces_of_field = split3(dot6(split3(lines), [table_ref[i] for i in range(3)]))
    for group in range(2):
        for i, piece in enumerate(pieces_of_field):
            field[group, :, i * 128:(i + 1) * 128] = piece[:, group * 128:(group + 1) * 128]
    await_signals(3)
    point = lax.broadcasted_iota(jnp.int32, (128, 128), 0).astype(F32)

    def cell(n):
        owner = lax.rem(place[2] + 1 + lax.div(n, 8), 4)
        own_cell = lax.rem(n, 8)
        cyl, cz = lax.div(own_cell, 4), owner * 4 + lax.rem(own_cell, 4)

        def row(f):
            return atoms_ref[owner, own_cell, f:f + 1, :]

        ox, oy, oz, fx, fy, fz = [row(f) for f in range(6)]
        charge = by_species(row(6), charges)
        lower_z = oz + (lax.rem(cz, 8) * 16).astype(F32)
        lower = jnp.where(point == lower_z, 1.0, 0.0)
        slope = jnp.where(point == lower_z + 1.0, 1.0, 0.0) - lower
        right = jnp.concatenate([lower, slope], axis=1).astype(BF16)
        right = jnp.concatenate([right, right, right], axis=0)
        left = field_rows(field, lax.div(cz, 8), cyl)
        both = dot(left, right)
        tilt = both[:, 128:256].reshape(16, 16, 128)
        plain = both[:, 0:128].reshape(16, 16, 128) + fz * tilt
        spot = lax.broadcasted_iota(jnp.int32, (16, 128), 0).astype(F32)
        low_y, high_y = spot == oy, spot == oy + 1.0
        wy = jnp.where(low_y, 1.0 - fy, 0.0) + jnp.where(high_y, fy, 0.0)
        sy = jnp.where(high_y, 1.0, 0.0) - jnp.where(low_y, 1.0, 0.0)

        def fold(value):
            return value[:, 0:8] + value[:, 8:16]

        plain_w, plain_s, tilt_w = fold(plain * wy), fold(plain * sy), fold(tilt * wy)
        x_sum = jnp.zeros((8, 128), F32)
        y_sum, z_sum = x_sum, x_sum
        for x in range(16):
            low_x, high_x = ox == x, ox == x - 1
            wx = jnp.where(low_x, 1.0 - fx, 0.0) + jnp.where(high_x, fx, 0.0)
            sx = jnp.where(high_x, 1.0, 0.0) - jnp.where(low_x, 1.0, 0.0)
            x_sum = x_sum + sx * plain_w[x]
            y_sum = y_sum + wx * plain_s[x]
            z_sum = z_sum + wx * tilt_w[x]
        for f, value in enumerate((x_sum, y_sum, z_sum)):
            out[owner, own_cell, f:f + 1, :] = -charge * jnp.sum(value, axis=0, keepdims=True)
        out[owner, own_cell, 3:4, :] = charge

    def group(g, _):
        def later(n, _):
            cell(n)
            return 0

        lax.fori_loop(g * 8 + 1, g * 8 + 8, later, 0)
        return 0

    copies = []
    for g in range(4):
        cell(g * 8)
        if g:
            copies.append(column_copy(out, back_ref, place, send_sem, recv_sem, g - 1))
        group(g, 0)

    def mine(n, _):
        back_ref[place[2], n] = out[place[2], n]
        return 0

    lax.fori_loop(0, 8, mine, 0)
    for copy in copies:
        copy.wait()


def field_rows(field, group, cyl):
    start = pl.multiple_of(cyl * 16, 16)
    return jnp.concatenate([field[group, pl.ds(start + 32 * x, 16), :] for x in range(16)], axis=0)


TABLE, MIXED = tables()


def constants():
    return (parts_of(TABLE), parts_of(TABLE.T)[:2], parts_of(MIXED)[:2], parts_of(MIXED.T))


def gather_pass(charge, counts, offset, fraction, species, table):
    return pl.pallas_call(
        gather_kernel,
        out_shape=[
            jax.ShapeDtypeStruct((6, 4, 6, 4, 128), F32),
            jax.ShapeDtypeStruct((4, 8, 8, 128), F32),
            jax.ShapeDtypeStruct((1024, 128), F32),
        ],
        in_specs=[SMEM_SPEC] * 2 + [VMEM_SPEC] * 4,
        out_specs=[VMEM_SPEC] * 3,
        scratch_shapes=[pltpu.VMEM((4, 8, 8, 128), F32), pltpu.VMEM((256, 512), F32), DMA((26,)), DMA((26,)), DMA((3,)),
                        DMA((3,))],
        compiler_params=comm_params(0),
        name="gather_pass",
    )(charge, counts, offset, fraction, species, table)


def plane_pass(planes, slope, table, turned, mixed, mixed_turned):
    return pl.pallas_call(
        plane_kernel,
        out_shape=[jax.ShapeDtypeStruct((4, 8, 4, 8, 128), F32), jax.ShapeDtypeStruct((6, 4, 6, 1, 128), F32)],
        in_specs=[VMEM_SPEC] * 6,
        out_specs=[VMEM_SPEC] * 2,
        scratch_shapes=[DMA((26,)), DMA((26,))],
        compiler_params=comm_params(1),
        name="plane_pass",
    )(planes, slope, table, turned, mixed, mixed_turned)


def sample_pass(charge, lines, atoms, table):
    return pl.pallas_call(
        sample_kernel,
        out_shape=jax.ShapeDtypeStruct((4, 8, 4, 128), F32),
        in_specs=[SMEM_SPEC] + [VMEM_SPEC] * 3,
        out_specs=VMEM_SPEC,
        scratch_shapes=[pltpu.VMEM((2, 512, 384), BF16), pltpu.VMEM((4, 8, 4, 128), F32), DMA((3,)), DMA((3,))],
        compiler_params=comm_params(2),
        name="sample_pass",
    )(charge, lines, atoms, table)


def on_device(cell_counts, grid_offset, fraction, species, species_density, species_pair, species_embed, species_charge):
    counts = cell_counts.reshape(32)
    table, turned, mixed, mixed_turned = constants()
    extended, columns, lines = gather_pass(
        species_charge, counts, grid_offset.reshape(32, 3, 128), fraction.reshape(32, 3, 128), species.reshape(8, 4, 128),
        table)
    extended = extended.reshape(144, 4, 128)
    planes = lax.all_to_all(lines.reshape(128, 8, 128), AXES, split_axis=0, concat_axis=0, tiled=True)
    density, slope = density_pass(species_density, species_pair, species_embed, extended)
    planes, wide_slope = plane_pass(
        planes.reshape(4, 8, 4, 8, 128), slope.reshape(4, 2, 4, 1, 128), table, turned, mixed, mixed_turned)
    lines = lax.all_to_all(planes.reshape(128, 8, 128), AXES, split_axis=0, concat_axis=0, tiled=True)
    eam = force_pass(counts, species_density, species_pair, extended, wide_slope.reshape(144, 1, 128))
    electric = sample_pass(species_charge, lines.reshape(1024, 128), columns, table)
    electric = electric.reshape(4, 2, 4, 4, 128)[:, :, :, 0:3]
    eam = eam.reshape(3, 4, 2, 4, 128).transpose(1, 2, 3, 0, 4)
    return eam + COUPLING * electric, density.reshape(4, 2, 4, 128)


def solution(mesh):
    return jax.shard_map(
        on_device,
        mesh=mesh,
        in_specs=(
            P("gx", "gy", "gz"),
            P("gx", "gy", "gz", None, None),
            P("gx", "gy", "gz", None, None),
            P("gx", "gy", "gz", None),
            P(),
            P(),
            P(),
            P(),
        ),
        out_specs=(P("gx", "gy", "gz", None, None), P("gx", "gy", "gz", None)),
        check_vma=False,
    )
```

time: 171 us -> 125 us (0.73)
  Pallas kernels: 141 us -> 108 us
  other arithmetic: 10.8 us -> 0.64 us
  starting transfers between devices: 12.2 us -> 9.85 us
    pallas_call x1, Pallas kernels: 63.4 us -> 41.9 us  [force_pass(): pl.pallas_call(force_kernel, out_shape=jax.ShapeDtypeStruct((3, 32, 128),...]
    pallas_call x7 -> x4, Pallas kernels: 77.1 us -> 65.9 us  [the longest x1 22.5 us: gather_pass(): pl.pallas_call(gather_kernel, out_shape=[jax.ShapeDtypeStruct((6, 4, 6, 4...]
    mul x2 -> x0, other arithmetic: 8.24 us -> none  [the longest x1 7.59 us: on_device(): charge = species_value(species, species_charge) * alive]
    slice x6 -> x0, local copies, waits for them, and re-layouts: 3.96 us -> none  [the longest x5 3.95 us: species_value(): lookup_table[kind_index]]
    unnamed x24, local copies, waits for them, and re-layouts: 1.38 us -> 3.2 us
  transfers between devices with their start and end apart: 2 -> 2, of which waited for: 0 -> 0; matrix products, arithmetic and copies ran while one was open for 0% -> 0% of each run, Pallas kernels for 57% -> 46%
where the time goes in v2:
time: 125 us; the launch traced here: 123 us
  Pallas kernels  108 us (86%)
  starting transfers between devices  9.85 us (8%)
  local copies, waits for them, and re-layouts  3.98 us (3%)
    pallas_call x1, Pallas kernels, force_pass(): pl.pallas_call(force_kernel, out_shape=jax.ShapeDtypeStruct((3, 32, 128),...  41.9 us
    pallas_call x1, Pallas kernels, gather_pass(): pl.pallas_call(gather_kernel, out_shape=[jax.ShapeDtypeStruct((6, 4, 6, 4...  22.5 us
    pallas_call x1, Pallas kernels, density_pass(): pl.pallas_call(density_kernel, out_shape=[jax.ShapeDtypeStruct((8, 4, 128...  15.3 us
    pallas_call x1, Pallas kernels, sample_pass(): pl.pallas_call(sample_kernel, out_shape=jax.ShapeDtypeStruct((4, 8, 4, 12...  14.3 us
    pallas_call x1, Pallas kernels, plane_pass(): pl.pallas_call(plane_kernel, out_shape=[jax.ShapeDtypeStruct((4, 8, 4, 8,...  13.8 us
    all_to_all x1, starting transfers between devices, on_device(): lax.all_to_all(planes.reshape(128, 8, 128), AXES, split_axis=0, concat_ax...  5.46 us
    all_to_all x1, starting transfers between devices, on_device(): lax.all_to_all(lines.reshape(128, 8, 128), AXES, split_axis=0, concat_axi...  4.39 us
    unnamed x24, local copies, waits for them, and re-layouts  3.2 us
  transfers between devices with their start and end apart: 2, of which 0 were waited for; matrix products, arithmetic and copies ran while one was open for 0% of the time, Pallas kernels for 46%

profile of v2, /device:TPU:1, one launch (start us, length us, event | category | flops | bytes accessed | tf_op | source)
XLA Modules:
  0.0 123.1 jit_solution(3372698963340652624)
XLA Ops:
  0.6 0.8 reshape.46.count_ref
  1.4 0.0 copy-start.10
  1.4 0.8 copy.14
  2.2 0.0 copy-done.10
  2.2 0.0 copy-start.5
  2.3 0.0 copy-start.6
  2.3 0.7 copy-done.5
  3.0 0.0 copy-done.6
  3.0 0.0 copy-start
  3.0 1.0 copy-done
  4.0 22.5 %gather_pass.1 = (f32[6,4,6,4,128]{4,3,2,1,0:T(4,128)S(1)}, f32[4,8,8,128]{3,2,1,0:T(8,128)S(1)}, f32[1024,128]{1,0:T(8,128)}) custom-call(f32[2]{0:T(128)S(1)} %copy-done.6, s32[32]{0:T(128)S(1)} %reshape.46.count_ref, s32[32,3,128]{2,1,0:T(4,128)S(1)} %bitcast.18, f32[32,3,128]{2,1,0:T(4,128)S(1)} %bitcast.19, s32[8,4,128]{2,1,0:T(4,128)S(1)} %bitcast.23, ...), custom_call_target="tpu_custom_call" | custom-call | tf_op jit(solution)/shard_map/gather_pass/pallas_call | solution.py:677
  26.5 4.4 %all-to-all-start = ((f32[128,8,128]{2,1,0:T(8,128)}), f32[128,8,128]{2,1,0:T(8,128)S(1)}, u32[]{:S(2)}, u32[]{:S(2)}) async-start(f32[128,8,128]{2,1,0:T(8,128)} %bitcast.4), calls=%async_computation | async-start | bytes 1048576 | tf_op jit(solution)/shard_map/all_to_all | solution.py:724
  30.9 0.0 copy-start.7
  30.9 0.0 copy-start.8
  30.9 0.0 copy-start.9
  30.9 0.6 copy-done.7
  31.5 0.0 copy-done.8
  31.5 0.0 copy-done.9
  31.6 0.0 copy-start.1
  31.6 0.0 copy-start.2
  31.6 0.0 copy-start.3
  31.6 0.0 copy-start.4
  31.6 15.3 %density_pass.1 = (f32[8,4,128]{2,1,0:T(4,128)}, f32[32,1,128]{2,1,0:T(1,128)S(1)}) custom-call(f32[2]{0:T(128)S(1)} %copy-done.8, f32[2]{0:T(128)S(1)} %copy-done.9, f32[2]{0:T(128)S(1)} %copy-done.7, f32[144,4,128]{2,1,0:T(4,128)S(1)} %bitcast.24), custom_call_target="tpu_custom_call" | custom-call | flops 10000000000 | bytes 1000000 | tf_op jit(solution)/shard_map/density_pass/pallas_call | solution.py:348
  46.9 0.0 all-to-all-done
  46.9 0.0 copy-done.1
  46.9 0.0 copy-done.2
  46.9 0.0 copy-done.3
  46.9 0.0 copy-done.4
  46.9 13.8 %plane_pass.1 = (f32[4,8,4,8,128]{4,3,2,1,0:T(8,128)}, f32[6,4,6,1,128]{4,3,2,1,0:T(1,128)S(1)}) custom-call(f32[4,8,4,8,128]{4,3,2,1,0:T(8,128)S(1)} %bitcast.16, f32[4,2,4,1,128]{4,3,2,1,0:T(1,128)S(1)} %bitcast.22, bf16[3,256,256]{2,1,0:T(8,128)(2,1)S(1)} %copy-done.1, bf16[2,256,256]{2,1,0:T(8,128)(2,1)S(1)} %copy-done.4, ...), custom_call_target="tpu_custom_call" | custom-call | tf_op jit(solution)/shard_map/plane_pass/pallas_call | solution.py:694
  60.7 5.5 %all-to-all-start.1 = ((f32[128,8,128]{2,1,0:T(8,128)}), f32[128,8,128]{2,1,0:T(8,128)S(1)}, u32[]{:S(2)}, u32[]{:S(2)}) async-start(f32[128,8,128]{2,1,0:T(8,128)} %bitcast.10), calls=%async_computation.1 | async-start | bytes 1048576 | tf_op jit(solution)/shard_map/all_to_all | solution.py:728
  66.2 41.9 %force_pass.1 = f32[3,32,128]{2,1,0:T(8,128)S(1)} custom-call(s32[32]{0:T(128)S(1)} %reshape.46.count_ref, f32[2]{0:T(128)S(1)} %copy-done.8, f32[2]{0:T(128)S(1)} %copy-done.9, f32[144,4,128]{2,1,0:T(4,128)S(1)} %bitcast.25, f32[144,1,128]{2,1,0:T(1,128)S(1)} %bitcast.26), custom_call_target="tpu_custom_call" | custom-call | flops 20000000000 | bytes 1000000 | tf_op jit(solution)/shard_map/force_pass/pallas_call | solution.py:361
  108.1 0.0 all-to-all-done.1
  108.1 14.3 %sample_pass.1 = f32[4,8,4,128]{3,2,1,0:T(4,128)S(1)} custom-call(f32[2]{0:T(128)S(1)} %copy-done.6, f32[1024,128]{1,0:T(8,128)S(1)} %bitcast.17, f32[4,8,8,128]{3,2,1,0:T(8,128)S(1)} %get-tuple-element.14.atoms_ref, bf16[3,256,256]{2,1,0:T(8,128)(2,1)S(1)} %copy-done.1), custom_call_target="tpu_custom_call" | custom-call | tf_op jit(solution)/shard_map/sample_pass/pallas_call | solution.py:706
  122.4 0.6 fusion
  (1 shorter events, 0.0 us)
Async XLA Ops:
  1.4 0.8 copy-start.10
  2.2 0.7 copy-start.5
  2.3 0.7 copy-start.6
  3.0 1.0 copy-start
  26.5 20.4 %all-to-all-start = ((f32[128,8,128]{2,1,0:T(8,128)}), f32[128,8,128]{2,1,0:T(8,128)S(1)}, u32[]{:S(2)}, u32[]{:S(2)}) async-start(f32[128,8,128]{2,1,0:T(8,128)} %bitcast.4), calls=%async_computation | async-start | bytes 1048576 | tf_op jit(solution)/shard_map/all_to_all | solution.py:724
  30.9 0.7 copy-start.7
  30.9 0.7 copy-start.8
  30.9 0.7 copy-start.9
  31.6 15.3 %copy-start.1 = (bf16[3,256,256]{2,1,0:T(8,128)(2,1)S(1)}, bf16[3,256,256]{2,1,0:T(8,128)(2,1)}, u32[]{:S(2)}) copy-start(bf16[3,256,256]{2,1,0:T(8,128)(2,1)} %constant.10.clone.table_ref) | copy-start | bytes 1179652
  31.6 15.3 %copy-start.2 = (bf16[3,512,256]{2,1,0:T(8,128)(2,1)S(1)}, bf16[3,512,256]{2,1,0:T(8,128)(2,1)}, u32[]{:S(2)}) copy-start(bf16[3,512,256]{2,1,0:T(8,128)(2,1)} %constant.13.clone.mixed_turned_ref) | copy-start | bytes 2359300
  31.6 15.3 %copy-start.3 = (bf16[2,256,512]{2,1,0:T(8,128)(2,1)S(1)}, bf16[2,256,512]{2,1,0:T(8,128)(2,1)}, u32[]{:S(2)}) copy-start(bf16[2,256,512]{2,1,0:T(8,128)(2,1)} %constant.12.clone.mixed_ref) | copy-start | bytes 1572868
  31.6 15.3 %copy-start.4 = (bf16[2,256,256]{2,1,0:T(8,128)(2,1)S(1)}, bf16[2,256,256]{2,1,0:T(8,128)(2,1)}, u32[]{:S(2)}) copy-start(bf16[2,256,256]{2,1,0:T(8,128)(2,1)} %constant.11.clone.turned_ref) | copy-start | bytes 786436
  60.7 47.4 %all-to-all-start.1 = ((f32[128,8,128]{2,1,0:T(8,128)}), f32[128,8,128]{2,1,0:T(8,128)S(1)}, u32[]{:S(2)}, u32[]{:S(2)}) async-start(f32[128,8,128]{2,1,0:T(8,128)} %bitcast.10), calls=%async_computation.1 | async-start | bytes 1048576 | tf_op jit(solution)/shard_map/all_to_all | solution.py:728

commit v3 on v2

--- a/solution.py
+++ b/solution.py
@@ -197,16 +197,27 @@
     lax.fori_loop(0, 32, cell, 0, unroll=4)
 
 
+def split3(value):
+    first = value.astype(BF16)
+    rest = value - first.astype(F32)
+    second = rest.astype(BF16)
+    return first, second, (rest - second.astype(F32)).astype(BF16)
+
+
+def lane_sums(rows):
+    ones = jnp.ones((8, rows.shape[1]), BF16)
+    return lax.dot_general(ones, rows, (((1,), (1,)), ((), ())), preferred_element_type=F32)
+
+
 def right_side(feat_b, cell):
     r = pl.multiple_of(cell * KF, KF)
     return jnp.concatenate([feat_b[pl.ds(r + KF * dz, KF), :] for dz in range(3)], axis=1)
 
 
-def density_kernel(amplitude_ref, pair_ref, embed_ref, ext_ref, density_ref, slope_ref, feat_b, own_t, keep, mat):
+def density_kernel(amplitude_ref, pair_ref, embed_ref, ext_ref, density_ref, slope_ref, feat_b, own_t, keep, totals, mat):
     amplitudes, pairs, embeds = [[filled(ref, k) for k in range(2)] for ref in (amplitude_ref, pair_ref, embed_ref)]
     source_features(ext_ref, None, None, feat_b, [cube_root(value) for value in amplitudes], None)
     target_features(ext_ref, own_t, keep, None, None, None)
-    mat[...] = jnp.zeros((128, 128), F32)
     lanes = lax.broadcasted_iota(jnp.int32, (128, 128), 1)
     other = lanes != lax.broadcasted_iota(jnp.int32, (128, 128), 0)
 
@@ -224,25 +235,34 @@
                     if dx == 1 and dy == 1 and dz == 1:
                         part = jnp.where(other, part, 0.0)
                     total = total + part * part * part
-        sums = jnp.sum(total, axis=1, keepdims=True)
-        return sums
+        return total
+
+    def settle(n):
+        first, second, _ = split3(totals[...])
+        sums = lane_sums(jnp.concatenate([first, second], axis=1))
+        mat[pl.ds(2 * n, 1), :] = sums[0:1, 0:128]
+        mat[pl.ds(2 * n + 1, 1), :] = sums[0:1, 128:256]
+
+    totals[...] = jnp.zeros((256, 128), F32)
 
     def both(n, _):
-        first, second = target(2 * n), target(2 * n + 1)
-        mat[...] = jnp.where(lanes == 2 * n, first, jnp.where(lanes == 2 * n + 1, second, mat[...]))
+        settle(jnp.maximum(n - 1, 0))
+        totals[0:128, :] = target(2 * n)
+        totals[128:256, :] = target(2 * n + 1)
         return 0
 
     lax.fori_loop(0, 16, both, 0)
+    settle(15)
     code = keep[3]
     alive = by_species(code, (1.0, 1.0))
-    density = mat[...].T[0:32] * alive
+    density = mat[0:32, :] * alive
     density_ref[...] = density.reshape(8, 4, 128)
     tilts = [jnp.concatenate([3.0 * embed / (pair * pair)] * 4, axis=0) for embed, pair in zip(embeds, pairs)]
     slope_ref[...] = (by_species(code, tilts) / jnp.sqrt(1.0 + density)).reshape(32, 1, 128)
 
 
 def force_kernel(count_ref, amplitude_ref, pair_ref, ext_ref, slope_ref, out_ref, feat_b, own_t, keep, wide, near_a, near_b,
-                 mat, table):
+                 part_a, part_b, mat, table):
     amplitudes, pairs = [[filled(ref, k) for k in range(2)] for ref in (amplitude_ref, pair_ref)]
     ratios = [amplitude / (pair * pair) for amplitude, pair in zip(amplitudes, pairs)]
     gains = [-4.0 * pair / amplitude for amplitude, pair in zip(amplitudes, pairs)]
@@ -257,7 +277,8 @@
         return 0
 
     lax.fori_loop(0, 32, fill, 0)
-    mat[...] = jnp.zeros((128, 128), F32)
+    part_a[...] = jnp.zeros((4, 128, 128), F32)
+    part_b[...] = jnp.zeros((4, 128, 128), F32)
     lane = lax.broadcasted_iota(jnp.int32, (ROWS, 128), 1)
     lane3 = lax.broadcasted_iota(jnp.int32, (ROWS // 8, 8, 128), 2)
     row3 = lax.broadcasted_iota(jnp.int32, (ROWS // 8, 8, 128), 0) * 8 + lax.broadcasted_iota(
@@ -277,7 +298,7 @@
             near[part * 8 + k] = product[:, 0:128]
             near[part * 8 + k + 1] = product[:, 128:256]
 
-    def chunk(t, near, c):
+    def chunk(t, near, part, c):
         rows = pl.ds(pl.multiple_of(c * ROWS, ROWS), ROWS)
         base = corner(t)
 
@@ -297,39 +318,44 @@
             mx = mx + value * wide[r, 0]
             my = my + value * wide[r, 1]
             mz = mz + value * wide[r, 2]
-        old = mat[rows, :]
         for m, value in enumerate((m0, mx, my, mz)):
-            total = jnp.sum(value.reshape(ROWS, 128), axis=1, keepdims=True)
-            old = jnp.where(lane == t * 4 + m, total, old)
-        mat[rows, :] = old
+            part[m, rows, :] = value.reshape(ROWS, 128)
+
+    def settle(t, part):
+        for m in (0, 2):
+            first, second, third = split3(jnp.concatenate([part[m], part[m + 1]], axis=0))
+            sums = lane_sums(jnp.concatenate([first, second], axis=1)) + lane_sums(third)
+            mat[pl.ds(t * 4 + m, 1), :] = sums[0:1, 0:128]
+            mat[pl.ds(t * 4 + m + 1, 1), :] = sums[0:1, 128:256]
 
     for part in range(4):
         multiply(0, near_a, part)
 
-    def target(t, near, following):
+    def target(t, near, following, part, before):
         later = jnp.minimum(t + 1, 31)
 
         def rest(c, _):
-            chunk(t, near, c)
+            chunk(t, near, part, c)
             return 0
 
-        for part in range(4):
-            multiply(later, following, part)
-            chunk(t, near, part)
-        lax.fori_loop(4, lax.div(count_ref[t] + ROWS - 1, ROWS), rest, 0)
+        settle(jnp.maximum(t - 1, 0), before)
+        for n in range(4):
+            multiply(later, following, n)
+            chunk(t, near, part, n)
+        lax.fori_loop(4, lax.div(count_ref[lax.div(t, 8), lax.rem(lax.div(t, 4), 2), lax.rem(t, 4)] + ROWS - 1, ROWS), rest, 0)
 
     def pair(n, _):
-        target(2 * n, near_a, near_b)
-        target(2 * n + 1, near_b, near_a)
+        target(2 * n, near_a, near_b, part_a, part_b)
+        target(2 * n + 1, near_b, near_a, part_b, part_a)
         return 0
 
     lax.fori_loop(0, 16, pair, 0)
-    mat[...] = mat[...].T
-
+    settle(31, part_b)
     whole = mat[pl.ds(0, 32, stride=4), :]
     amplitude = by_species(keep[3], [jnp.concatenate([value] * 4, axis=0) for value in amplitudes])
     for m in range(3):
-        out_ref[m] = amplitude * (mat[pl.ds(m + 1, 32, stride=4), :] - keep[m] * whole)
+        value = amplitude * (mat[pl.ds(m + 1, 32, stride=4), :] - keep[m] * whole)
+        out_ref[:, m] = value.reshape(8, 4, 128)
 
 
 def sel_matrix():
@@ -350,7 +376,7 @@
         out_shape=[jax.ShapeDtypeStruct((8, 4, 128), F32), jax.ShapeDtypeStruct((32, 1, 128), F32)],
         in_specs=[SMEM_SPEC] * 3 + [VMEM_SPEC],
         out_specs=[VMEM_SPEC] * 2,
-        scratch_shapes=features_scratch() + [pltpu.VMEM((128, 128), F32)],
+        scratch_shapes=features_scratch() + [pltpu.VMEM((256, 128), F32), pltpu.VMEM((128, 128), F32)],
         compiler_params=pltpu.CompilerParams(vmem_limit_bytes=16 << 20),
         cost_estimate=pl.CostEstimate(flops=10_000_000_000, bytes_accessed=1_000_000, transcendentals=0),
         name="density_pass",
@@ -360,13 +386,15 @@
 def force_pass(counts, amplitude, pair, ext, slope):
     return pl.pallas_call(
         force_kernel,
-        out_shape=jax.ShapeDtypeStruct((3, 32, 128), F32),
+        out_shape=jax.ShapeDtypeStruct((8, 3, 4, 128), F32),
         in_specs=[SMEM_SPEC] * 3 + [VMEM_SPEC] * 2,
         out_specs=VMEM_SPEC,
         scratch_shapes=features_scratch() + [
             pltpu.VMEM((144, 5, 8, 128), F32),
             pltpu.VMEM((32, 128, 128), F32),
             pltpu.VMEM((32, 128, 128), F32),
+            pltpu.VMEM((4, 128, 128), F32),
+            pltpu.VMEM((4, 128, 128), F32),
             pltpu.VMEM((128, 128), F32),
             pltpu.SMEM((64,), jnp.int32),
         ],
@@ -414,13 +442,6 @@
     return dot(a[0], b[0]) + (dot(a[1], b[0]) + dot(a[0], b[1]))
 
 
-def split3(value):
-    first = value.astype(BF16)
-    rest = value - first.astype(F32)
-    second = rest.astype(BF16)
-    return first, second, (rest - second.astype(F32)).astype(BF16)
-
-
 def dot6(a, b):
     small = dot(a[1], b[1]) + (dot(a[2], b[0]) + dot(a[0], b[2]))
     return dot(a[0], b[0]) + (dot(a[1], b[0]) + dot(a[0], b[1]) + small)
@@ -458,7 +479,7 @@
         rho[pl.ds(pl.multiple_of(cz * 16, 16), 16), :] = value
         return 0
 
-    lax.fori_loop(0, 16, layer, 0)
+    lax.fori_loop(0, 16, layer, 0, unroll=2)
     lines = dot3((table_ref[0], table_ref[1]), split(rho[...]))
     for plane in range(2):
         for xq in range(4):
@@ -472,20 +493,21 @@
     signal([toward(place, side) for side in SIDES] + [column_devices(place)[1]])
     slot = lax.broadcasted_iota(jnp.int32, (1, 128), 1)
 
-    def pack(t, _):
-        x, y, z = lax.div(t, 8), lax.rem(lax.div(t, 4), 2), lax.rem(t, 4)
-        offset, fraction = offset_ref[t].astype(F32), fraction_ref[t]
-        kind = species_ref[lax.div(t, 4), pl.ds(z, 1), :].astype(F32)
-        code = jnp.where(slot < count_ref[t], kind, -1.0)
-        ext_ref[x + 1, y + 1, z + 1, 0:3, :] = (offset + 0.5 + fraction) * (1.0 / PPC)
-        ext_ref[x + 1, y + 1, z + 1, 3:4, :] = code
-        atoms[x, y * 4 + z, 0:3, :] = offset
-        atoms[x, y * 4 + z, 3:6, :] = fraction
-        atoms[x, y * 4 + z, 6:7, :] = code
-        atoms[x, y * 4 + z, 7:8, :] = code
-        return 0
-
-    lax.fori_loop(0, 32, pack, 0)
+    def pack(n, _):
+        x, y = lax.div(n, 2), lax.rem(n, 2)
+        for z in range(4):
+            code = jnp.where(slot < count_ref[x, y, z], species_ref[x, y, z:z + 1, :].astype(F32), -1.0)
+            for d in range(3):
+                offset, fraction = offset_ref[x, y, d, z:z + 1, :].astype(F32), fraction_ref[x, y, d, z:z + 1, :]
+                ext_ref[x + 1, y + 1, z + 1, d:d + 1, :] = (offset + 0.5 + fraction) * (1.0 / PPC)
+                atoms[x, y * 4 + z, d:d + 1, :] = offset
+                atoms[x, y * 4 + z, d + 3:d + 4, :] = fraction
+            ext_ref[x + 1, y + 1, z + 1, 3:4, :] = code
+            atoms[x, y * 4 + z, 6:7, :] = code
+            atoms[x, y * 4 + z, 7:8, :] = code
+        return 0
+
+    lax.fori_loop(0, 8, pack, 0)
 
     def keep(n, _):
         got_ref[place[2], n] = atoms[place[2], n]
@@ -634,29 +656,25 @@
             y_sum = y_sum + wx * plain_s[x]
             z_sum = z_sum + wx * tilt_w[x]
         for f, value in enumerate((x_sum, y_sum, z_sum)):
-            out[owner, own_cell, f:f + 1, :] = -charge * jnp.sum(value, axis=0, keepdims=True)
-        out[owner, own_cell, 3:4, :] = charge
+            out[owner, cyl, f, pl.ds(lax.rem(own_cell, 4), 1), :] = -charge * jnp.sum(value, axis=0, keepdims=True)
 
     def group(g, _):
         def later(n, _):
             cell(n)
             return 0
 
-        lax.fori_loop(g * 8 + 1, g * 8 + 8, later, 0)
+        lax.fori_loop(g * 8 + 2, g * 8 + 8, later, 0, unroll=2)
         return 0
 
     copies = []
     for g in range(4):
         cell(g * 8)
+        cell(g * 8 + 1)
         if g:
             copies.append(column_copy(out, back_ref, place, send_sem, recv_sem, g - 1))
         group(g, 0)
 
-    def mine(n, _):
-        back_ref[place[2], n] = out[place[2], n]
-        return 0
-
-    lax.fori_loop(0, 8, mine, 0)
+    back_ref[place[2]] = out[place[2]]
     for copy in copies:
         copy.wait()
 
@@ -705,32 +723,30 @@
 def sample_pass(charge, lines, atoms, table):
     return pl.pallas_call(
         sample_kernel,
-        out_shape=jax.ShapeDtypeStruct((4, 8, 4, 128), F32),
+        out_shape=jax.ShapeDtypeStruct((4, 2, 3, 4, 128), F32),
         in_specs=[SMEM_SPEC] + [VMEM_SPEC] * 3,
         out_specs=VMEM_SPEC,
-        scratch_shapes=[pltpu.VMEM((2, 512, 384), BF16), pltpu.VMEM((4, 8, 4, 128), F32), DMA((3,)), DMA((3,))],
+        scratch_shapes=[pltpu.VMEM((2, 512, 384), BF16), pltpu.VMEM((4, 2, 3, 4, 128), F32), DMA((3,)), DMA((3,))],
         compiler_params=comm_params(2),
         name="sample_pass",
     )(charge, lines, atoms, table)
 
 
 def on_device(cell_counts, grid_offset, fraction, species, species_density, species_pair, species_embed, species_charge):
-    counts = cell_counts.reshape(32)
     table, turned, mixed, mixed_turned = constants()
+    order = (0, 1, 3, 2, 4)
     extended, columns, lines = gather_pass(
-        species_charge, counts, grid_offset.reshape(32, 3, 128), fraction.reshape(32, 3, 128), species.reshape(8, 4, 128),
-        table)
+        species_charge, cell_counts, grid_offset.transpose(order), fraction.transpose(order), species, table)
     extended = extended.reshape(144, 4, 128)
     planes = lax.all_to_all(lines.reshape(128, 8, 128), AXES, split_axis=0, concat_axis=0, tiled=True)
     density, slope = density_pass(species_density, species_pair, species_embed, extended)
     planes, wide_slope = plane_pass(
         planes.reshape(4, 8, 4, 8, 128), slope.reshape(4, 2, 4, 1, 128), table, turned, mixed, mixed_turned)
     lines = lax.all_to_all(planes.reshape(128, 8, 128), AXES, split_axis=0, concat_axis=0, tiled=True)
-    eam = force_pass(counts, species_density, species_pair, extended, wide_slope.reshape(144, 1, 128))
+    eam = force_pass(cell_counts, species_density, species_pair, extended, wide_slope.reshape(144, 1, 128))
     electric = sample_pass(species_charge, lines.reshape(1024, 128), columns, table)
-    electric = electric.reshape(4, 2, 4, 4, 128)[:, :, :, 0:3]
-    eam = eam.reshape(3, 4, 2, 4, 128).transpose(1, 2, 3, 0, 4)
-    return eam + COUPLING * electric, density.reshape(4, 2, 4, 128)
+    forces = eam.reshape(4, 2, 3, 4, 128) + COUPLING * electric
+    return forces.transpose(order), density.reshape(4, 2, 4, 128)
 
 
 def solution(mesh):

time: 125 us -> 112 us (0.90); the launches traced: 123 us -> 111 us
  Pallas kernels: 108 us -> 94.7 us
  local copies, waits for them, and re-layouts: 3.98 us -> 5.33 us
    pallas_call x2, Pallas kernels: 56.2 us -> 45.1 us  [the longest x1 31.9 us: force_pass(): pl.pallas_call(force_kernel, out_shape=jax.ShapeDtypeStruct((8, 3, 4, 128...]
    unnamed x24 -> x28, local copies, waits for them, and re-layouts: 3.2 us -> 5.33 us
  transfers between devices with their start and end apart: 2 -> 2, of which waited for: 0 -> 0; matrix products, arithmetic and copies ran while one was open for 0% -> 0% of each run, Pallas kernels for 46% -> 42%
where the time goes in v3:
time: 112 us; the launch traced here: 111 us
  Pallas kernels  94.7 us (85%)
  starting transfers between devices  9.86 us (9%)
  local copies, waits for them, and re-layouts  5.33 us (5%)
    pallas_call x1, Pallas kernels, force_pass(): pl.pallas_call(force_kernel, out_shape=jax.ShapeDtypeStruct((8, 3, 4, 128...  31.9 us
    pallas_call x1, Pallas kernels, gather_pass(): pl.pallas_call(gather_kernel, out_shape=[jax.ShapeDtypeStruct((6, 4, 6, 4...  21.3 us
    pallas_call x1, Pallas kernels, density_pass(): pl.pallas_call(density_kernel, out_shape=[jax.ShapeDtypeStruct((8, 4, 128...  14.5 us
    pallas_call x1, Pallas kernels, plane_pass(): pl.pallas_call(plane_kernel, out_shape=[jax.ShapeDtypeStruct((4, 8, 4, 8,...  13.8 us
    pallas_call x1, Pallas kernels, sample_pass(): pl.pallas_call(sample_kernel, out_shape=jax.ShapeDtypeStruct((4, 2, 3, 4,...  13.3 us
    all_to_all x1, starting transfers between devices, on_device(): lax.all_to_all(planes.reshape(128, 8, 128), AXES, split_axis=0, concat_ax...  5.47 us
    unnamed x28, local copies, waits for them, and re-layouts  5.33 us
    all_to_all x1, starting transfers between devices, on_device(): lax.all_to_all(lines.reshape(128, 8, 128), AXES, split_axis=0, concat_axi...  4.39 us
  transfers between devices with their start and end apart: 2, of which 0 were waited for; matrix products, arithmetic and copies ran while one was open for 0% of the time, Pallas kernels for 42%

profile of v3, /device:TPU:1, one launch (start us, length us, event | category | flops | bytes accessed | tf_op | source)
XLA Modules:
  0.0 111.3 jit_solution(7960656689712915915)
XLA Ops:
  0.6 0.0 copy-start.10
  0.6 0.6 copy-done.10
  1.3 0.0 copy-start
  1.3 1.0 copy-done
  2.3 0.0 copy-start.5
  2.3 0.8 copy-done.5
  3.1 0.0 copy-start.6
  3.1 0.8 copy-done.6
  3.9 0.0 copy-start.7
  3.9 0.7 copy-done.7
  4.6 0.0 copy-start.8
  4.6 0.7 copy-done.8
  5.3 21.3 %gather_pass.1 = (f32[6,4,6,4,128]{4,3,2,1,0:T(4,128)S(1)}, f32[4,8,8,128]{3,2,1,0:T(8,128)S(1)}, f32[1024,128]{1,0:T(8,128)}) custom-call(f32[2]{0:T(128)S(1)} %copy-done.10, s32[4,2,4]{2,1,0:T(2,128)S(1)} %copy-done.8, s32[4,2,3,4,128]{4,3,2,1,0:T(4,128)S(1)} %bitcast.15, f32[4,2,3,4,128]{4,3,2,1,0:T(4,128)S(1)} %bitcast.16, ...), custom_call_target="tpu_custom_call" | custom-call | tf_op jit(solution)/shard_map/gather_pass/pallas_call | solution.py:695
  26.6 4.4 %all-to-all-start = ((f32[128,8,128]{2,1,0:T(8,128)}), f32[128,8,128]{2,1,0:T(8,128)S(1)}, u32[]{:S(2)}, u32[]{:S(2)}) async-start(f32[128,8,128]{2,1,0:T(8,128)} %bitcast.3), calls=%async_computation | async-start | bytes 1048576 | tf_op jit(solution)/shard_map/all_to_all | solution.py:741
  31.0 0.0 copy-start.11
  31.0 0.0 copy-start.12
  31.0 0.0 copy-start.13
  31.0 0.6 copy-done.11
  31.7 0.0 copy-done.12
  31.7 0.0 copy-done.13
  31.7 0.0 copy-start.1
  31.7 0.0 copy-start.2
  31.7 0.0 copy-start.3
  31.7 0.0 copy-start.4
  31.7 14.5 %density_pass.1 = (f32[8,4,128]{2,1,0:T(4,128)}, f32[32,1,128]{2,1,0:T(1,128)S(1)}) custom-call(f32[2]{0:T(128)S(1)} %copy-done.12, f32[2]{0:T(128)S(1)} %copy-done.13, f32[2]{0:T(128)S(1)} %copy-done.11, f32[144,4,128]{2,1,0:T(4,128)S(1)} %bitcast.19), custom_call_target="tpu_custom_call" | custom-call | flops 10000000000 | bytes 1000000 | tf_op jit(solution)/shard_map/density_pass/pallas_call | solution.py:374
  46.2 0.0 all-to-all-done
  46.2 0.0 copy-done.1
  46.2 0.0 copy-done.2
  46.2 0.0 copy-done.3
  46.2 0.0 copy-done.4
  46.2 13.8 %plane_pass.1 = (f32[4,8,4,8,128]{4,3,2,1,0:T(8,128)}, f32[6,4,6,1,128]{4,3,2,1,0:T(1,128)S(1)}) custom-call(f32[4,8,4,8,128]{4,3,2,1,0:T(8,128)S(1)} %bitcast.13, f32[4,2,4,1,128]{4,3,2,1,0:T(1,128)S(1)} %bitcast.18, bf16[3,256,256]{2,1,0:T(8,128)(2,1)S(1)} %copy-done.1, bf16[2,256,256]{2,1,0:T(8,128)(2,1)S(1)} %copy-done.4, ...), custom_call_target="tpu_custom_call" | custom-call | tf_op jit(solution)/shard_map/plane_pass/pallas_call | solution.py:712
  60.0 0.0 copy-start.9
  60.1 5.5 %all-to-all-start.1 = ((f32[128,8,128]{2,1,0:T(8,128)}), f32[128,8,128]{2,1,0:T(8,128)S(1)}, u32[]{:S(2)}, u32[]{:S(2)}) async-start(f32[128,8,128]{2,1,0:T(8,128)} %bitcast.8), calls=%async_computation.1 | async-start | bytes 1048576 | tf_op jit(solution)/shard_map/all_to_all | solution.py:745
  65.5 0.0 copy-done.9
  65.5 31.9 %force_pass.1 = f32[8,3,4,128]{3,2,1,0:T(4,128)S(1)} custom-call(s32[4,2,4]{2,1,0:T(2,128)S(1)} %copy-done.9, f32[2]{0:T(128)S(1)} %copy-done.12, f32[2]{0:T(128)S(1)} %copy-done.13, f32[144,4,128]{2,1,0:T(4,128)S(1)} %bitcast.20, f32[144,1,128]{2,1,0:T(1,128)S(1)} %bitcast.21), custom_call_target="tpu_custom_call" | custom-call | flops 20000000000 | bytes 1000000 | tf_op jit(solution)/shard_map/force_pass/pallas_call | solution.py:387
  97.4 0.0 all-to-all-done.1
  97.4 13.3 %sample_pass.1 = f32[4,2,3,4,128]{4,3,2,1,0:T(4,128)S(1)} custom-call(f32[2]{0:T(128)S(1)} %copy-done.10, f32[1024,128]{1,0:T(8,128)S(1)} %bitcast.14, f32[4,8,8,128]{3,2,1,0:T(8,128)S(1)} %get-tuple-element.14.atoms_ref, bf16[3,256,256]{2,1,0:T(8,128)(2,1)S(1)} %copy-done.1), custom_call_target="tpu_custom_call" | custom-call | tf_op jit(solution)/shard_map/sample_pass/pallas_call | solution.py:724
  110.7 0.6 add_bitcast_fusion
Async XLA Ops:
  0.6 0.7 copy-start.10
  1.3 1.0 copy-start
  2.3 0.8 copy-start.5
  3.1 0.8 copy-start.6
  3.9 0.7 copy-start.7
  4.6 0.7 copy-start.8
  26.6 19.6 %all-to-all-start = ((f32[128,8,128]{2,1,0:T(8,128)}), f32[128,8,128]{2,1,0:T(8,128)S(1)}, u32[]{:S(2)}, u32[]{:S(2)}) async-start(f32[128,8,128]{2,1,0:T(8,128)} %bitcast.3), calls=%async_computation | async-start | bytes 1048576 | tf_op jit(solution)/shard_map/all_to_all | solution.py:741
  31.0 0.7 copy-start.11
  31.0 0.7 copy-start.12
  31.0 0.7 copy-start.13
  31.7 14.5 %copy-start.1 = (bf16[3,256,256]{2,1,0:T(8,128)(2,1)S(1)}, bf16[3,256,256]{2,1,0:T(8,128)(2,1)}, u32[]{:S(2)}) copy-start(bf16[3,256,256]{2,1,0:T(8,128)(2,1)} %constant.10.clone.table_ref) | copy-start | bytes 1179652
  31.7 14.5 %copy-start.2 = (bf16[3,512,256]{2,1,0:T(8,128)(2,1)S(1)}, bf16[3,512,256]{2,1,0:T(8,128)(2,1)}, u32[]{:S(2)}) copy-start(bf16[3,512,256]{2,1,0:T(8,128)(2,1)} %constant.13.clone.mixed_turned_ref) | copy-start | bytes 2359300
  31.7 14.5 %copy-start.3 = (bf16[2,256,512]{2,1,0:T(8,128)(2,1)S(1)}, bf16[2,256,512]{2,1,0:T(8,128)(2,1)}, u32[]{:S(2)}) copy-start(bf16[2,256,512]{2,1,0:T(8,128)(2,1)} %constant.12.clone.mixed_ref) | copy-start | bytes 1572868
  31.7 14.5 %copy-start.4 = (bf16[2,256,256]{2,1,0:T(8,128)(2,1)S(1)}, bf16[2,256,256]{2,1,0:T(8,128)(2,1)}, u32[]{:S(2)}) copy-start(bf16[2,256,256]{2,1,0:T(8,128)(2,1)} %constant.11.clone.turned_ref) | copy-start | bytes 786436
  60.0 5.5 %copy-start.9 = (s32[4,2,4]{2,1,0:T(2,128)S(1)}, s32[4,2,4]{2,1,0:T(2,128)}, u32[]{:S(2)}) copy-start(s32[4,2,4]{2,1,0:T(2,128)} %count_ref.3) | copy-start | bytes 388
  60.1 37.4 %all-to-all-start.1 = ((f32[128,8,128]{2,1,0:T(8,128)}), f32[128,8,128]{2,1,0:T(8,128)S(1)}, u32[]{:S(2)}, u32[]{:S(2)}) async-start(f32[128,8,128]{2,1,0:T(8,128)} %bitcast.8), calls=%async_computation.1 | async-start | bytes 1048576 | tf_op jit(solution)/shard_map/all_to_all | solution.py:745

commit v4 on v3

--- a/solution.py
+++ b/solution.py
@@ -134,13 +134,18 @@
     return ones, twos
 
 
+def cell_at(r):
+    return lax.div(r, 24), lax.rem(lax.div(r, 6), 4), lax.rem(r, 6)
+
+
 def source_features(ext_ref, slope_ref, wide, feat_b, scales, ratios):
     ones, twos = patterns((0, 2, 5), (1, 3), (24,), (25,))
     low_six, low_four, low_two, low_three = [sublane() < n for n in (6, 4, 2, 3)]
 
     def cell(r, _):
         def row(f):
-            return jnp.broadcast_to(ext_ref[r, f:f + 1, :], (8, 128))
+            x, y, z = cell_at(r)
+            return jnp.broadcast_to(ext_ref[x, y, z, f:f + 1, :], (8, 128))
 
         x = row(0) + (lax.div(r, 24) - 3).astype(F32)
         y = row(1) + (lax.rem(lax.div(r, 6), 4) - 2).astype(F32)
@@ -150,7 +155,7 @@
         if wide is not None:
             wide[r, 0], wide[r, 1], wide[r, 2] = x, y, z
             wide[r, 3] = jnp.where(code == 1.0, ratios[1], ratios[0])
-            wide[r, 4] = jnp.broadcast_to(slope_ref[r], (8, 128))
+            wide[r, 4] = jnp.broadcast_to(slope_ref[cell_at(r)], (8, 128))
         square = -scale * (x * x + y * y + z * z)
         double = scale + scale
         x, y, z = double * x, double * y, double * z
@@ -175,7 +180,8 @@
         r = corner(t) + 31
 
         def row(f):
-            return jnp.broadcast_to(ext_ref[r, f:f + 1, :], (8, 128))
+            x, y, z = cell_at(r)
+            return jnp.broadcast_to(ext_ref[x, y, z, f:f + 1, :], (8, 128))
 
         x = row(0) + (lax.div(t, 8) - 2).astype(F32)
         y = row(1) + (lax.rem(lax.div(t, 4), 2) - 1).astype(F32)
@@ -187,7 +193,7 @@
         tail = jnp.zeros((8, 128), F32)
         if gains is not None:
             second = code == 1.0
-            tilt = jnp.broadcast_to(slope_ref[r], (8, 128)) / jnp.where(second, ratios[1], ratios[0])
+            tilt = jnp.broadcast_to(slope_ref[cell_at(r)], (8, 128)) / jnp.where(second, ratios[1], ratios[0])
             tail = jnp.where(low_five, jnp.where(second, gains[1], gains[0]), jnp.where(low_seven, tilt, 0.0))
         blocks = [jnp.where(low_six, rest, x), jnp.where(low_four, x, y), jnp.where(low_two, y, z),
                   jnp.where(low_three, 1.0, tail)]
@@ -214,10 +220,12 @@
     return jnp.concatenate([feat_b[pl.ds(r + KF * dz, KF), :] for dz in range(3)], axis=1)
 
 
-def density_kernel(amplitude_ref, pair_ref, embed_ref, ext_ref, density_ref, slope_ref, feat_b, own_t, keep, totals, mat):
-    amplitudes, pairs, embeds = [[filled(ref, k) for k in range(2)] for ref in (amplitude_ref, pair_ref, embed_ref)]
+def density_features(ext_ref, amplitudes, feat_b, own_t, keep):
     source_features(ext_ref, None, None, feat_b, [cube_root(value) for value in amplitudes], None)
     target_features(ext_ref, own_t, keep, None, None, None)
+
+
+def densities(pairs, embeds, density_ref, slope_ref, feat_b, own_t, keep, totals, mat):
     lanes = lax.broadcasted_iota(jnp.int32, (128, 128), 1)
     other = lanes != lax.broadcasted_iota(jnp.int32, (128, 128), 0)
 
@@ -258,13 +266,14 @@
     density = mat[0:32, :] * alive
     density_ref[...] = density.reshape(8, 4, 128)
     tilts = [jnp.concatenate([3.0 * embed / (pair * pair)] * 4, axis=0) for embed, pair in zip(embeds, pairs)]
-    slope_ref[...] = (by_species(code, tilts) / jnp.sqrt(1.0 + density)).reshape(32, 1, 128)
-
-
-def force_kernel(count_ref, amplitude_ref, pair_ref, ext_ref, slope_ref, out_ref, feat_b, own_t, keep, wide, near_a, near_b,
+    slope_ref[...] = (by_species(code, tilts) / jnp.sqrt(1.0 + density)).reshape(4, 2, 4, 1, 128)
+
+
+def force_kernel(count_ref, amplitude_ref, pair_ref, ext_ref, slope_ref, given_ref, out_ref, density_ref, feat_b, own_t, keep, wide, near_a, near_b,
                  part_a, part_b, mat, table):
     amplitudes, pairs = [[filled(ref, k) for k in range(2)] for ref in (amplitude_ref, pair_ref)]
     ratios = [amplitude / (pair * pair) for amplitude, pair in zip(amplitudes, pairs)]
+    density_ref[...] = given_ref[...]
     gains = [-4.0 * pair / amplitude for amplitude, pair in zip(amplitudes, pairs)]
     source_features(ext_ref, slope_ref, wide, feat_b, pairs, ratios)
     target_features(ext_ref, own_t, keep, slope_ref, gains, ratios)
@@ -370,25 +379,12 @@
     return [pltpu.VMEM((146 * KF, 128), BF16), pltpu.VMEM((32, 128, KF), BF16), pltpu.VMEM((4, 32, 128), F32)]
 
 
-def density_pass(amplitude, pair, embed, ext):
-    return pl.pallas_call(
-        density_kernel,
-        out_shape=[jax.ShapeDtypeStruct((8, 4, 128), F32), jax.ShapeDtypeStruct((32, 1, 128), F32)],
-        in_specs=[SMEM_SPEC] * 3 + [VMEM_SPEC],
-        out_specs=[VMEM_SPEC] * 2,
-        scratch_shapes=features_scratch() + [pltpu.VMEM((256, 128), F32), pltpu.VMEM((128, 128), F32)],
-        compiler_params=pltpu.CompilerParams(vmem_limit_bytes=16 << 20),
-        cost_estimate=pl.CostEstimate(flops=10_000_000_000, bytes_accessed=1_000_000, transcendentals=0),
-        name="density_pass",
-    )(amplitude, pair, embed, ext)
-
-
-def force_pass(counts, amplitude, pair, ext, slope):
+def force_pass(counts, amplitude, pair, ext, slope, density):
     return pl.pallas_call(
         force_kernel,
-        out_shape=jax.ShapeDtypeStruct((8, 3, 4, 128), F32),
-        in_specs=[SMEM_SPEC] * 3 + [VMEM_SPEC] * 2,
-        out_specs=VMEM_SPEC,
+        out_shape=[jax.ShapeDtypeStruct((8, 3, 4, 128), F32), jax.ShapeDtypeStruct((8, 4, 128), F32)],
+        in_specs=[SMEM_SPEC] * 3 + [VMEM_SPEC] * 3,
+        out_specs=[VMEM_SPEC] * 2,
         scratch_shapes=features_scratch() + [
             pltpu.VMEM((144, 5, 8, 128), F32),
             pltpu.VMEM((32, 128, 128), F32),
@@ -401,7 +397,7 @@
         compiler_params=pltpu.CompilerParams(vmem_limit_bytes=24 << 20),
         cost_estimate=pl.CostEstimate(flops=20_000_000_000, bytes_accessed=1_000_000, transcendentals=0),
         name="force_pass",
-    )(counts, amplitude, pair, ext, slope)
+    )(counts, amplitude, pair, ext, slope, density)
 
 
 EWALD_SPLIT = 0.7
@@ -487,10 +483,35 @@
                 plane * 128:(plane + 1) * 128, xq * 128:(xq + 1) * 128]
 
 
-def gather_kernel(charge_ref, count_ref, offset_ref, fraction_ref, species_ref, table_ref, ext_ref, got_ref, out_ref,
-                  atoms, rho, send_sem, recv_sem, column_send, column_recv):
+def device_at(d):
+    return lax.div(d, 32), lax.rem(lax.div(d, 4), 8), lax.rem(d, 4)
+
+
+def front_kernel(charge_hbm, amplitude_hbm, pair_hbm, embed_hbm, count_hbm, offset_hbm, fraction_hbm, species_hbm, table_hbm,
+                 turned_hbm, mixed_hbm, mixed_turned_hbm, ext_ref, got_ref, density_ref, wide_ref, out_ref,
+                 charge_ref, amplitude_ref, pair_ref, embed_ref, count_ref, offset_ref, fraction_ref, species_ref, table_ref,
+                 turned_ref, mixed_ref, mixed_turned_ref, atoms, rho, lines, planes, slopes, feat_b, own_t, rows, totals, mat,
+                 load_sem, halo_send, halo_recv, column_send, column_recv, slope_send, slope_recv, line_send, line_recv):
     place = here()
-    signal([toward(place, side) for side in SIDES] + [column_devices(place)[1]])
+    me = place[0] * 32 + place[1] * 4 + place[2]
+    loads = [
+        pltpu.make_async_copy(src, dst, load_sem.at[n])
+        for n, (src, dst) in enumerate((
+            (count_hbm, count_ref), (species_hbm, species_ref), (offset_hbm, offset_ref), (fraction_hbm, fraction_ref),
+            (charge_hbm, charge_ref), (amplitude_hbm, amplitude_ref), (pair_hbm, pair_ref), (embed_hbm, embed_ref),
+            (table_hbm, table_ref), (turned_hbm, turned_ref), (mixed_hbm, mixed_ref), (mixed_turned_hbm, mixed_turned_ref)))
+    ]
+    for load in loads:
+        load.start()
+    barrier = pltpu.get_barrier_semaphore()
+
+    def greet(i, _):
+        pl.semaphore_signal(barrier, inc=1, device_id=device_at(lax.rem(me + i, 128)), device_id_type=MESH)
+        return 0
+
+    lax.fori_loop(1, 128, greet, 0)
+    for load in loads[:4]:
+        load.wait()
     slot = lax.broadcasted_iota(jnp.int32, (1, 128), 1)
 
     def pack(n, _):
@@ -509,37 +530,57 @@
 
     lax.fori_loop(0, 8, pack, 0)
 
-    def keep(n, _):
+    def keep_own(n, _):
         got_ref[place[2], n] = atoms[place[2], n]
         return 0
 
-    lax.fori_loop(0, 8, keep, 0)
-    await_signals(27)
+    lax.fori_loop(0, 8, keep_own, 0)
+    for load in loads[4:]:
+        load.wait()
+    pl.semaphore_wait(barrier, 127)
     columns = column_copies(atoms, got_ref, place, column_send, column_recv)
-    halo = halo_copies(ext_ref, 1, ext_ref, place, send_sem, recv_sem)
+    halo = halo_copies(ext_ref, 1, ext_ref, place, halo_send, halo_recv)
     for copy in columns:
         copy.wait()
-    spread_and_transform(got_ref, [charge_ref[k] for k in range(2)], table_ref, out_ref, rho)
+    spread_and_transform(got_ref, [charge_ref[k] for k in range(2)], table_ref, lines, rho)
     for copy in halo:
         copy.wait()
-
-
-def plane_kernel(in_ref, slope_ref, table_ref, turned_ref, mixed_ref, mixed_turned_ref, out_ref, wide_ref, send_sem,
-                 recv_sem):
-    place = here()
-    devices = [toward(place, side) for side in SIDES]
-    signal(devices)
-
-    def keep(t, _):
+    amplitudes, pairs, embeds = [[filled(ref, k) for k in range(2)] for ref in (amplitude_ref, pair_ref, embed_ref)]
+    density_features(ext_ref, amplitudes, feat_b, own_t, rows)
+
+    def line_copy(i):
+        other = lax.rem(me + i, 128)
+        return pltpu.make_async_remote_copy(
+            src_ref=lines.at[pl.ds(pl.multiple_of(other * 8, 8), 8), :],
+            dst_ref=planes.at[pl.ds(pl.multiple_of(me * 8, 8), 8), :],
+            send_sem=line_send.at[i],
+            recv_sem=line_recv.at[i],
+            device_id=device_at(other),
+            device_id_type=MESH,
+        )
+
+    def send_line(i, _):
+        line_copy(i).start()
+        return 0
+
+    def wait_line(i, _):
+        line_copy(i).wait()
+        return 0
+
+    lax.fori_loop(1, 128, send_line, 0)
+    mine = pl.ds(pl.multiple_of(me * 8, 8), 8)
+    planes[mine, :] = lines[mine, :]
+    densities(pairs, embeds, density_ref, slopes, feat_b, own_t, rows, totals, mat)
+
+    def keep_slope(t, _):
         x, y, z = lax.div(t, 8), lax.rem(lax.div(t, 4), 2), lax.rem(t, 4)
-        wide_ref[x + 1, y + 1, z + 1] = slope_ref[x, y, z]
-        return 0
-
-    lax.fori_loop(0, 32, keep, 0)
-    await_signals(26)
-    halo = halo_copies(slope_ref, 0, wide_ref, place, send_sem, recv_sem)
-    transform_planes(place[0] * 32 + place[1] * 4 + place[2], in_ref, table_ref, turned_ref, mixed_ref, mixed_turned_ref,
-                     out_ref)
+        wide_ref[x + 1, y + 1, z + 1] = slopes[x, y, z]
+        return 0
+
+    lax.fori_loop(0, 32, keep_slope, 0)
+    halo = halo_copies(slopes, 0, wide_ref, place, slope_send, slope_recv)
+    lax.fori_loop(1, 128, wait_line, 0)
+    transform_planes(me, planes, table_ref, turned_ref, mixed_ref, mixed_turned_ref, out_ref)
     for copy in halo:
         copy.wait()
 
@@ -548,7 +589,8 @@
     lane = lax.broadcasted_iota(jnp.int32, (16, 8, 128), 2)
 
     def pick(ref, half, g):
-        return jnp.concatenate([ref[gx, half * 4 + g] for gx in range(4)], axis=0)
+        starts = [(gx * 32 + (half * 4 + g) * 4) * 8 for gx in range(4)]
+        return jnp.concatenate([ref[start:start + 32, :] for start in starts], axis=0).reshape(16, 8, 128)
 
     rows = []
     for xr in range(4):
@@ -598,7 +640,8 @@
                     moved = pltpu.roll(moved, (xr - g) * 32 % 128, 1)
                 value = jnp.where(lax.div(lane, 32) == xr, moved.reshape(16, 8, 128), value)
             for gx in range(4):
-                out_ref[gx, half * 4 + g] = value[gx * 4:(gx + 1) * 4]
+                start = (gx * 32 + (half * 4 + g) * 4) * 8
+                out_ref[start:start + 32, :] = value[gx * 4:(gx + 1) * 4].reshape(32, 128)
 
 
 def sample_kernel(charge_ref, in_ref, atoms_ref, table_ref, back_ref, field, out, send_sem, recv_sem):
@@ -691,33 +734,42 @@
     return (parts_of(TABLE), parts_of(TABLE.T)[:2], parts_of(MIXED)[:2], parts_of(MIXED.T))
 
 
-def gather_pass(charge, counts, offset, fraction, species, table):
+def front_pass(*arrays):
+    hbm = pl.BlockSpec(memory_space=pltpu.HBM)
+    small = [pltpu.SMEM((2,), F32)] * 4 + [pltpu.SMEM((4, 2, 4), jnp.int32)]
     return pl.pallas_call(
-        gather_kernel,
+        front_kernel,
         out_shape=[
             jax.ShapeDtypeStruct((6, 4, 6, 4, 128), F32),
             jax.ShapeDtypeStruct((4, 8, 8, 128), F32),
+            jax.ShapeDtypeStruct((8, 4, 128), F32),
+            jax.ShapeDtypeStruct((6, 4, 6, 1, 128), F32),
             jax.ShapeDtypeStruct((1024, 128), F32),
         ],
-        in_specs=[SMEM_SPEC] * 2 + [VMEM_SPEC] * 4,
-        out_specs=[VMEM_SPEC] * 3,
-        scratch_shapes=[pltpu.VMEM((4, 8, 8, 128), F32), pltpu.VMEM((256, 512), F32), DMA((26,)), DMA((26,)), DMA((3,)),
-                        DMA((3,))],
+        in_specs=[hbm] * 12,
+        out_specs=[VMEM_SPEC] * 5,
+        scratch_shapes=small + [
+            pltpu.VMEM((4, 2, 3, 4, 128), jnp.int32),
+            pltpu.VMEM((4, 2, 3, 4, 128), F32),
+            pltpu.VMEM((4, 2, 4, 128), jnp.int32),
+            pltpu.VMEM((3, 256, 256), BF16),
+            pltpu.VMEM((2, 256, 256), BF16),
+            pltpu.VMEM((2, 256, 512), BF16),
+            pltpu.VMEM((3, 512, 256), BF16),
+            pltpu.VMEM((4, 8, 8, 128), F32),
+            pltpu.VMEM((256, 512), F32),
+            pltpu.VMEM((1024, 128), F32),
+            pltpu.VMEM((1024, 128), F32),
+            pltpu.VMEM((4, 2, 4, 1, 128), F32),
+        ] + features_scratch() + [
+            pltpu.VMEM((256, 128), F32),
+            pltpu.VMEM((128, 128), F32),
+            DMA((12,)),
+            DMA((26,)), DMA((26,)), DMA((3,)), DMA((3,)), DMA((26,)), DMA((26,)), DMA((128,)), DMA((128,)),
+        ],
         compiler_params=comm_params(0),
-        name="gather_pass",
-    )(charge, counts, offset, fraction, species, table)
-
-
-def plane_pass(planes, slope, table, turned, mixed, mixed_turned):
-    return pl.pallas_call(
-        plane_kernel,
-        out_shape=[jax.ShapeDtypeStruct((4, 8, 4, 8, 128), F32), jax.ShapeDtypeStruct((6, 4, 6, 1, 128), F32)],
-        in_specs=[VMEM_SPEC] * 6,
-        out_specs=[VMEM_SPEC] * 2,
-        scratch_shapes=[DMA((26,)), DMA((26,))],
-        compiler_params=comm_params(1),
-        name="plane_pass",
-    )(planes, slope, table, turned, mixed, mixed_turned)
+        name="front_pass",
+    )(*arrays)
 
 
 def sample_pass(charge, lines, atoms, table):
@@ -735,15 +787,11 @@
 def on_device(cell_counts, grid_offset, fraction, species, species_density, species_pair, species_embed, species_charge):
     table, turned, mixed, mixed_turned = constants()
     order = (0, 1, 3, 2, 4)
-    extended, columns, lines = gather_pass(
-        species_charge, cell_counts, grid_offset.transpose(order), fraction.transpose(order), species, table)
-    extended = extended.reshape(144, 4, 128)
-    planes = lax.all_to_all(lines.reshape(128, 8, 128), AXES, split_axis=0, concat_axis=0, tiled=True)
-    density, slope = density_pass(species_density, species_pair, species_embed, extended)
-    planes, wide_slope = plane_pass(
-        planes.reshape(4, 8, 4, 8, 128), slope.reshape(4, 2, 4, 1, 128), table, turned, mixed, mixed_turned)
+    extended, columns, density, wide_slope, planes = front_pass(
+        species_charge, species_density, species_pair, species_embed, cell_counts, grid_offset.transpose(order),
+        fraction.transpose(order), species, table, turned, mixed, mixed_turned)
     lines = lax.all_to_all(planes.reshape(128, 8, 128), AXES, split_axis=0, concat_axis=0, tiled=True)
-    eam = force_pass(cell_counts, species_density, species_pair, extended, wide_slope.reshape(144, 1, 128))
+    eam, density = force_pass(cell_counts, species_density, species_pair, extended, wide_slope, density)
     electric = sample_pass(species_charge, lines.reshape(1024, 128), columns, table)
     forces = eam.reshape(4, 2, 3, 4, 128) + COUPLING * electric
     return forces.transpose(order), density.reshape(4, 2, 4, 128)

time: 112 us -> 109 us (0.973)
  starting transfers between devices: 9.86 us -> 6.24 us
  local copies, waits for them, and re-layouts: 5.33 us -> 8.47 us
  Pallas kernels: 94.7 us -> 92.4 us
    all_to_all x1 -> x0, starting transfers between devices: 4.39 us -> none  [on_device(): lax.all_to_all(lines.reshape(128, 8, 128), AXES, split_axis=0, concat_axi...]
    unnamed x28, local copies, waits for them, and re-layouts: 5.33 us -> 8.47 us
    pallas_call x1, Pallas kernels: 13.3 us -> 10.2 us  [sample_pass(): pl.pallas_call(sample_kernel, out_shape=jax.ShapeDtypeStruct((4, 2, 3, 4,...]
    pallas_call x4 -> x2, Pallas kernels: 81.5 us -> 82.2 us  [the longest x1 47.3 us: front_pass(): pl.pallas_call(front_kernel, out_shape=[jax.ShapeDtypeStruct((6, 4, 6, 4,...]
  transfers between devices with their start and end apart: 2 -> 1, of which waited for: 0 -> 0; matrix products, arithmetic and copies ran while one was open for 0% -> 0% of each run, Pallas kernels for 42% -> 32%
where the time goes in v4:
time: 109 us; the launch traced here: 108 us
  Pallas kernels  92.4 us (85%)
  local copies, waits for them, and re-layouts  8.47 us (8%)
  starting transfers between devices  6.24 us (6%)
    pallas_call x1, Pallas kernels, front_pass(): pl.pallas_call(front_kernel, out_shape=[jax.ShapeDtypeStruct((6, 4, 6, 4,...  47.3 us
    pallas_call x1, Pallas kernels, force_pass(): pl.pallas_call(force_kernel, out_shape=[jax.ShapeDtypeStruct((8, 3, 4, 12...  34.8 us
    pallas_call x1, Pallas kernels, sample_pass(): pl.pallas_call(sample_kernel, out_shape=jax.ShapeDtypeStruct((4, 2, 3, 4,...  10.2 us
    unnamed x28, local copies, waits for them, and re-layouts  8.47 us
    all_to_all x1, starting transfers between devices, on_device(): lax.all_to_all(planes.reshape(128, 8, 128), AXES, split_axis=0, concat_ax...  6.24 us
  transfers between devices with their start and end apart: 1, of which 0 were waited for; matrix products, arithmetic and copies ran while one was open for 0% of the time, Pallas kernels for 32%

profile of v4, /device:TPU:1, one launch (start us, length us, event | category | flops | bytes accessed | tf_op | source)
XLA Modules:
  0.0 108.4 jit_solution(6819236560963744805)
XLA Ops:
  0.6 0.0 copy-start.13
  0.6 0.0 copy-start.10
  0.7 0.0 copy-start.11
  0.7 0.0 copy-start.12
  0.7 0.6 copy-done.13
  1.3 0.0 copy-done.10
  1.3 0.0 copy-done.11
  1.3 0.0 copy-done.12
  1.3 0.0 copy-start
  1.3 1.0 copy-done
  2.3 0.0 copy-start.2
  2.3 1.1 %copy-done.2 = bf16[3,512,256]{2,1,0:T(8,128)(2,1)S(1)} copy-done((bf16[3,512,256]{2,1,0:T(8,128)(2,1)S(1)}, bf16[3,512,256]{2,1,0:T(8,128)(2,1)}, u32[]{:S(2)}) %copy-start.2) | copy-done | bytes 786456
  3.5 0.0 copy-start.3
  3.5 1.0 copy-done.3
  4.5 0.0 copy-start.4
  4.5 0.9 copy-done.4
  5.5 0.0 copy-start.5
  5.5 0.8 copy-done.5
  6.3 0.0 copy-start.6
  6.3 0.8 copy-done.6
  7.1 0.0 copy-start.7
  7.1 0.7 copy-done.7
  7.8 0.0 copy-start.8
  7.8 0.7 copy-done.8
  8.5 47.3 %front_pass.1 = (f32[6,4,6,4,128]{4,3,2,1,0:T(4,128)S(1)}, f32[4,8,8,128]{3,2,1,0:T(8,128)S(1)}, f32[8,4,128]{2,1,0:T(4,128)S(1)}, f32[6,4,6,1,128]{4,3,2,1,0:T(1,128)S(1)}, f32[1024,128]{1,0:T(8,128)}) custom-call(f32[2]{0:T(128)S(1)} %copy-done.10, f32[2]{0:T(128)S(1)} %copy-done.12, f32[2]{0:T(128)S(1)} %copy-done.13, f32[2]{0:T(128)S(1)} %copy-done.11, ...), custom_call_target="tpu_custom_call" | custom-call | tf_op jit(solution)/shard_map/front_pass/pallas_call | solution.py:740
  55.8 6.2 %all-to-all-start = ((f32[128,8,128]{2,1,0:T(8,128)}), f32[128,8,128]{2,1,0:T(8,128)S(1)}, u32[]{:S(2)}, u32[]{:S(2)}) async-start(f32[128,8,128]{2,1,0:T(8,128)} %bitcast.3), calls=%async_computation | async-start | bytes 1048576 | tf_op jit(solution)/shard_map/all_to_all | solution.py:793
  62.1 0.0 copy-start.9
  62.1 0.7 copy-done.9
  62.7 0.0 copy-start.1
  62.8 34.8 %force_pass.1 = (f32[8,3,4,128]{3,2,1,0:T(4,128)S(1)}, f32[8,4,128]{2,1,0:T(4,128)}) custom-call(s32[4,2,4]{2,1,0:T(2,128)S(1)} %copy-done.9, f32[2]{0:T(128)S(1)} %copy-done.12, f32[2]{0:T(128)S(1)} %copy-done.13, f32[6,4,6,4,128]{4,3,2,1,0:T(4,128)S(1)} %get-tuple-element.9.ext_ref, f32[6,4,6,1,128]{4,3,2,1,0:T(1,128)S(1)} %get-tuple-element.10.slope_ref, ...), custom_call_target="tpu_custom_call" | custom-call | flops 20000000000 | bytes 1000000 | tf_op jit(solution)/shard_map/force_pass/pallas_call | solution.py:383
  97.6 0.0 all-to-all-done
  97.6 0.0 copy-done.1
  97.6 10.2 %sample_pass.1 = f32[4,2,3,4,128]{4,3,2,1,0:T(4,128)S(1)} custom-call(f32[2]{0:T(128)S(1)} %copy-done.10, f32[1024,128]{1,0:T(8,128)S(1)} %bitcast.8, f32[4,8,8,128]{3,2,1,0:T(8,128)S(1)} %get-tuple-element.14.atoms_ref, bf16[3,256,256]{2,1,0:T(8,128)(2,1)S(1)} %copy-done.1), custom_call_target="tpu_custom_call" | custom-call | tf_op jit(solution)/shard_map/sample_pass/pallas_call | solution.py:776
  107.8 0.6 add_bitcast_fusion
Async XLA Ops:
  0.6 0.7 copy-start.13
  0.6 0.7 copy-start.10
  0.7 0.7 copy-start.11
  0.7 0.7 copy-start.12
  1.3 1.0 copy-start
  2.3 1.1 %copy-start.2 = (bf16[3,512,256]{2,1,0:T(8,128)(2,1)S(1)}, bf16[3,512,256]{2,1,0:T(8,128)(2,1)}, u32[]{:S(2)}) copy-start(bf16[3,512,256]{2,1,0:T(8,128)(2,1)} %constant.13.clone.mixed_turned_hbm) | copy-start | bytes 2359300
  3.5 1.0 copy-start.3
  4.5 0.9 copy-start.4
  5.5 0.8 copy-start.5
  6.3 0.8 copy-start.6
  7.1 0.7 copy-start.7
  7.8 0.7 copy-start.8
  55.8 41.8 %all-to-all-start = ((f32[128,8,128]{2,1,0:T(8,128)}), f32[128,8,128]{2,1,0:T(8,128)S(1)}, u32[]{:S(2)}, u32[]{:S(2)}) async-start(f32[128,8,128]{2,1,0:T(8,128)} %bitcast.3), calls=%async_computation | async-start | bytes 1048576 | tf_op jit(solution)/shard_map/all_to_all | solution.py:793
  62.1 0.7 copy-start.9
  62.7 34.8 %copy-start.1 = (bf16[3,256,256]{2,1,0:T(8,128)(2,1)S(1)}, bf16[3,256,256]{2,1,0:T(8,128)(2,1)}, u32[]{:S(2)}) copy-start(bf16[3,256,256]{2,1,0:T(8,128)(2,1)} %constant.10.clone.table_hbm.table_ref) | copy-start | bytes 1179652

commit v5 on v4

--- a/solution.py
+++ b/solution.py
@@ -220,12 +220,7 @@
     return jnp.concatenate([feat_b[pl.ds(r + KF * dz, KF), :] for dz in range(3)], axis=1)
 
 
-def density_features(ext_ref, amplitudes, feat_b, own_t, keep):
-    source_features(ext_ref, None, None, feat_b, [cube_root(value) for value in amplitudes], None)
-    target_features(ext_ref, own_t, keep, None, None, None)
-
-
-def densities(pairs, embeds, density_ref, slope_ref, feat_b, own_t, keep, totals, mat):
+def density_steps(feat_b, own_t, totals, mat):
     lanes = lax.broadcasted_iota(jnp.int32, (128, 128), 1)
     other = lanes != lax.broadcasted_iota(jnp.int32, (128, 128), 0)
 
@@ -251,16 +246,19 @@
         mat[pl.ds(2 * n, 1), :] = sums[0:1, 0:128]
         mat[pl.ds(2 * n + 1, 1), :] = sums[0:1, 128:256]
 
-    totals[...] = jnp.zeros((256, 128), F32)
-
     def both(n, _):
         settle(jnp.maximum(n - 1, 0))
         totals[0:128, :] = target(2 * n)
         totals[128:256, :] = target(2 * n + 1)
         return 0
 
-    lax.fori_loop(0, 16, both, 0)
-    settle(15)
+    def run(first, last):
+        lax.fori_loop(first, last, both, 0)
+
+    return run, lambda: settle(15)
+
+
+def densities(pairs, embeds, density_ref, slope_ref, keep, mat):
     code = keep[3]
     alive = by_species(code, (1.0, 1.0))
     density = mat[0:32, :] * alive
@@ -269,8 +267,21 @@
     slope_ref[...] = (by_species(code, tilts) / jnp.sqrt(1.0 + density)).reshape(4, 2, 4, 1, 128)
 
 
-def force_kernel(count_ref, amplitude_ref, pair_ref, ext_ref, slope_ref, given_ref, out_ref, density_ref, feat_b, own_t, keep, wide, near_a, near_b,
-                 part_a, part_b, mat, table):
+def force_kernel(count_hbm, amplitude_hbm, pair_hbm, ext_hbm, slope_hbm, given_hbm, electric_hbm, out_ref, density_ref,
+                 count_ref, amplitude_ref, pair_ref, ext_ref, slope_ref, given_ref, electric_ref, feat_b, own_t, keep, wide,
+                 near_a, near_b, part_a, part_b, mat, table, load_sem):
+    loads = [
+        pltpu.make_async_copy(src, dst, load_sem.at[n])
+        for n, (src, dst) in enumerate((
+            (amplitude_hbm, amplitude_ref), (pair_hbm, pair_ref), (ext_hbm, ext_ref), (slope_hbm, slope_ref),
+            (count_hbm, count_ref), (given_hbm, given_ref), (electric_hbm, electric_ref)))
+    ]
+    for load in loads:
+        load.start()
+    part_a[...] = jnp.zeros((4, 128, 128), F32)
+    part_b[...] = jnp.zeros((4, 128, 128), F32)
+    for load in loads:
+        load.wait()
     amplitudes, pairs = [[filled(ref, k) for k in range(2)] for ref in (amplitude_ref, pair_ref)]
     ratios = [amplitude / (pair * pair) for amplitude, pair in zip(amplitudes, pairs)]
     density_ref[...] = given_ref[...]
@@ -286,8 +297,6 @@
         return 0
 
     lax.fori_loop(0, 32, fill, 0)
-    part_a[...] = jnp.zeros((4, 128, 128), F32)
-    part_b[...] = jnp.zeros((4, 128, 128), F32)
     lane = lax.broadcasted_iota(jnp.int32, (ROWS, 128), 1)
     lane3 = lax.broadcasted_iota(jnp.int32, (ROWS // 8, 8, 128), 2)
     row3 = lax.broadcasted_iota(jnp.int32, (ROWS // 8, 8, 128), 0) * 8 + lax.broadcasted_iota(
@@ -364,7 +373,7 @@
     amplitude = by_species(keep[3], [jnp.concatenate([value] * 4, axis=0) for value in amplitudes])
     for m in range(3):
         value = amplitude * (mat[pl.ds(m + 1, 32, stride=4), :] - keep[m] * whole)
-        out_ref[:, m] = value.reshape(8, 4, 128)
+        out_ref[:, m] = value.reshape(8, 4, 128) + COUPLING * electric_ref[:, m]
 
 
 def sel_matrix():
@@ -379,13 +388,21 @@
     return [pltpu.VMEM((146 * KF, 128), BF16), pltpu.VMEM((32, 128, KF), BF16), pltpu.VMEM((4, 32, 128), F32)]
 
 
-def force_pass(counts, amplitude, pair, ext, slope, density):
+def force_pass(*arrays):
     return pl.pallas_call(
         force_kernel,
         out_shape=[jax.ShapeDtypeStruct((8, 3, 4, 128), F32), jax.ShapeDtypeStruct((8, 4, 128), F32)],
-        in_specs=[SMEM_SPEC] * 3 + [VMEM_SPEC] * 3,
+        in_specs=[pl.BlockSpec(memory_space=pltpu.HBM)] * 7,
         out_specs=[VMEM_SPEC] * 2,
-        scratch_shapes=features_scratch() + [
+        scratch_shapes=[
+            pltpu.SMEM((4, 2, 4), jnp.int32),
+            pltpu.SMEM((2,), F32),
+            pltpu.SMEM((2,), F32),
+            pltpu.VMEM((6, 4, 6, 4, 128), F32),
+            pltpu.VMEM((6, 4, 6, 1, 128), F32),
+            pltpu.VMEM((8, 4, 128), F32),
+            pltpu.VMEM((8, 3, 4, 128), F32),
+        ] + features_scratch() + [
             pltpu.VMEM((144, 5, 8, 128), F32),
             pltpu.VMEM((32, 128, 128), F32),
             pltpu.VMEM((32, 128, 128), F32),
@@ -393,11 +410,12 @@
             pltpu.VMEM((4, 128, 128), F32),
             pltpu.VMEM((128, 128), F32),
             pltpu.SMEM((64,), jnp.int32),
+            pltpu.SemaphoreType.DMA((7,)),
         ],
-        compiler_params=pltpu.CompilerParams(vmem_limit_bytes=24 << 20),
+        compiler_params=pltpu.CompilerParams(vmem_limit_bytes=67043328),
         cost_estimate=pl.CostEstimate(flops=20_000_000_000, bytes_accessed=1_000_000, transcendentals=0),
         name="force_pass",
-    )(counts, amplitude, pair, ext, slope, density)
+    )(*arrays)
 
 
 EWALD_SPLIT = 0.7
@@ -448,7 +466,7 @@
     return jnp.where(point == lower, 1.0 - weight, 0.0) + jnp.where(point == lower + 1.0, weight, 0.0)
 
 
-def spread_and_transform(atoms_ref, charges, table_ref, out_ref, rho):
+def spread_and_transform(atoms_ref, charges, table_ref, out_ref, rho, gz, arrivals):
     def layer(cz, _):
         source, cell = lax.div(cz, 4), lax.rem(cz, 4)
 
@@ -475,7 +493,11 @@
         rho[pl.ds(pl.multiple_of(cz * 16, 16), 16), :] = value
         return 0
 
-    lax.fori_loop(0, 16, layer, 0, unroll=2)
+    for n, arrival in enumerate([None] + arrivals):
+        if arrival is not None:
+            arrival.wait()
+        start = lax.rem(gz + 4 - n, 4) * 4
+        lax.fori_loop(start, start + 4, layer, 0, unroll=False)
     lines = dot3((table_ref[0], table_ref[1]), split(rho[...]))
     for plane in range(2):
         for xq in range(4):
@@ -488,10 +510,11 @@
 
 
 def front_kernel(charge_hbm, amplitude_hbm, pair_hbm, embed_hbm, count_hbm, offset_hbm, fraction_hbm, species_hbm, table_hbm,
-                 turned_hbm, mixed_hbm, mixed_turned_hbm, ext_ref, got_ref, density_ref, wide_ref, out_ref,
+                 turned_hbm, mixed_hbm, mixed_turned_hbm, ext_ref, density_ref, wide_ref, electric_ref,
                  charge_ref, amplitude_ref, pair_ref, embed_ref, count_ref, offset_ref, fraction_ref, species_ref, table_ref,
-                 turned_ref, mixed_ref, mixed_turned_ref, atoms, rho, lines, planes, slopes, feat_b, own_t, rows, totals, mat,
-                 load_sem, halo_send, halo_recv, column_send, column_recv, slope_send, slope_recv, line_send, line_recv):
+                 turned_ref, mixed_ref, mixed_turned_ref, atoms, got_ref, rho, lines, planes, fields, back, slopes, feat_b, own_t, rows, totals, mat, field, out,
+                 load_sem, halo_send, halo_recv, column_send, column_recv, slope_send, slope_recv, line_send, line_recv,
+                 field_send, field_recv, return_send, return_recv):
     place = here()
     me = place[0] * 32 + place[1] * 4 + place[2]
     loads = [
@@ -540,37 +563,50 @@
     pl.semaphore_wait(barrier, 127)
     columns = column_copies(atoms, got_ref, place, column_send, column_recv)
     halo = halo_copies(ext_ref, 1, ext_ref, place, halo_send, halo_recv)
-    for copy in columns:
-        copy.wait()
-    spread_and_transform(got_ref, [charge_ref[k] for k in range(2)], table_ref, lines, rho)
+    charges = [charge_ref[k] for k in range(2)]
+    spread_and_transform(got_ref, charges, table_ref, lines, rho, place[2], columns)
     for copy in halo:
         copy.wait()
     amplitudes, pairs, embeds = [[filled(ref, k) for k in range(2)] for ref in (amplitude_ref, pair_ref, embed_ref)]
-    density_features(ext_ref, amplitudes, feat_b, own_t, rows)
-
-    def line_copy(i):
-        other = lax.rem(me + i, 128)
-        return pltpu.make_async_remote_copy(
-            src_ref=lines.at[pl.ds(pl.multiple_of(other * 8, 8), 8), :],
-            dst_ref=planes.at[pl.ds(pl.multiple_of(me * 8, 8), 8), :],
-            send_sem=line_send.at[i],
-            recv_sem=line_recv.at[i],
-            device_id=device_at(other),
-            device_id_type=MESH,
-        )
-
-    def send_line(i, _):
-        line_copy(i).start()
-        return 0
-
-    def wait_line(i, _):
-        line_copy(i).wait()
-        return 0
-
-    lax.fori_loop(1, 128, send_line, 0)
-    mine = pl.ds(pl.multiple_of(me * 8, 8), 8)
-    planes[mine, :] = lines[mine, :]
-    densities(pairs, embeds, density_ref, slopes, feat_b, own_t, rows, totals, mat)
+
+    def exchange(src, dst, send_sem, recv_sem):
+        def tile_copy(i):
+            other = lax.rem(me + i, 128)
+            return pltpu.make_async_remote_copy(
+                src_ref=src.at[pl.ds(pl.multiple_of(other * 8, 8), 8), :],
+                dst_ref=dst.at[pl.ds(pl.multiple_of(me * 8, 8), 8), :],
+                send_sem=send_sem.at[i],
+                recv_sem=recv_sem.at[i],
+                device_id=device_at(other),
+                device_id_type=MESH,
+            )
+
+        def start(i, _):
+            tile_copy(i).start()
+            return 0
+
+        def finish(i, _):
+            tile_copy(i).wait()
+            return 0
+
+        lax.fori_loop(1, 128, start, 0)
+        mine = pl.ds(pl.multiple_of(me * 8, 8), 8)
+        dst[mine, :] = src[mine, :]
+        return lambda: lax.fori_loop(1, 128, finish, 0)
+
+    target_features(ext_ref, own_t, rows, None, None, None)
+    finish_lines = exchange(lines, planes, line_send, line_recv)
+    source_features(ext_ref, None, None, feat_b, [cube_root(value) for value in amplitudes], None)
+    run, end = density_steps(feat_b, own_t, totals, mat)
+    totals[...] = jnp.zeros((256, 128), F32)
+    run(0, 7)
+    finish_lines()
+    transform_planes(me, planes, table_ref, turned_ref, mixed_ref, mixed_turned_ref, fields)
+    run(7, 8)
+    finish_fields = exchange(fields, back, field_send, field_recv)
+    run(8, 16)
+    end()
+    densities(pairs, embeds, density_ref, slopes, rows, mat)
 
     def keep_slope(t, _):
         x, y, z = lax.div(t, 8), lax.rem(lax.div(t, 4), 2), lax.rem(t, 4)
@@ -579,8 +615,8 @@
 
     lax.fori_loop(0, 32, keep_slope, 0)
     halo = halo_copies(slopes, 0, wide_ref, place, slope_send, slope_recv)
-    lax.fori_loop(1, 128, wait_line, 0)
-    transform_planes(me, planes, table_ref, turned_ref, mixed_ref, mixed_turned_ref, out_ref)
+    finish_fields()
+    sample(place, charges, back, got_ref, table_ref, electric_ref, field, out, return_send, return_recv)
     for copy in halo:
         copy.wait()
 
@@ -644,10 +680,7 @@
                 out_ref[start:start + 32, :] = value[gx * 4:(gx + 1) * 4].reshape(32, 128)
 
 
-def sample_kernel(charge_ref, in_ref, atoms_ref, table_ref, back_ref, field, out, send_sem, recv_sem):
-    place = here()
-    signal(column_devices(place))
-    charges = [charge_ref[k] for k in range(2)]
+def sample(place, charges, in_ref, atoms_ref, table_ref, back_ref, field, out, send_sem, recv_sem):
     columns = [
         jnp.concatenate([in_ref[pl.ds(plane * 4 + xq, 128, stride=8), :] for xq in range(4)], axis=1)
         for plane in range(2)
@@ -658,7 +691,6 @@
     for group in range(2):
         for i, piece in enumerate(pieces_of_field):
             field[group, :, i * 128:(i + 1) * 128] = piece[:, group * 128:(group + 1) * 128]
-    await_signals(3)
     point = lax.broadcasted_iota(jnp.int32, (128, 128), 0).astype(F32)
 
     def cell(n):
@@ -741,13 +773,12 @@
         front_kernel,
         out_shape=[
             jax.ShapeDtypeStruct((6, 4, 6, 4, 128), F32),
-            jax.ShapeDtypeStruct((4, 8, 8, 128), F32),
             jax.ShapeDtypeStruct((8, 4, 128), F32),
             jax.ShapeDtypeStruct((6, 4, 6, 1, 128), F32),
-            jax.ShapeDtypeStruct((1024, 128), F32),
+            jax.ShapeDtypeStruct((4, 2, 3, 4, 128), F32),
         ],
         in_specs=[hbm] * 12,
-        out_specs=[VMEM_SPEC] * 5,
+        out_specs=[VMEM_SPEC] * 4,
         scratch_shapes=small + [
             pltpu.VMEM((4, 2, 3, 4, 128), jnp.int32),
             pltpu.VMEM((4, 2, 3, 4, 128), F32),
@@ -757,44 +788,36 @@
             pltpu.VMEM((2, 256, 512), BF16),
             pltpu.VMEM((3, 512, 256), BF16),
             pltpu.VMEM((4, 8, 8, 128), F32),
+            pltpu.VMEM((4, 8, 8, 128), F32),
             pltpu.VMEM((256, 512), F32),
+            pltpu.VMEM((1024, 128), F32),
+            pltpu.VMEM((1024, 128), F32),
             pltpu.VMEM((1024, 128), F32),
             pltpu.VMEM((1024, 128), F32),
             pltpu.VMEM((4, 2, 4, 1, 128), F32),
         ] + features_scratch() + [
             pltpu.VMEM((256, 128), F32),
             pltpu.VMEM((128, 128), F32),
+            pltpu.VMEM((2, 512, 384), BF16),
+            pltpu.VMEM((4, 2, 3, 4, 128), F32),
             DMA((12,)),
             DMA((26,)), DMA((26,)), DMA((3,)), DMA((3,)), DMA((26,)), DMA((26,)), DMA((128,)), DMA((128,)),
+            DMA((128,)), DMA((128,)), DMA((3,)), DMA((3,)),
         ],
-        compiler_params=comm_params(0),
+        compiler_params=pltpu.CompilerParams(collective_id=0, has_side_effects=True, vmem_limit_bytes=67043328),
         name="front_pass",
     )(*arrays)
-
-
-def sample_pass(charge, lines, atoms, table):
-    return pl.pallas_call(
-        sample_kernel,
-        out_shape=jax.ShapeDtypeStruct((4, 2, 3, 4, 128), F32),
-        in_specs=[SMEM_SPEC] + [VMEM_SPEC] * 3,
-        out_specs=VMEM_SPEC,
-        scratch_shapes=[pltpu.VMEM((2, 512, 384), BF16), pltpu.VMEM((4, 2, 3, 4, 128), F32), DMA((3,)), DMA((3,))],
-        compiler_params=comm_params(2),
-        name="sample_pass",
-    )(charge, lines, atoms, table)
 
 
 def on_device(cell_counts, grid_offset, fraction, species, species_density, species_pair, species_embed, species_charge):
     table, turned, mixed, mixed_turned = constants()
     order = (0, 1, 3, 2, 4)
-    extended, columns, density, wide_slope, planes = front_pass(
+    extended, density, wide_slope, electric = front_pass(
         species_charge, species_density, species_pair, species_embed, cell_counts, grid_offset.transpose(order),
         fraction.transpose(order), species, table, turned, mixed, mixed_turned)
-    lines = lax.all_to_all(planes.reshape(128, 8, 128), AXES, split_axis=0, concat_axis=0, tiled=True)
-    eam, density = force_pass(cell_counts, species_density, species_pair, extended, wide_slope, density)
-    electric = sample_pass(species_charge, lines.reshape(1024, 128), columns, table)
-    forces = eam.reshape(4, 2, 3, 4, 128) + COUPLING * electric
-    return forces.transpose(order), density.reshape(4, 2, 4, 128)
+    forces, density = force_pass(
+        cell_counts, species_density, species_pair, extended, wide_slope, density, electric.reshape(8, 3, 4, 128))
+    return forces.reshape(4, 2, 3, 4, 128).transpose(order), density.reshape(4, 2, 4, 128)
 
 
 def solution(mesh):

time: 109 us -> 95.8 us (0.88)
  local copies, waits for them, and re-layouts: 8.47 us -> 0 us
  starting transfers between devices: 6.24 us -> 0 us
  Pallas kernels: 92.4 us -> 95.6 us
    pallas_call x1, Pallas kernels: 47.3 us -> 60.7 us  [front_pass(): pl.pallas_call(front_kernel, out_shape=[jax.ShapeDtypeStruct((6, 4, 6, 4,...]
    pallas_call x1 -> x0, Pallas kernels: 10.2 us -> none  [sample_pass(): pl.pallas_call(sample_kernel, out_shape=jax.ShapeDtypeStruct((4, 2, 3, 4,...]
    unnamed x28 -> x0, local copies, waits for them, and re-layouts: 8.47 us -> none
    all_to_all x1 -> x0, starting transfers between devices: 6.24 us -> none  [on_device(): lax.all_to_all(planes.reshape(128, 8, 128), AXES, split_axis=0, concat_ax...]
  transfers between devices with their start and end apart: 1 -> 0, of which waited for: 0 -> 0; matrix products, arithmetic and copies ran while one was open for 0% -> 0% of each run, Pallas kernels for 32% -> 0%
where the time goes in v5:
time: 95.8 us; the launch traced here: 96.3 us
  Pallas kernels  95.6 us (100%)
    pallas_call x1, Pallas kernels, front_pass(): pl.pallas_call(front_kernel, out_shape=[jax.ShapeDtypeStruct((6, 4, 6, 4,...  60.7 us
    pallas_call x1, Pallas kernels, force_pass(): pl.pallas_call(force_kernel, out_shape=[jax.ShapeDtypeStruct((8, 3, 4, 12...  34.9 us

profile of v5, /device:TPU:1, one launch (start us, length us, event | category | flops | bytes accessed | tf_op | source)
XLA Modules:
  0.0 96.3 jit_solution(17941872481085018338)
XLA Ops:
  0.6 60.7 %front_pass.1 = (f32[6,4,6,4,128]{4,3,2,1,0:T(4,128)}, f32[8,4,128]{2,1,0:T(4,128)}, f32[6,4,6,1,128]{4,3,2,1,0:T(1,128)}, f32[4,2,3,4,128]{4,3,2,1,0:T(4,128)}) custom-call(f32[2]{0:T(128)} %charge_hbm.1, f32[2]{0:T(128)} %amplitude_hbm.3, f32[2]{0:T(128)} %pair_hbm.3, f32[2]{0:T(128)} %embed_hbm.1, s32[4,2,4]{2,1,0:T(2,128)} %count_hbm.3, ...), custom_call_target="tpu_custom_call" | custom-call | tf_op jit(solution)/shard_map/front_pass/pallas_call | solution.py:772
  61.3 34.9 %force_pass.1 = (f32[8,3,4,128]{3,2,1,0:T(4,128)}, f32[8,4,128]{2,1,0:T(4,128)}) custom-call(s32[4,2,4]{2,1,0:T(2,128)} %count_hbm.3, f32[2]{0:T(128)} %amplitude_hbm.3, f32[2]{0:T(128)} %pair_hbm.3, f32[6,4,6,4,128]{4,3,2,1,0:T(4,128)} %get-tuple-element.8.ext_hbm, f32[6,4,6,1,128]{4,3,2,1,0:T(1,128)} %get-tuple-element.9.slope_hbm, ...), custom_call_target="tpu_custom_call" | custom-call | flops 20000000000 | bytes 1000000 | tf_op jit(solution)/shard_map/force_pass/pallas_call | solution.py:392

commit v6 on v5

--- a/solution.py
+++ b/solution.py
@@ -30,20 +30,9 @@
     return tuple(lax.rem(p + s + n, n) for p, s, n in zip(place, side, SIZES))
 
 
-def signal(devices):
-    barrier = pltpu.get_barrier_semaphore()
-    for device in devices:
-        pl.semaphore_signal(barrier, inc=1, device_id=device, device_id_type=MESH)
-
-
-def await_signals(count):
-    pl.semaphore_wait(pltpu.get_barrier_semaphore(), count)
-
-
 def send(src, dst, send_sem, recv_sem, device):
     copy = pltpu.make_async_remote_copy(
         src_ref=src, dst_ref=dst, send_sem=send_sem, recv_sem=recv_sem, device_id=device, device_id_type=MESH)
-    copy.start()
     return copy
 
 
@@ -56,6 +45,8 @@
             dst.append(pl.ds(1, cells) if s == 0 else pl.ds(0 if s == 1 else cells + 1, 1))
         copies.append(send(own_ref.at[tuple(src)], ext_ref.at[tuple(dst)], send_sem.at[n], recv_sem.at[n],
                            toward(place, side)))
+    for copy in copies:
+        copy.start()
     return copies
 
 
@@ -66,19 +57,13 @@
 
 
 def column_copies(src_ref, dst_ref, place, send_sem, recv_sem):
-    return [column_copy(src_ref, dst_ref, place, send_sem, recv_sem, n) for n in range(3)]
-
-
-def column_devices(place):
-    gx, gy, gz = place
-    return [(gx, gy, lax.rem(gz + n + 1, 4)) for n in range(3)]
+    copies = [column_copy(src_ref, dst_ref, place, send_sem, recv_sem, n) for n in range(3)]
+    for copy in copies:
+        copy.start()
+    return copies
 
 
 DMA = pltpu.SemaphoreType.DMA
-
-
-def comm_params(number):
-    return pltpu.CompilerParams(collective_id=number, has_side_effects=True, vmem_limit_bytes=32 << 20)
 
 
 ROWS = 16
@@ -505,10 +490,6 @@
                 plane * 128:(plane + 1) * 128, xq * 128:(xq + 1) * 128]
 
 
-def device_at(d):
-    return lax.div(d, 32), lax.rem(lax.div(d, 4), 8), lax.rem(d, 4)
-
-
 def front_kernel(charge_hbm, amplitude_hbm, pair_hbm, embed_hbm, count_hbm, offset_hbm, fraction_hbm, species_hbm, table_hbm,
                  turned_hbm, mixed_hbm, mixed_turned_hbm, ext_ref, density_ref, wide_ref, electric_ref,
                  charge_ref, amplitude_ref, pair_ref, embed_ref, count_ref, offset_ref, fraction_ref, species_ref, table_ref,
@@ -528,11 +509,12 @@
         load.start()
     barrier = pltpu.get_barrier_semaphore()
 
-    def greet(i, _):
-        pl.semaphore_signal(barrier, inc=1, device_id=device_at(lax.rem(me + i, 128)), device_id_type=MESH)
-        return 0
-
-    lax.fori_loop(1, 128, greet, 0)
+    def greet(other, _):
+        pl.semaphore_signal(barrier, inc=1, device_id=other, device_id_type=pl.DeviceIdType.LOGICAL)
+        return 0
+
+    lax.fori_loop(me + 1, 128, greet, 0)
+    lax.fori_loop(0, me, greet, 0)
     for load in loads[:4]:
         load.wait()
     slot = lax.broadcasted_iota(jnp.int32, (1, 128), 1)
@@ -570,29 +552,28 @@
     amplitudes, pairs, embeds = [[filled(ref, k) for k in range(2)] for ref in (amplitude_ref, pair_ref, embed_ref)]
 
     def exchange(src, dst, send_sem, recv_sem):
-        def tile_copy(i):
-            other = lax.rem(me + i, 128)
-            return pltpu.make_async_remote_copy(
+        mine = pl.ds(pl.multiple_of(me * 8, 8), 8)
+
+        def start(other, _):
+            pltpu.make_async_remote_copy(
                 src_ref=src.at[pl.ds(pl.multiple_of(other * 8, 8), 8), :],
-                dst_ref=dst.at[pl.ds(pl.multiple_of(me * 8, 8), 8), :],
-                send_sem=send_sem.at[i],
-                recv_sem=recv_sem.at[i],
-                device_id=device_at(other),
-                device_id_type=MESH,
-            )
-
-        def start(i, _):
-            tile_copy(i).start()
+                dst_ref=dst.at[mine, :],
+                send_sem=send_sem.at[0],
+                recv_sem=recv_sem.at[0],
+                device_id=other,
+                device_id_type=pl.DeviceIdType.LOGICAL,
+            ).start()
             return 0
 
-        def finish(i, _):
-            tile_copy(i).wait()
-            return 0
-
-        lax.fori_loop(1, 128, start, 0)
-        mine = pl.ds(pl.multiple_of(me * 8, 8), 8)
+        lax.fori_loop(me + 1, 128, start, 0)
+        lax.fori_loop(0, me, start, 0)
         dst[mine, :] = src[mine, :]
-        return lambda: lax.fori_loop(1, 128, finish, 0)
+
+        def finish():
+            pltpu.make_async_copy(src.at[0:1016, :], dst.at[0:1016, :], recv_sem.at[0]).wait()
+            pltpu.make_async_copy(src.at[0:1016, :], dst.at[0:1016, :], send_sem.at[0]).wait()
+
+        return finish
 
     target_features(ext_ref, own_t, rows, None, None, None)
     finish_lines = exchange(lines, planes, line_send, line_recv)
@@ -642,7 +623,7 @@
         rows.append(jnp.concatenate(pair, axis=1))
     plane = jnp.concatenate(rows, axis=0)
     turned = (turned_ref[0], turned_ref[1])
-    along_y = split(dot3(split(plane), turned))
+    along_y = dot3(split(plane), turned)
 
     row = lax.broadcasted_iota(jnp.int32, (256, 256), 0)
     col = lax.broadcasted_iota(jnp.int32, (256, 256), 1)
@@ -650,8 +631,7 @@
     wave_x = jnp.where(row <= 128, row, row - 128).astype(F32) * scale
     wave_y = jnp.where(col <= 128, col, col - 128).astype(F32) * scale
     flat = wave_x * wave_x + wave_y * wave_y
-    side = lax.div(lax.rem(lax.broadcasted_iota(jnp.int32, (256, 512), 1), 8), 4)
-    side_turned = lax.div(lax.rem(lax.broadcasted_iota(jnp.int32, (512, 256), 0), 8), 4)
+    side = lax.div(lax.rem(lax.broadcasted_iota(jnp.int32, (512, 256), 0), 8), 4)
     total = None
     for p in range(2):
         mode = me if p == 0 else jnp.where(me == 0, 128, me)
@@ -660,11 +640,9 @@
         anchor = squared == 0.0
         green = jnp.where(anchor, 0.0, 4.0 * math.pi * jnp.exp(-squared / (4.0 * EWALD_SPLIT * EWALD_SPLIT))
                           / jnp.where(anchor, 1.0, squared))
-        left = [jnp.where(side == p, mixed_ref[i].astype(F32), 0.0).astype(BF16) for i in range(2)]
-        modes = split3(dot3(left, along_y) * green)
-        back = [jnp.where(side_turned == p, mixed_turned_ref[i].astype(F32), 0.0).astype(BF16) for i in range(3)]
-        part = dot6(back, modes)
-        total = part if total is None else total + part
+        modes = split3(dot3((mixed_ref[0], mixed_ref[1]), split(jnp.where(side == p, along_y, 0.0))) * green)
+        part = dot6([mixed_turned_ref[i] for i in range(3)], modes)
+        total = part if total is None else jnp.where(side == 0, total, part)
     field = dot6(split3(total), [table_ref[i] for i in range(3)])
     for half in range(2):
         block = [field[xr * 128:(xr + 1) * 128, half * 128:(half + 1) * 128] for xr in range(4)]
@@ -734,21 +712,19 @@
             out[owner, cyl, f, pl.ds(lax.rem(own_cell, 4), 1), :] = -charge * jnp.sum(value, axis=0, keepdims=True)
 
     def group(g, _):
-        def later(n, _):
-            cell(n)
-            return 0
-
-        lax.fori_loop(g * 8 + 2, g * 8 + 8, later, 0, unroll=2)
-        return 0
-
-    copies = []
-    for g in range(4):
-        cell(g * 8)
-        cell(g * 8 + 1)
-        if g:
-            copies.append(column_copy(out, back_ref, place, send_sem, recv_sem, g - 1))
-        group(g, 0)
-
+        for n in range(2):
+            cell(g * 8 + n)
+
+        @pl.when(g > 0)
+        def _():
+            column_copy(out, back_ref, place, send_sem, recv_sem, g - 1).start()
+
+        for n in range(2, 8):
+            cell(g * 8 + n)
+        return 0
+
+    lax.fori_loop(0, 4, group, 0)
+    copies = [column_copy(out, back_ref, place, send_sem, recv_sem, n) for n in range(3)]
     back_ref[place[2]] = out[place[2]]
     for copy in copies:
         copy.wait()
@@ -801,8 +777,8 @@
             pltpu.VMEM((2, 512, 384), BF16),
             pltpu.VMEM((4, 2, 3, 4, 128), F32),
             DMA((12,)),
-            DMA((26,)), DMA((26,)), DMA((3,)), DMA((3,)), DMA((26,)), DMA((26,)), DMA((128,)), DMA((128,)),
-            DMA((128,)), DMA((128,)), DMA((3,)), DMA((3,)),
+            DMA((26,)), DMA((26,)), DMA((3,)), DMA((3,)), DMA((26,)), DMA((26,)), DMA((1,)), DMA((1,)),
+            DMA((1,)), DMA((1,)), DMA((3,)), DMA((3,)),
         ],
         compiler_params=pltpu.CompilerParams(collective_id=0, has_side_effects=True, vmem_limit_bytes=67043328),
         name="front_pass",

time: 95.8 us -> 88.2 us (0.921)
  Pallas kernels: 95.6 us -> 87.4 us
    pallas_call x1, Pallas kernels: 60.7 us -> 51.8 us  [front_pass(): pl.pallas_call(front_kernel, out_shape=[jax.ShapeDtypeStruct((6, 4, 6, 4,...]
where the time goes in v6:
time: 88.2 us; the launch traced here: 88 us
  Pallas kernels  87.4 us (99%)
    pallas_call x1, Pallas kernels, front_pass(): pl.pallas_call(front_kernel, out_shape=[jax.ShapeDtypeStruct((6, 4, 6, 4,...  51.8 us
    pallas_call x1, Pallas kernels, force_pass(): pl.pallas_call(force_kernel, out_shape=[jax.ShapeDtypeStruct((8, 3, 4, 12...  35.6 us

profile of v6, /device:TPU:1, one launch (start us, length us, event | category | flops | bytes accessed | tf_op | source)
XLA Modules:
  0.0 88.0 jit_solution(5466500429327428617)
XLA Ops:
  0.6 51.8 %front_pass.1 = (f32[6,4,6,4,128]{4,3,2,1,0:T(4,128)}, f32[8,4,128]{2,1,0:T(4,128)}, f32[6,4,6,1,128]{4,3,2,1,0:T(1,128)}, f32[4,2,3,4,128]{4,3,2,1,0:T(4,128)}) custom-call(f32[2]{0:T(128)} %charge_hbm.1, f32[2]{0:T(128)} %amplitude_hbm.3, f32[2]{0:T(128)} %pair_hbm.3, f32[2]{0:T(128)} %embed_hbm.1, s32[4,2,4]{2,1,0:T(2,128)} %count_hbm.3, ...), custom_call_target="tpu_custom_call" | custom-call | tf_op jit(solution)/shard_map/front_pass/pallas_call | solution.py:748
  52.4 35.6 %force_pass.1 = (f32[8,3,4,128]{3,2,1,0:T(4,128)}, f32[8,4,128]{2,1,0:T(4,128)}) custom-call(s32[4,2,4]{2,1,0:T(2,128)} %count_hbm.3, f32[2]{0:T(128)} %amplitude_hbm.3, f32[2]{0:T(128)} %pair_hbm.3, f32[6,4,6,4,128]{4,3,2,1,0:T(4,128)} %get-tuple-element.8.ext_hbm, f32[6,4,6,1,128]{4,3,2,1,0:T(1,128)} %get-tuple-element.9.slope_hbm, ...), custom_call_target="tpu_custom_call" | custom-call | flops 20000000000 | bytes 1000000 | tf_op jit(solution)/shard_map/force_pass/pallas_call | solution.py:377

commit v7 on v6

--- a/solution.py
+++ b/solution.py
@@ -123,7 +123,7 @@
     return lax.div(r, 24), lax.rem(lax.div(r, 6), 4), lax.rem(r, 6)
 
 
-def source_features(ext_ref, slope_ref, wide, feat_b, scales, ratios):
+def source_features(ext_ref, feat_b, scales, first, last):
     ones, twos = patterns((0, 2, 5), (1, 3), (24,), (25,))
     low_six, low_four, low_two, low_three = [sublane() < n for n in (6, 4, 2, 3)]
 
@@ -137,16 +137,34 @@
         z = row(2) + (lax.rem(r, 6) - 3).astype(F32)
         code = row(3)
         scale = by_species(code, scales)
-        if wide is not None:
-            wide[r, 0], wide[r, 1], wide[r, 2] = x, y, z
-            wide[r, 3] = jnp.where(code == 1.0, ratios[1], ratios[0])
-            wide[r, 4] = jnp.broadcast_to(slope_ref[cell_at(r)], (8, 128))
         square = -scale * (x * x + y * y + z * z)
         double = scale + scale
         x, y, z = double * x, double * y, double * z
         blocks = [jnp.where(low_six, scale, x), jnp.where(low_four, x, y), jnp.where(low_two, y, z),
                   jnp.where(low_three, square, 0.0)]
         feat_b[pl.ds(pl.multiple_of(r * KF, KF), KF), :] = assemble(blocks, ones, twos).astype(BF16)
+        return 0
+
+    def four(n, _):
+        for i in range(4):
+            cell(n * 4 + i, 0)
+        return 0
+
+    lax.fori_loop(first // 4, last // 4, four, 0)
+
+
+def fill_wide(ext_ref, slope_ref, wide, ratios):
+    def cell(r, _):
+        place = cell_at(r)
+
+        def row(f):
+            return jnp.broadcast_to(ext_ref[place + (slice(f, f + 1), slice(None))], (8, 128))
+
+        wide[r, 0] = row(0) + (place[0] - 3).astype(F32)
+        wide[r, 1] = row(1) + (place[1] - 2).astype(F32)
+        wide[r, 2] = row(2) + (place[2] - 3).astype(F32)
+        wide[r, 3] = jnp.where(row(3) == 1.0, ratios[1], ratios[0])
+        wide[r, 4] = jnp.broadcast_to(slope_ref[place], (8, 128))
         return 0
 
     lax.fori_loop(0, 144, cell, 0, unroll=4)
@@ -252,26 +270,26 @@
     slope_ref[...] = (by_species(code, tilts) / jnp.sqrt(1.0 + density)).reshape(4, 2, 4, 1, 128)
 
 
-def force_kernel(count_hbm, amplitude_hbm, pair_hbm, ext_hbm, slope_hbm, given_hbm, electric_hbm, out_ref, density_ref,
+def force_kernel(count_hbm, amplitude_hbm, pair_hbm, ext_hbm, slope_hbm, given_hbm, electric_hbm, feat_hbm, out_ref, density_ref,
                  count_ref, amplitude_ref, pair_ref, ext_ref, slope_ref, given_ref, electric_ref, feat_b, own_t, keep, wide,
                  near_a, near_b, part_a, part_b, mat, table, load_sem):
     loads = [
         pltpu.make_async_copy(src, dst, load_sem.at[n])
         for n, (src, dst) in enumerate((
             (amplitude_hbm, amplitude_ref), (pair_hbm, pair_ref), (ext_hbm, ext_ref), (slope_hbm, slope_ref),
-            (count_hbm, count_ref), (given_hbm, given_ref), (electric_hbm, electric_ref)))
+            (count_hbm, count_ref), (given_hbm, given_ref), (electric_hbm, electric_ref),
+            (feat_hbm, feat_b.at[0:144 * KF, :])))
     ]
     for load in loads:
         load.start()
     part_a[...] = jnp.zeros((4, 128, 128), F32)
     part_b[...] = jnp.zeros((4, 128, 128), F32)
-    for load in loads:
+    for load in loads[:4]:
         load.wait()
     amplitudes, pairs = [[filled(ref, k) for k in range(2)] for ref in (amplitude_ref, pair_ref)]
     ratios = [amplitude / (pair * pair) for amplitude, pair in zip(amplitudes, pairs)]
-    density_ref[...] = given_ref[...]
     gains = [-4.0 * pair / amplitude for amplitude, pair in zip(amplitudes, pairs)]
-    source_features(ext_ref, slope_ref, wide, feat_b, pairs, ratios)
+    fill_wide(ext_ref, slope_ref, wide, ratios)
     target_features(ext_ref, own_t, keep, slope_ref, gains, ratios)
     feat_b[144 * KF:146 * KF, :] = jnp.concatenate([sel_matrix()[:, 0:128], sel_matrix()[:, 128:256]], axis=0)
 
@@ -331,6 +349,9 @@
             mat[pl.ds(t * 4 + m, 1), :] = sums[0:1, 0:128]
             mat[pl.ds(t * 4 + m + 1, 1), :] = sums[0:1, 128:256]
 
+    for load in loads[4:]:
+        load.wait()
+    density_ref[...] = given_ref[...]
     for part in range(4):
         multiply(0, near_a, part)
 
@@ -377,7 +398,7 @@
     return pl.pallas_call(
         force_kernel,
         out_shape=[jax.ShapeDtypeStruct((8, 3, 4, 128), F32), jax.ShapeDtypeStruct((8, 4, 128), F32)],
-        in_specs=[pl.BlockSpec(memory_space=pltpu.HBM)] * 7,
+        in_specs=[pl.BlockSpec(memory_space=pltpu.HBM)] * 8,
         out_specs=[VMEM_SPEC] * 2,
         scratch_shapes=[
             pltpu.SMEM((4, 2, 4), jnp.int32),
@@ -395,7 +416,7 @@
             pltpu.VMEM((4, 128, 128), F32),
             pltpu.VMEM((128, 128), F32),
             pltpu.SMEM((64,), jnp.int32),
-            pltpu.SemaphoreType.DMA((7,)),
+            pltpu.SemaphoreType.DMA((8,)),
         ],
         compiler_params=pltpu.CompilerParams(vmem_limit_bytes=67043328),
         cost_estimate=pl.CostEstimate(flops=20_000_000_000, bytes_accessed=1_000_000, transcendentals=0),
@@ -491,11 +512,11 @@
 
 
 def front_kernel(charge_hbm, amplitude_hbm, pair_hbm, embed_hbm, count_hbm, offset_hbm, fraction_hbm, species_hbm, table_hbm,
-                 turned_hbm, mixed_hbm, mixed_turned_hbm, ext_ref, density_ref, wide_ref, electric_ref,
+                 turned_hbm, mixed_hbm, mixed_turned_hbm, ext_ref, density_ref, wide_ref, electric_ref, feat_hbm,
                  charge_ref, amplitude_ref, pair_ref, embed_ref, count_ref, offset_ref, fraction_ref, species_ref, table_ref,
-                 turned_ref, mixed_ref, mixed_turned_ref, atoms, got_ref, rho, lines, planes, fields, back, slopes, feat_b, own_t, rows, totals, mat, field, out,
+                 turned_ref, mixed_ref, mixed_turned_ref, atoms, got_ref, rho, lines, planes, fields, back, slopes, feat_b, own_t, rows, feat_c, totals, mat, field, out,
                  load_sem, halo_send, halo_recv, column_send, column_recv, slope_send, slope_recv, line_send, line_recv,
-                 field_send, field_recv, return_send, return_recv):
+                 field_send, field_recv, return_send, return_recv, feat_sem):
     place = here()
     me = place[0] * 32 + place[1] * 4 + place[2]
     loads = [
@@ -540,6 +561,7 @@
         return 0
 
     lax.fori_loop(0, 8, keep_own, 0)
+    target_features(ext_ref, own_t, rows, None, None, None)
     for load in loads[4:]:
         load.wait()
     pl.semaphore_wait(barrier, 127)
@@ -575,17 +597,18 @@
 
         return finish
 
-    target_features(ext_ref, own_t, rows, None, None, None)
+    roots = [cube_root(value) for value in amplitudes]
+    source_features(ext_ref, feat_b, roots, 0, 24)
     finish_lines = exchange(lines, planes, line_send, line_recv)
-    source_features(ext_ref, None, None, feat_b, [cube_root(value) for value in amplitudes], None)
+    source_features(ext_ref, feat_b, roots, 24, 144)
     run, end = density_steps(feat_b, own_t, totals, mat)
     totals[...] = jnp.zeros((256, 128), F32)
-    run(0, 7)
+    run(0, 8)
     finish_lines()
     transform_planes(me, planes, table_ref, turned_ref, mixed_ref, mixed_turned_ref, fields)
-    run(7, 8)
+    run(8, 9)
     finish_fields = exchange(fields, back, field_send, field_recv)
-    run(8, 16)
+    run(9, 16)
     end()
     densities(pairs, embeds, density_ref, slopes, rows, mat)
 
@@ -596,10 +619,14 @@
 
     lax.fori_loop(0, 32, keep_slope, 0)
     halo = halo_copies(slopes, 0, wide_ref, place, slope_send, slope_recv)
+    source_features(ext_ref, feat_c, pairs, 0, 144)
     finish_fields()
+    feat_copy = pltpu.make_async_copy(feat_c, feat_hbm, feat_sem.at[0])
+    feat_copy.start()
     sample(place, charges, back, got_ref, table_ref, electric_ref, field, out, return_send, return_recv)
     for copy in halo:
         copy.wait()
+    feat_copy.wait()
 
 
 def transform_planes(me, in_ref, table_ref, turned_ref, mixed_ref, mixed_turned_ref, out_ref):
@@ -752,9 +779,10 @@
             jax.ShapeDtypeStruct((8, 4, 128), F32),
             jax.ShapeDtypeStruct((6, 4, 6, 1, 128), F32),
             jax.ShapeDtypeStruct((4, 2, 3, 4, 128), F32),
+            jax.ShapeDtypeStruct((144 * KF, 128), BF16),
         ],
         in_specs=[hbm] * 12,
-        out_specs=[VMEM_SPEC] * 4,
+        out_specs=[VMEM_SPEC] * 4 + [hbm],
         scratch_shapes=small + [
             pltpu.VMEM((4, 2, 3, 4, 128), jnp.int32),
             pltpu.VMEM((4, 2, 3, 4, 128), F32),
@@ -772,13 +800,14 @@
             pltpu.VMEM((1024, 128), F32),
             pltpu.VMEM((4, 2, 4, 1, 128), F32),
         ] + features_scratch() + [
+            pltpu.VMEM((144 * KF, 128), BF16),
             pltpu.VMEM((256, 128), F32),
             pltpu.VMEM((128, 128), F32),
             pltpu.VMEM((2, 512, 384), BF16),
             pltpu.VMEM((4, 2, 3, 4, 128), F32),
             DMA((12,)),
             DMA((26,)), DMA((26,)), DMA((3,)), DMA((3,)), DMA((26,)), DMA((26,)), DMA((1,)), DMA((1,)),
-            DMA((1,)), DMA((1,)), DMA((3,)), DMA((3,)),
+            DMA((1,)), DMA((1,)), DMA((3,)), DMA((3,)), DMA((1,)),
         ],
         compiler_params=pltpu.CompilerParams(collective_id=0, has_side_effects=True, vmem_limit_bytes=67043328),
         name="front_pass",
@@ -788,11 +817,12 @@
 def on_device(cell_counts, grid_offset, fraction, species, species_density, species_pair, species_embed, species_charge):
     table, turned, mixed, mixed_turned = constants()
     order = (0, 1, 3, 2, 4)
-    extended, density, wide_slope, electric = front_pass(
+    extended, density, wide_slope, electric, features = front_pass(
         species_charge, species_density, species_pair, species_embed, cell_counts, grid_offset.transpose(order),
         fraction.transpose(order), species, table, turned, mixed, mixed_turned)
     forces, density = force_pass(
-        cell_counts, species_density, species_pair, extended, wide_slope, density, electric.reshape(8, 3, 4, 128))
+        cell_counts, species_density, species_pair, extended, wide_slope, density, electric.reshape(8, 3, 4, 128),
+        features)
     return forces.reshape(4, 2, 3, 4, 128).transpose(order), density.reshape(4, 2, 4, 128)
 
 

time: 88.2 us -> 85.6 us (0.971)
  Pallas kernels: 87.4 us -> 84.5 us
    pallas_call x1, Pallas kernels: 35.6 us -> 33.7 us  [force_pass(): pl.pallas_call(force_kernel, out_shape=[jax.ShapeDtypeStruct((8, 3, 4, 12...]
    pallas_call x1, Pallas kernels: 51.8 us -> 50.7 us  [front_pass(): pl.pallas_call(front_kernel, out_shape=[jax.ShapeDtypeStruct((6, 4, 6, 4,...]
where the time goes in v7:
time: 85.6 us; the launch traced here: 85.1 us
  Pallas kernels  84.5 us (99%)
    pallas_call x1, Pallas kernels, front_pass(): pl.pallas_call(front_kernel, out_shape=[jax.ShapeDtypeStruct((6, 4, 6, 4,...  50.7 us
    pallas_call x1, Pallas kernels, force_pass(): pl.pallas_call(force_kernel, out_shape=[jax.ShapeDtypeStruct((8, 3, 4, 12...  33.7 us

profile of v7, /device:TPU:1, one launch (start us, length us, event | category | flops | bytes accessed | tf_op | source)
XLA Modules:
  0.0 85.1 jit_solution(5709761471992378711)
XLA Ops:
  0.6 50.7 %front_pass.1 = (f32[6,4,6,4,128]{4,3,2,1,0:T(4,128)}, f32[8,4,128]{2,1,0:T(4,128)}, f32[6,4,6,1,128]{4,3,2,1,0:T(1,128)}, f32[4,2,3,4,128]{4,3,2,1,0:T(4,128)}, bf16[4608,128]{1,0:T(8,128)(2,1)}) custom-call(f32[2]{0:T(128)} %charge_hbm.1, f32[2]{0:T(128)} %amplitude_hbm.3, f32[2]{0:T(128)} %pair_hbm.3, f32[2]{0:T(128)} %embed_hbm.1, s32[4,2,4]{2,1,0:T(2,128)} %count_hbm.3, ...), custom_call_target="tpu_custom_call" | custom-call | tf_op jit(solution)/shard_map/front_pass/pallas_call | solution.py:775
  51.4 33.7 %force_pass.1 = (f32[8,3,4,128]{3,2,1,0:T(4,128)}, f32[8,4,128]{2,1,0:T(4,128)}) custom-call(s32[4,2,4]{2,1,0:T(2,128)} %count_hbm.3, f32[2]{0:T(128)} %amplitude_hbm.3, f32[2]{0:T(128)} %pair_hbm.3, f32[6,4,6,4,128]{4,3,2,1,0:T(4,128)} %get-tuple-element.9.ext_hbm, f32[6,4,6,1,128]{4,3,2,1,0:T(1,128)} %get-tuple-element.10.slope_hbm, ...), custom_call_target="tpu_custom_call" | custom-call | flops 20000000000 | bytes 1000000 | tf_op jit(solution)/shard_map/force_pass/pallas_call | solution.py:398

commit v8 on v7

--- a/solution.py
+++ b/solution.py
@@ -119,22 +119,19 @@
     return ones, twos
 
 
-def cell_at(r):
-    return lax.div(r, 24), lax.rem(lax.div(r, 6), 4), lax.rem(r, 6)
-
-
 def source_features(ext_ref, feat_b, scales, first, last):
     ones, twos = patterns((0, 2, 5), (1, 3), (24,), (25,))
     low_six, low_four, low_two, low_three = [sublane() < n for n in (6, 4, 2, 3)]
 
-    def cell(r, _):
+    def cell(n, cx, cy, cz):
+        r = n * 6 + cz
+
         def row(f):
-            x, y, z = cell_at(r)
-            return jnp.broadcast_to(ext_ref[x, y, z, f:f + 1, :], (8, 128))
-
-        x = row(0) + (lax.div(r, 24) - 3).astype(F32)
-        y = row(1) + (lax.rem(lax.div(r, 6), 4) - 2).astype(F32)
-        z = row(2) + (lax.rem(r, 6) - 3).astype(F32)
+            return jnp.broadcast_to(ext_ref[cx, cy, cz, f:f + 1, :], (8, 128))
+
+        x = row(0) + (cx - 3).astype(F32)
+        y = row(1) + (cy - 2).astype(F32)
+        z = row(2) + (cz - 3.0)
         code = row(3)
         scale = by_species(code, scales)
         square = -scale * (x * x + y * y + z * z)
@@ -143,31 +140,32 @@
         blocks = [jnp.where(low_six, scale, x), jnp.where(low_four, x, y), jnp.where(low_two, y, z),
                   jnp.where(low_three, square, 0.0)]
         feat_b[pl.ds(pl.multiple_of(r * KF, KF), KF), :] = assemble(blocks, ones, twos).astype(BF16)
-        return 0
-
-    def four(n, _):
-        for i in range(4):
-            cell(n * 4 + i, 0)
-        return 0
-
-    lax.fori_loop(first // 4, last // 4, four, 0)
+
+    def column(n, _):
+        for z in range(6):
+            cell(n, lax.div(n, 4), lax.rem(n, 4), z)
+        return 0
+
+    lax.fori_loop(first, last, column, 0)
 
 
 def fill_wide(ext_ref, slope_ref, wide, ratios):
-    def cell(r, _):
-        place = cell_at(r)
-
-        def row(f):
-            return jnp.broadcast_to(ext_ref[place + (slice(f, f + 1), slice(None))], (8, 128))
-
-        wide[r, 0] = row(0) + (place[0] - 3).astype(F32)
-        wide[r, 1] = row(1) + (place[1] - 2).astype(F32)
-        wide[r, 2] = row(2) + (place[2] - 3).astype(F32)
-        wide[r, 3] = jnp.where(row(3) == 1.0, ratios[1], ratios[0])
-        wide[r, 4] = jnp.broadcast_to(slope_ref[place], (8, 128))
-        return 0
-
-    lax.fori_loop(0, 144, cell, 0, unroll=4)
+    def column(n, _):
+        cx, cy = lax.div(n, 4), lax.rem(n, 4)
+        offset_x, offset_y = (cx - 3).astype(F32), (cy - 2).astype(F32)
+        for cz in range(6):
+            def row(f):
+                return jnp.broadcast_to(ext_ref[cx, cy, cz, f:f + 1, :], (8, 128))
+
+            r = n * 6 + cz
+            wide[r, 0] = row(0) + offset_x
+            wide[r, 1] = row(1) + offset_y
+            wide[r, 2] = row(2) + (cz - 3.0)
+            wide[r, 3] = jnp.where(row(3) == 1.0, ratios[1], ratios[0])
+            wide[r, 4] = jnp.broadcast_to(slope_ref[cx, cy, cz], (8, 128))
+        return 0
+
+    lax.fori_loop(0, 24, column, 0)
 
 
 def corner(t):
@@ -179,31 +177,34 @@
     low_six, low_four, low_two, low_three = [sublane() < n for n in (6, 4, 2, 3)]
     low_five, low_seven = sublane() < 5, sublane() < 7
 
-    def cell(t, _):
-        r = corner(t) + 31
+    def cell(n, cx, cy, cz):
+        t, place = n * 4 + cz, (cx + 1, cy + 1, cz + 1)
 
         def row(f):
-            x, y, z = cell_at(r)
-            return jnp.broadcast_to(ext_ref[x, y, z, f:f + 1, :], (8, 128))
-
-        x = row(0) + (lax.div(t, 8) - 2).astype(F32)
-        y = row(1) + (lax.rem(lax.div(t, 4), 2) - 1).astype(F32)
-        z = row(2) + (lax.rem(t, 4) - 2).astype(F32)
+            return jnp.broadcast_to(ext_ref[place + (slice(f, f + 1), slice(None))], (8, 128))
+
+        x = row(0) + (cx - 2).astype(F32)
+        y = row(1) + (cy - 1).astype(F32)
+        z = row(2) + (cz - 2.0)
         code = row(3)
-        for n, value in enumerate((x, y, z, code)):
-            keep[n, pl.ds(t, 1), :] = value[0:1]
+        for k, value in enumerate((x, y, z, code)):
+            keep[k, pl.ds(t, 1), :] = value[0:1]
         rest = 1.0 - (x * x + y * y + z * z)
         tail = jnp.zeros((8, 128), F32)
         if gains is not None:
             second = code == 1.0
-            tilt = jnp.broadcast_to(slope_ref[cell_at(r)], (8, 128)) / jnp.where(second, ratios[1], ratios[0])
+            tilt = jnp.broadcast_to(slope_ref[place], (8, 128)) / jnp.where(second, ratios[1], ratios[0])
             tail = jnp.where(low_five, jnp.where(second, gains[1], gains[0]), jnp.where(low_seven, tilt, 0.0))
         blocks = [jnp.where(low_six, rest, x), jnp.where(low_four, x, y), jnp.where(low_two, y, z),
                   jnp.where(low_three, 1.0, tail)]
         own_t[t] = assemble(blocks, ones, twos).T.astype(BF16)
-        return 0
-
-    lax.fori_loop(0, 32, cell, 0, unroll=4)
+
+    def column(n, _):
+        for cz in range(4):
+            cell(n, lax.div(n, 2), lax.rem(n, 2), cz)
+        return 0
+
+    lax.fori_loop(0, 8, column, 0)
 
 
 def split3(value):
@@ -503,7 +504,7 @@
         if arrival is not None:
             arrival.wait()
         start = lax.rem(gz + 4 - n, 4) * 4
-        lax.fori_loop(start, start + 4, layer, 0, unroll=False)
+        lax.fori_loop(start, start + 4, layer, 0)
     lines = dot3((table_ref[0], table_ref[1]), split(rho[...]))
     for plane in range(2):
         for xq in range(4):
@@ -598,9 +599,9 @@
         return finish
 
     roots = [cube_root(value) for value in amplitudes]
-    source_features(ext_ref, feat_b, roots, 0, 24)
+    source_features(ext_ref, feat_b, roots, 0, 4)
     finish_lines = exchange(lines, planes, line_send, line_recv)
-    source_features(ext_ref, feat_b, roots, 24, 144)
+    source_features(ext_ref, feat_b, roots, 4, 24)
     run, end = density_steps(feat_b, own_t, totals, mat)
     totals[...] = jnp.zeros((256, 128), F32)
     run(0, 8)
@@ -619,12 +620,15 @@
 
     lax.fori_loop(0, 32, keep_slope, 0)
     halo = halo_copies(slopes, 0, wide_ref, place, slope_send, slope_recv)
-    source_features(ext_ref, feat_c, pairs, 0, 144)
+    source_features(ext_ref, feat_c, pairs, 0, 14)
     finish_fields()
+    returns = sample(place, charges, back, got_ref, table_ref, electric_ref, field, out, return_send, return_recv)
+    source_features(ext_ref, feat_c, pairs, 14, 24)
+    for copy in halo:
+        copy.wait()
     feat_copy = pltpu.make_async_copy(feat_c, feat_hbm, feat_sem.at[0])
     feat_copy.start()
-    sample(place, charges, back, got_ref, table_ref, electric_ref, field, out, return_send, return_recv)
-    for copy in halo:
+    for copy in returns:
         copy.wait()
     feat_copy.wait()
 
@@ -753,8 +757,7 @@
     lax.fori_loop(0, 4, group, 0)
     copies = [column_copy(out, back_ref, place, send_sem, recv_sem, n) for n in range(3)]
     back_ref[place[2]] = out[place[2]]
-    for copy in copies:
-        copy.wait()
+    return copies
 
 
 def field_rows(field, group, cyl):

time: 85.6 us -> 83.8 us (0.979)
  Pallas kernels: 84.5 us -> 83.1 us
    pallas_call x1, Pallas kernels: 33.7 us -> 32.5 us  [force_pass(): pl.pallas_call(force_kernel, out_shape=[jax.ShapeDtypeStruct((8, 3, 4, 12...]
where the time goes in v8:
time: 83.8 us; the launch traced here: 83.7 us
  Pallas kernels  83.1 us (99%)
    pallas_call x1, Pallas kernels, front_pass(): pl.pallas_call(front_kernel, out_shape=[jax.ShapeDtypeStruct((6, 4, 6, 4,...  50.5 us
    pallas_call x1, Pallas kernels, force_pass(): pl.pallas_call(force_kernel, out_shape=[jax.ShapeDtypeStruct((8, 3, 4, 12...  32.5 us

profile of v8, /device:TPU:1, one launch (start us, length us, event | category | flops | bytes accessed | tf_op | source)
XLA Modules:
  0.0 83.7 jit_solution(14183839526205818401)
XLA Ops:
  0.6 50.5 %front_pass.1 = (f32[6,4,6,4,128]{4,3,2,1,0:T(4,128)}, f32[8,4,128]{2,1,0:T(4,128)}, f32[6,4,6,1,128]{4,3,2,1,0:T(1,128)}, f32[4,2,3,4,128]{4,3,2,1,0:T(4,128)}, bf16[4608,128]{1,0:T(8,128)(2,1)}) custom-call(f32[2]{0:T(128)} %charge_hbm.1, f32[2]{0:T(128)} %amplitude_hbm.3, f32[2]{0:T(128)} %pair_hbm.3, f32[2]{0:T(128)} %embed_hbm.1, s32[4,2,4]{2,1,0:T(2,128)} %count_hbm.3, ...), custom_call_target="tpu_custom_call" | custom-call | tf_op jit(solution)/shard_map/front_pass/pallas_call | solution.py:778
  51.2 32.5 %force_pass.1 = (f32[8,3,4,128]{3,2,1,0:T(4,128)}, f32[8,4,128]{2,1,0:T(4,128)}) custom-call(s32[4,2,4]{2,1,0:T(2,128)} %count_hbm.3, f32[2]{0:T(128)} %amplitude_hbm.3, f32[2]{0:T(128)} %pair_hbm.3, f32[6,4,6,4,128]{4,3,2,1,0:T(4,128)} %get-tuple-element.9.ext_hbm, f32[6,4,6,1,128]{4,3,2,1,0:T(1,128)} %get-tuple-element.10.slope_hbm, ...), custom_call_target="tpu_custom_call" | custom-call | flops 20000000000 | bytes 1000000 | tf_op jit(solution)/shard_map/force_pass/pallas_call | solution.py:399

commit v9 on v8

--- a/solution.py
+++ b/solution.py
@@ -577,7 +577,8 @@
     def exchange(src, dst, send_sem, recv_sem):
         mine = pl.ds(pl.multiple_of(me * 8, 8), 8)
 
-        def start(other, _):
+        def start(_, other):
+            other = lax.rem(other + 37, 128)
             pltpu.make_async_remote_copy(
                 src_ref=src.at[pl.ds(pl.multiple_of(other * 8, 8), 8), :],
                 dst_ref=dst.at[mine, :],
@@ -586,10 +587,9 @@
                 device_id=other,
                 device_id_type=pl.DeviceIdType.LOGICAL,
             ).start()
-            return 0
-
-        lax.fori_loop(me + 1, 128, start, 0)
-        lax.fori_loop(0, me, start, 0)
+            return other
+
+        lax.fori_loop(1, 128, start, me)
         dst[mine, :] = src[mine, :]
 
         def finish():

time: 83.8 us -> 86.5 us (1.032); the launches traced: 83.7 us -> 85.4 us
  Pallas kernels: 83.1 us -> 84.7 us
    pallas_call x1, Pallas kernels: 50.5 us -> 53 us  [front_pass(): pl.pallas_call(front_kernel, out_shape=[jax.ShapeDtypeStruct((6, 4, 6, 4,...]
where the time goes in v9:
time: 86.5 us; the launch traced here: 85.4 us
  Pallas kernels  84.7 us (98%)
    pallas_call x1, Pallas kernels, front_pass(): pl.pallas_call(front_kernel, out_shape=[jax.ShapeDtypeStruct((6, 4, 6, 4,...  53 us
    pallas_call x1, Pallas kernels, force_pass(): pl.pallas_call(force_kernel, out_shape=[jax.ShapeDtypeStruct((8, 3, 4, 12...  31.8 us

profile of v9, /device:TPU:1, one launch (start us, length us, event | category | flops | bytes accessed | tf_op | source)
XLA Modules:
  0.0 85.4 jit_solution(6438722976301132534)
XLA Ops:
  0.6 53.0 %front_pass.1 = (f32[6,4,6,4,128]{4,3,2,1,0:T(4,128)}, f32[8,4,128]{2,1,0:T(4,128)}, f32[6,4,6,1,128]{4,3,2,1,0:T(1,128)}, f32[4,2,3,4,128]{4,3,2,1,0:T(4,128)}, bf16[4608,128]{1,0:T(8,128)(2,1)}) custom-call(f32[2]{0:T(128)} %charge_hbm.1, f32[2]{0:T(128)} %amplitude_hbm.3, f32[2]{0:T(128)} %pair_hbm.3, f32[2]{0:T(128)} %embed_hbm.1, s32[4,2,4]{2,1,0:T(2,128)} %count_hbm.3, ...), custom_call_target="tpu_custom_call" | custom-call | tf_op jit(solution)/shard_map/front_pass/pallas_call | solution.py:778
  53.6 31.8 %force_pass.1 = (f32[8,3,4,128]{3,2,1,0:T(4,128)}, f32[8,4,128]{2,1,0:T(4,128)}) custom-call(s32[4,2,4]{2,1,0:T(2,128)} %count_hbm.3, f32[2]{0:T(128)} %amplitude_hbm.3, f32[2]{0:T(128)} %pair_hbm.3, f32[6,4,6,4,128]{4,3,2,1,0:T(4,128)} %get-tuple-element.9.ext_hbm, f32[6,4,6,1,128]{4,3,2,1,0:T(1,128)} %get-tuple-element.10.slope_hbm, ...), custom_call_target="tpu_custom_call" | custom-call | flops 20000000000 | bytes 1000000 | tf_op jit(solution)/shard_map/force_pass/pallas_call | solution.py:399

commit v10 on v8

--- a/solution.py
+++ b/solution.py
@@ -577,7 +577,7 @@
     def exchange(src, dst, send_sem, recv_sem):
         mine = pl.ds(pl.multiple_of(me * 8, 8), 8)
 
-        def start(other, _):
+        def start(other):
             pltpu.make_async_remote_copy(
                 src_ref=src.at[pl.ds(pl.multiple_of(other * 8, 8), 8), :],
                 dst_ref=dst.at[mine, :],
@@ -586,10 +586,14 @@
                 device_id=other,
                 device_id_type=pl.DeviceIdType.LOGICAL,
             ).start()
+
+        def both_ways(i, _):
+            start(lax.rem(me + i, 128))
+            start(lax.rem(me + 128 - i, 128))
             return 0
 
-        lax.fori_loop(me + 1, 128, start, 0)
-        lax.fori_loop(0, me, start, 0)
+        lax.fori_loop(1, 64, both_ways, 0)
+        start(lax.rem(me + 64, 128))
         dst[mine, :] = src[mine, :]
 
         def finish():

time: 83.8 us -> 84.9 us (1.013)
    pallas_call x1, Pallas kernels: 50.5 us -> 52.5 us  [front_pass(): pl.pallas_call(front_kernel, out_shape=[jax.ShapeDtypeStruct((6, 4, 6, 4,...]
    pallas_call x1, Pallas kernels: 32.5 us -> 31.3 us  [force_pass(): pl.pallas_call(force_kernel, out_shape=[jax.ShapeDtypeStruct((8, 3, 4, 12...]
where the time goes in v10:
time: 84.9 us; the launch traced here: 84.4 us
  Pallas kernels  83.8 us (99%)
    pallas_call x1, Pallas kernels, front_pass(): pl.pallas_call(front_kernel, out_shape=[jax.ShapeDtypeStruct((6, 4, 6, 4,...  52.5 us
    pallas_call x1, Pallas kernels, force_pass(): pl.pallas_call(force_kernel, out_shape=[jax.ShapeDtypeStruct((8, 3, 4, 12...  31.3 us

profile of v10, /device:TPU:1, one launch (start us, length us, event | category | flops | bytes accessed | tf_op | source)
XLA Modules:
  0.0 84.4 jit_solution(9722654842091752430)
XLA Ops:
  0.6 52.5 %front_pass.1 = (f32[6,4,6,4,128]{4,3,2,1,0:T(4,128)}, f32[8,4,128]{2,1,0:T(4,128)}, f32[6,4,6,1,128]{4,3,2,1,0:T(1,128)}, f32[4,2,3,4,128]{4,3,2,1,0:T(4,128)}, bf16[4608,128]{1,0:T(8,128)(2,1)}) custom-call(f32[2]{0:T(128)} %charge_hbm.1, f32[2]{0:T(128)} %amplitude_hbm.3, f32[2]{0:T(128)} %pair_hbm.3, f32[2]{0:T(128)} %embed_hbm.1, s32[4,2,4]{2,1,0:T(2,128)} %count_hbm.3, ...), custom_call_target="tpu_custom_call" | custom-call | tf_op jit(solution)/shard_map/front_pass/pallas_call | solution.py:782
  53.1 31.3 %force_pass.1 = (f32[8,3,4,128]{3,2,1,0:T(4,128)}, f32[8,4,128]{2,1,0:T(4,128)}) custom-call(s32[4,2,4]{2,1,0:T(2,128)} %count_hbm.3, f32[2]{0:T(128)} %amplitude_hbm.3, f32[2]{0:T(128)} %pair_hbm.3, f32[6,4,6,4,128]{4,3,2,1,0:T(4,128)} %get-tuple-element.9.ext_hbm, f32[6,4,6,1,128]{4,3,2,1,0:T(1,128)} %get-tuple-element.10.slope_hbm, ...), custom_call_target="tpu_custom_call" | custom-call | flops 20000000000 | bytes 1000000 | tf_op jit(solution)/shard_map/force_pass/pallas_call | solution.py:399
